TPU v7x, 32 devices: a whole 2x2x4 slice. The times are simulated.
32 devices in a mesh: dp: 8 (over z, y), mp: 4 (over x, core).
Axes of the slice: x: 2, y: 2, z: 4, core: 2. Of those that a mesh axis runs over, the one named last changes fastest.
Arguments:
- inputs: bfloat16 [16384, 1024], P(('dp', 'mp')), may hold values from -6 to 6
- first_values: bfloat16 [16384, 8, 64], P('dp', 'mp'), may hold values from -6 to 6
- cotangent: bfloat16 [16384, 1024], P(('dp', 'mp')), may hold values from -6 to 6
- seq_lengths: int32 [32], P('dp'), may hold values from 0 to 1024, as said below
- value_owner: int32 [8], replicated, may hold values from 0 to 7, each once
- attn_norm_gain: float32 [1024], replicated, may hold values from 0.5 to 1.5
- attn_norm_bias: float32 [1024], replicated, may hold values from -3 to 3
- qkv_weight: bfloat16 [1024, 8, 5, 64], P(None, 'mp'), may hold values from -0.25 to 0.25
- qv_bias: float32 [8, 3, 64], P('mp'), may hold values from -3 to 3
- out_weight: bfloat16 [8, 2, 64, 1024], P('mp'), may hold values from -0.75 to 0.75
- out_bias: float32 [1024], replicated, may hold values from -3 to 3
- mlp_norm_gain: float32 [1024], replicated, may hold values from 0.5 to 1.5
- mlp_norm_bias: float32 [1024], replicated, may hold values from -3 to 3
- up_weight: bfloat16 [1024, 4096], P(None, 'mp'), may hold values from -0.1875 to 0.1875
- up_bias: float32 [4096], P('mp'), may hold values from -3 to 3
- down_weight: bfloat16 [4096, 1024], P('mp'), may hold values from -0.09375 to 0.09375
- down_bias: float32 [1024], replicated, may hold values from -3 to 3
Outputs:
- output: bfloat16 [16384, 1024], P(('dp', 'mp'))
- grad_inputs: bfloat16 [16384, 1024], P(('dp', 'mp'))
- grad_first_values: bfloat16 [16384, 8, 64], P('dp', 'mp')
- grad_attn_norm_gain: float32 [1024], replicated
- grad_attn_norm_bias: float32 [1024], replicated
- grad_qkv_weight: float32 [1024, 8, 5, 64], P(None, 'mp')
- grad_qv_bias: float32 [8, 3, 64], P('mp')
- grad_out_weight: float32 [8, 2, 64, 1024], P('mp')
- grad_out_bias: float32 [1024], replicated
- grad_mlp_norm_gain: float32 [1024], replicated
- grad_mlp_norm_bias: float32 [1024], replicated
- grad_up_weight: float32 [1024, 4096], P(None, 'mp')
- grad_up_bias: float32 [4096], P('mp')
- grad_down_weight: float32 [4096, 1024], P('mp')
- grad_down_bias: float32 [1024], replicated
Inputs may be any that keep to these rules, and one draw needn't show every extreme that they name: `seq_lengths`: each data group's 4 entries, in row order, are the lengths of the sequences packed into its 2048 rows: each 512 or 1024, then zeros for unused slots; they sum to 2048, and some group holds a sequence of 1024. A permutation: skip-value head p reuses the first layer's value head value_owner[p].
All inputs are finite; a program needn't handle non-finite values.
Results may differ from a plain program's by a relative error of at most 0.019.
Values may be sent and summed in bfloat16 or wider, within the bound.
A program may use at most 128 MiB of HBM per device.

v0:
```python
import jax
import jax.numpy as jnp
from jax import lax
from jax.sharding import PartitionSpec as P

SHORT = 512


EPSILON = 1e-05
MASKED = -1e30
GELU_C = 0.7978845608028654


def layer_norm(values, scale_gain, scale_bias):
    average = jnp.mean(values, axis=-1, keepdims=True)
    centered = values - average
    variance = jnp.mean(centered * centered, axis=-1, keepdims=True)
    return centered * lax.rsqrt(variance + EPSILON) * scale_gain + scale_bias


def gelu_tanh(values):
    return 0.5 * values * (1.0 + jnp.tanh(GELU_C * (values + 0.044715 * values * values * values)))


def row_starts(lengths, group_rows):
    ends = jnp.cumsum(lengths)
    begins = ends - lengths
    positions = jnp.arange(group_rows, dtype=jnp.int32)
    inside = begins[None, :] <= positions[:, None]
    return jnp.max(jnp.where(inside, begins[None, :], 0), axis=1)


def block_mask(starts, first_row, block_rows, span):
    own_rows = first_row + jnp.arange(block_rows, dtype=jnp.int32)
    key_rows = first_row - (span - block_rows) + jnp.arange(span, dtype=jnp.int32)
    begin = lax.dynamic_slice_in_dim(starts, first_row, block_rows, 0)
    return (key_rows[None, :] >= begin[:, None]) & (key_rows[None, :] <= own_rows[:, None])


def rows_product(left, right):
    return lax.dot_general(
        left, right, (((0,), (0,)), ((), ())), preferred_element_type=jnp.float32
    )


def back_product(left, weight):
    return lax.dot_general(
        left, weight, (((1,), (1,)), ((), ())), preferred_element_type=jnp.float32
    )


def padded_pair(keys, values_in, long_len):
    zero_pad = jnp.zeros((long_len,) + keys.shape[1:], keys.dtype)
    return (jnp.concatenate([zero_pad, keys], 0), jnp.concatenate([zero_pad, values_in], 0))


def attend_forward(queries, keys, values_in, starts, long_len, block_rows):
    group_rows, heads, width = queries.shape
    span = long_len + block_rows
    scale = width ** (-0.5)
    keys_pad, values_pad = padded_pair(keys, values_in, long_len)

    def one_block(block_index):
        first_row = block_index * block_rows
        query_blk = lax.dynamic_slice_in_dim(queries, first_row, block_rows, 0)
        key_blk = lax.dynamic_slice_in_dim(keys_pad, first_row, span, 0)
        value_blk = lax.dynamic_slice_in_dim(values_pad, first_row, span, 0)
        allowed = block_mask(starts, first_row, block_rows, span)
        scores = (
            jnp.einsum("qhd,khd->hqk", query_blk, key_blk, preferred_element_type=jnp.float32)
            * scale
        )
        scores = jnp.where(allowed[None], scores, MASKED)
        top_score = jnp.max(scores, axis=-1, keepdims=True)
        weights = jnp.exp(scores - top_score)
        totals = jnp.sum(weights, axis=-1, keepdims=True)
        probs = (weights / totals).astype(jnp.bfloat16)
        mixed = jnp.einsum("hqk,khd->qhd", probs, value_blk, preferred_element_type=jnp.float32)
        return (mixed.astype(jnp.bfloat16), top_score[..., 0] + jnp.log(totals[..., 0]))

    mixed, log_totals = lax.map(one_block, jnp.arange(group_rows // block_rows, dtype=jnp.int32))
    return (mixed.reshape(group_rows, heads, width), log_totals)


def attend_backward(queries, keys, values_in, grad_mixed, log_totals, starts, long_len, block_rows):
    group_rows, heads, width = queries.shape
    span = long_len + block_rows
    scale = width ** (-0.5)
    keys_pad, values_pad = padded_pair(keys, values_in, long_len)

    def one_block(carried, block_index):
        grad_keys, grad_values = carried
        first_row = block_index * block_rows
        query_blk = lax.dynamic_slice_in_dim(queries, first_row, block_rows, 0)
        key_blk = lax.dynamic_slice_in_dim(keys_pad, first_row, span, 0)
        value_blk = lax.dynamic_slice_in_dim(values_pad, first_row, span, 0)
        grad_blk = lax.dynamic_slice_in_dim(grad_mixed, first_row, block_rows, 0)
        allowed = block_mask(starts, first_row, block_rows, span)
        scores = (
            jnp.einsum("qhd,khd->hqk", query_blk, key_blk, preferred_element_type=jnp.float32)
            * scale
        )
        probs = jnp.where(allowed[None], jnp.exp(scores - log_totals[block_index][:, :, None]), 0.0)
        grad_probs = jnp.einsum(
            "qhd,khd->hqk", grad_blk, value_blk, preferred_element_type=jnp.float32
        )
        inner = jnp.sum(probs * grad_probs, axis=-1, keepdims=True)
        grad_scores = (probs * (grad_probs - inner)).astype(jnp.bfloat16)
        grad_query = (
            jnp.einsum("hqk,khd->qhd", grad_scores, key_blk, preferred_element_type=jnp.float32)
            * scale
        )
        grad_key = (
            jnp.einsum("hqk,qhd->khd", grad_scores, query_blk, preferred_element_type=jnp.float32)
            * scale
        )
        grad_value = jnp.einsum(
            "hqk,qhd->khd", probs.astype(jnp.bfloat16), grad_blk, preferred_element_type=jnp.float32
        )
        grad_keys = lax.dynamic_update_slice_in_dim(
            grad_keys,
            lax.dynamic_slice_in_dim(grad_keys, first_row, span, 0) + grad_key,
            first_row,
            0,
        )
        grad_values = lax.dynamic_update_slice_in_dim(
            grad_values,
            lax.dynamic_slice_in_dim(grad_values, first_row, span, 0) + grad_value,
            first_row,
            0,
        )
        return ((grad_keys, grad_values), grad_query)

    zero_grads = jnp.zeros((long_len + group_rows, heads, width), jnp.float32)
    (grad_keys, grad_values), grad_queries = lax.scan(
        one_block, (zero_grads, zero_grads), jnp.arange(group_rows // block_rows, dtype=jnp.int32)
    )
    return (
        grad_queries.reshape(group_rows, heads, width),
        grad_keys[long_len:],
        grad_values[long_len:],
    )


def body(
    inputs,
    first_values,
    cotangent,
    seq_lengths,
    value_owner,
    attn_norm_gain,
    attn_norm_bias,
    qkv_weight,
    qv_bias,
    out_weight,
    out_bias,
    mlp_norm_gain,
    mlp_norm_bias,
    up_weight,
    up_bias,
    down_weight,
    down_bias,
):
    local_rows = inputs.shape[0]
    model_width = inputs.shape[1]
    group_rows = local_rows * lax.axis_size("mp")
    pairs_dev = qkv_weight.shape[1]
    head_size = qkv_weight.shape[3]
    heads_dev = 2 * pairs_dev
    all_pairs = value_owner.shape[0]
    long_len = 2 * SHORT
    block_rows = min(512, group_rows)
    starts = row_starts(seq_lengths, group_rows)
    all_first = lax.all_gather(first_values, "mp", axis=1, tiled=True)
    owners = lax.dynamic_slice_in_dim(value_owner, lax.axis_index("mp") * pairs_dev, pairs_dev, 0)
    skip_values = jnp.take(all_first, owners, axis=1)
    qkv_flat = qkv_weight.reshape(model_width, pairs_dev * 5 * head_size)
    out_flat = out_weight.reshape(heads_dev * head_size, model_width)

    def run_forward(layer_in):
        inputs_f = layer_in.astype(jnp.float32)
        normed_one = layer_norm(inputs_f, attn_norm_gain, attn_norm_bias).astype(jnp.bfloat16)
        rows_one = lax.all_gather(normed_one, "mp", axis=0, tiled=True)
        projected = jnp.dot(rows_one, qkv_flat, preferred_element_type=jnp.float32)
        projected = projected.reshape(group_rows, pairs_dev, 5, head_size)
        queries = (projected[:, :, 0:2] + qv_bias[None, :, 0:2]).astype(jnp.bfloat16)
        queries = queries.reshape(group_rows, heads_dev, head_size)
        keys = projected[:, :, 2:4].astype(jnp.bfloat16).reshape(group_rows, heads_dev, head_size)
        fresh = (projected[:, :, 4] + qv_bias[None, :, 2]).astype(jnp.bfloat16)
        values_all = jnp.stack([fresh, skip_values], axis=2).reshape(
            group_rows, heads_dev, head_size
        )
        mixed, log_totals = attend_forward(queries, keys, values_all, starts, long_len, block_rows)
        mixed_flat = mixed.reshape(group_rows, heads_dev * head_size)
        picked = mixed_flat
        residual = (
            inputs_f
            + lax.psum_scatter(
                jnp.dot(picked, out_flat, preferred_element_type=jnp.float32).astype(jnp.bfloat16),
                "mp",
                scatter_dimension=0,
                tiled=True,
            ).astype(jnp.float32)
            + out_bias
        )
        normed_two = layer_norm(residual, mlp_norm_gain, mlp_norm_bias).astype(jnp.bfloat16)
        rows_two = lax.all_gather(normed_two, "mp", axis=0, tiled=True)
        hidden_pre = jnp.dot(rows_two, up_weight, preferred_element_type=jnp.float32) + up_bias
        hidden = gelu_tanh(hidden_pre).astype(jnp.bfloat16)
        picked = hidden
        layer_out = (
            residual
            + lax.psum_scatter(
                jnp.dot(picked, down_weight, preferred_element_type=jnp.float32).astype(
                    jnp.bfloat16
                ),
                "mp",
                scatter_dimension=0,
                tiled=True,
            ).astype(jnp.float32)
            + down_bias
        )
        return (
            layer_out,
            inputs_f,
            residual,
            rows_one,
            queries,
            keys,
            values_all,
            log_totals,
            mixed_flat,
            rows_two,
            hidden_pre,
            hidden,
        )

    saved = run_forward(inputs)
    output = saved[0].astype(jnp.bfloat16)
    again_in = lax.optimization_barrier((inputs, saved[0]))[0]
    saved = run_forward(again_in)
    (
        inputs_f,
        residual,
        rows_one,
        queries,
        keys,
        values_all,
        log_totals,
        mixed_flat,
        rows_two,
        hidden_pre,
        hidden,
    ) = saved[1:]
    grad_out_f = cotangent.astype(jnp.float32)
    grad_rows = lax.all_gather(cotangent, "mp", axis=0, tiled=True)
    grad_hidden = back_product(grad_rows, down_weight)
    gelu_pair = jax.vjp(gelu_tanh, hidden_pre)
    grad_pre = gelu_pair[1](grad_hidden)[0].astype(jnp.bfloat16)
    grad_down_weight = rows_product(hidden, grad_rows)
    grad_up_weight = rows_product(rows_two, grad_pre)
    grad_up_bias = jnp.sum(grad_pre.astype(jnp.float32), axis=0)
    grad_down_bias = jnp.sum(grad_out_f, axis=0)
    grad_normed_two = lax.psum_scatter(
        back_product(grad_pre, up_weight).astype(jnp.bfloat16),
        "mp",
        scatter_dimension=0,
        tiled=True,
    ).astype(jnp.float32)
    norm_two_pair = jax.vjp(layer_norm, residual, mlp_norm_gain, mlp_norm_bias)
    grad_through, grad_mlp_norm_gain, grad_mlp_norm_bias = norm_two_pair[1](grad_normed_two)
    grad_residual = grad_out_f + grad_through
    grad_out_bias = jnp.sum(grad_residual, axis=0)
    resid_rows = lax.all_gather(grad_residual.astype(jnp.bfloat16), "mp", axis=0, tiled=True)
    grad_out_weight = rows_product(mixed_flat, resid_rows).reshape(out_weight.shape)
    grad_mixed = back_product(resid_rows, out_flat).astype(jnp.bfloat16)
    grad_mixed = grad_mixed.reshape(group_rows, heads_dev, head_size)
    grad_query, grad_key, grad_value = attend_backward(
        queries, keys, values_all, grad_mixed, log_totals, starts, long_len, block_rows
    )
    grad_value = grad_value.reshape(group_rows, pairs_dev, 2, head_size)
    grad_projected = jnp.concatenate(
        [
            grad_query.reshape(group_rows, pairs_dev, 2, head_size),
            grad_key.reshape(group_rows, pairs_dev, 2, head_size),
            grad_value[:, :, 0:1],
        ],
        axis=2,
    ).astype(jnp.bfloat16)
    grad_qv_bias = jnp.concatenate(
        [
            jnp.sum(grad_projected[:, :, 0:2].astype(jnp.float32), axis=0),
            jnp.sum(grad_projected[:, :, 4:5].astype(jnp.float32), axis=0),
        ],
        axis=1,
    )
    grad_flat = grad_projected.reshape(group_rows, pairs_dev * 5 * head_size)
    grad_qkv_weight = rows_product(rows_one, grad_flat).reshape(qkv_weight.shape)
    grad_normed_one = lax.psum_scatter(
        back_product(grad_flat, qkv_flat).astype(jnp.bfloat16),
        "mp",
        scatter_dimension=0,
        tiled=True,
    ).astype(jnp.float32)
    norm_one_pair = jax.vjp(layer_norm, inputs_f, attn_norm_gain, attn_norm_bias)
    grad_through_one, grad_attn_norm_gain, grad_attn_norm_bias = norm_one_pair[1](grad_normed_one)
    grad_inputs = (grad_residual + grad_through_one).astype(jnp.bfloat16)
    every_skip = lax.all_gather(grad_value[:, :, 1].astype(jnp.bfloat16), "mp", axis=1, tiled=True)
    owned = lax.axis_index("mp") * pairs_dev + jnp.arange(pairs_dev, dtype=jnp.int32)
    every_pair = jnp.arange(all_pairs, dtype=jnp.int32)
    inverse = jnp.sum(
        jnp.where(value_owner[None, :] == owned[:, None], every_pair[None, :], 0), axis=1
    )
    grad_first = jnp.take(every_skip, inverse, axis=1)
    weight_sums = (
        lax.psum(grad_qkv_weight.astype(jnp.bfloat16), "dp").astype(jnp.float32),
        lax.psum(grad_qv_bias.astype(jnp.bfloat16), "dp").astype(jnp.float32),
        lax.psum(grad_out_weight.astype(jnp.bfloat16), "dp").astype(jnp.float32),
        lax.psum(grad_up_weight.astype(jnp.bfloat16), "dp").astype(jnp.float32),
        lax.psum(grad_up_bias.astype(jnp.bfloat16), "dp").astype(jnp.float32),
        lax.psum(grad_down_weight.astype(jnp.bfloat16), "dp").astype(jnp.float32),
    )
    norm_sums = lax.psum(
        (
            grad_attn_norm_gain,
            grad_attn_norm_bias,
            grad_out_bias,
            grad_mlp_norm_gain,
            grad_mlp_norm_bias,
            grad_down_bias,
        ),
        ("dp", "mp"),
    )
    return (
        output,
        grad_inputs,
        grad_first,
        norm_sums[0],
        norm_sums[1],
        weight_sums[0],
        weight_sums[1],
        weight_sums[2],
        norm_sums[2],
        norm_sums[3],
        norm_sums[4],
        weight_sums[3],
        weight_sums[4],
        weight_sums[5],
        norm_sums[5],
    )


def solution(mesh):
    return jax.shard_map(
        body,
        mesh=mesh,
        in_specs=(
            P(("dp", "mp"), None),
            P("dp", "mp", None),
            P(("dp", "mp"), None),
            P("dp"),
            P(),
            P(),
            P(),
            P(None, "mp", None, None),
            P("mp", None, None),
            P("mp", None, None, None),
            P(),
            P(),
            P(),
            P(None, "mp"),
            P("mp"),
            P("mp", None),
            P(),
        ),
        out_specs=(
            P(("dp", "mp"), None),
            P(("dp", "mp"), None),
            P("dp", "mp", None),
            P(),
            P(),
            P(None, "mp", None, None),
            P("mp", None, None),
            P("mp", None, None, None),
            P(),
            P(),
            P(),
            P(None, "mp"),
            P("mp"),
            P("mp", None),
            P(),
        ),
        check_vma=False,
    )
```

profile of v0, /device:TPU:0, one launch (start us, length us, event | category | flops | bytes accessed | tf_op | source)
XLA Modules:
  0.0 1231.9 jit_solution(12711491678477917356)
XLA Ops:
  13.3 21.6 %all-gather.12.cloned.1.call-done = bf16[2048,8,64]{0,2,1:T(8,128)(2,1)} async-done(((bf16[2048,2,64]{0,2,1:T(8,128)(2,1)}), bf16[2048,8,64]{0,2,1:T(8,128)(2,1)}) %all-gather.12.cloned.1.call-update) | async-done | bytes 2097168 | tf_op jit(solution)/shard_map/all_gather | solution.py:174
  38.0 33.5 %all-gather.10.cloned.1.call-done = bf16[2048,1024]{1,0:T(8,128)(2,1)} async-done(((bf16[512,1024]{1,0:T(8,128)(2,1)}), bf16[2048,1024]{1,0:T(8,128)(2,1)}) %all-gather.10.cloned.1.call-update) | async-done | bytes 4194320 | tf_op jit(solution)/shard_map/all_gather | solution.py:183
  81.7 132.5 %while.42 = (s32[]{:T(128)}, bf16[4,512,4,64]{1,3,2,0:T(8,128)(2,1)}, s32[4]{0:T(128)S(1)}, bf16[3072,4,64]{0,2,1:T(8,128)(2,1)}, s32[2048]{0:T(1024)S(1)}, /*in...) while((s32[]{:T(128)}, ...), condition=%wide.region_7.9_spmd, body=%wide.region_4.8_spmd.sunk | while | flops 832966144 | bytes 60332316 | solution.py:81
  91.2 16.2 %fusion.196 = (f32[4,512]{1,0:T(4,128)S(1)}, f32[4,512,1536]{2,1,0:T(8,128)}) fusion(f32[4,512,1536]{2,1,0:T(8,128)} %fusion.195, pred[512,1536]{1,0:T(8,128)(4,1)S(1)} %compare_and_fusion.8), kind=kOutput, calls=%fused_computation.224.clone.1 | output fusion | flops 18875904 | bytes 25960448 | tf_op jit(solution)/shard_map/while/body/eval_jaxpr/sub | solution.py:75
  124.4 16.2 %fusion.196 = (f32[4,512]{1,0:T(4,128)S(1)}, f32[4,512,1536]{2,1,0:T(8,128)}) fusion(f32[4,512,1536]{2,1,0:T(8,128)} %fusion.195, pred[512,1536]{1,0:T(8,128)(4,1)S(1)} %compare_and_fusion.8), kind=kOutput, calls=%fused_computation.224.clone.1 | output fusion | flops 18875904 | bytes 25960448 | tf_op jit(solution)/shard_map/while/body/eval_jaxpr/sub | solution.py:75
  157.5 16.2 %fusion.196 = (f32[4,512]{1,0:T(4,128)S(1)}, f32[4,512,1536]{2,1,0:T(8,128)}) fusion(f32[4,512,1536]{2,1,0:T(8,128)} %fusion.195, pred[512,1536]{1,0:T(8,128)(4,1)S(1)} %compare_and_fusion.8), kind=kOutput, calls=%fused_computation.224.clone.1 | output fusion | flops 18875904 | bytes 25960448 | tf_op jit(solution)/shard_map/while/body/eval_jaxpr/sub | solution.py:75
  190.6 16.2 %fusion.196 = (f32[4,512]{1,0:T(4,128)S(1)}, f32[4,512,1536]{2,1,0:T(8,128)}) fusion(f32[4,512,1536]{2,1,0:T(8,128)} %fusion.195, pred[512,1536]{1,0:T(8,128)(4,1)S(1)} %compare_and_fusion.8), kind=kOutput, calls=%fused_computation.224.clone.1 | output fusion | flops 18875904 | bytes 25960448 | tf_op jit(solution)/shard_map/while/body/eval_jaxpr/sub | solution.py:75
  220.2 44.4 %reduce-scatter.6.cloned.1.call-done = bf16[512,1024]{1,0:T(8,128)(2,1)} async-done(((bf16[2048,1024]{1,0:T(8,128)(2,1)}), bf16[512,1024]{1,0:T(8,128)(2,1)}) %reduce-scatter.6.cloned.1.call-update) | async-done | bytes 1048592 | tf_op jit(solution)/shard_map/reduce_scatter | solution.py:198
  268.6 34.6 %all-gather.14.cloned.1.call-done = bf16[2048,1024]{1,0:T(8,128)(2,1)} async-done(((bf16[512,1024]{1,0:T(8,128)(2,1)}), bf16[2048,1024]{1,0:T(8,128)(2,1)}) %all-gather.14.cloned.1.call-update) | async-done | bytes 4194320 | tf_op jit(solution)/shard_map/all_gather | solution.py:207
  303.2 12.9 %fusion.81 = bf16[2048,1024]{1,0:T(8,128)(2,1)} fusion(bf16[1024,1024]{1,0:T(8,128)(2,1)} %param.40, f32[1024]{0:T(1024)S(1)} %copy-done.60, bf16[2048,1024]{1,0:T(8,128)(2,1)} %all-gather.14.cloned.1.call-done, bf16[1024,1024]{1,0:T(8,128)(2,1)S(1)} %copy-done), kind=kOutput, calls=%fused_computation.106 | convolution fusion | flops 8613003264 | bytes 12587008 | tf_op jit(solution)/shard_map/dot_general | solution.py:214
  316.2 44.7 %reduce-scatter.8.cloned.1.call-done = bf16[512,1024]{1,0:T(8,128)(2,1)} async-done(((bf16[2048,1024]{1,0:T(8,128)(2,1)}), bf16[512,1024]{1,0:T(8,128)(2,1)}) %reduce-scatter.8.cloned.1.call-update) | async-done | bytes 1048592 | tf_op jit(solution)/shard_map/reduce_scatter | solution.py:213
  367.8 34.1 %all-gather.16.cloned.1.call-done = bf16[2048,1024]{1,0:T(8,128)(2,1)} async-done(((bf16[512,1024]{1,0:T(8,128)(2,1)}), bf16[2048,1024]{1,0:T(8,128)(2,1)}) %all-gather.16.cloned.1.call-update) | async-done | bytes 4194320 | tf_op jit(solution)/shard_map/all_gather | solution.py:183
  412.4 55.7 %while.43 = (s32[]{:T(128)}, bf16[4,512,4,64]{1,3,2,0:T(8,128)(2,1)}, f32[4,4,512]{2,1,0:T(4,128)S(1)}, s32[4]{0:T(128)S(1)}, bf16[3072,4,64]{0,2,1:T(8,128)(2,1...) while((s32[]{:T(128)}, ...), condition=%wide.region_17.19_spmd, body=%wide.region_14.18_spmd.sunk | while | flops 845545472 | bytes 49371432 | solution.py:81
  475.1 44.5 %reduce-scatter.10.cloned.1.call-done = bf16[512,1024]{1,0:T(8,128)(2,1)} async-done(((bf16[2048,1024]{1,0:T(8,128)(2,1)}), bf16[512,1024]{1,0:T(8,128)(2,1)}) %reduce-scatter.10.cloned.1.call-update) | async-done | bytes 1048592 | tf_op jit(solution)/shard_map/reduce_scatter | solution.py:198
  524.3 33.8 %all-gather.18.cloned.1.call-done = bf16[2048,1024]{1,0:T(8,128)(2,1)} async-done(((bf16[512,1024]{1,0:T(8,128)(2,1)}), bf16[2048,1024]{1,0:T(8,128)(2,1)}) %all-gather.18.cloned.1.call-update) | async-done | bytes 4194320 | tf_op jit(solution)/shard_map/all_gather | solution.py:207
  567.0 27.1 %all-gather.20.cloned.1.call-done = bf16[2048,1024]{1,0:T(8,128)(2,1)} async-done(((bf16[512,1024]{1,0:T(8,128)(2,1)}), bf16[2048,1024]{1,0:T(8,128)(2,1)}) %all-gather.20.cloned.1.call-update) | async-done | bytes 4194320 | tf_op jit(solution)/shard_map/all_gather | solution.py:256
  594.2 15.5 %fusion.141 = (bf16[1024]{0:T(1024)(128)(2,1)}, bf16[2048,1024]{1,0:T(8,128)(2,1)S(1)}) fusion(f32[2048,1024]{1,0:T(8,128)} %fusion.146, f32[1024]{0:T(1024)S(1)} %copy-done.61, bf16[2048,1024]{1,0:T(8,128)(2,1)} %all-gather.20.cloned.1.call-done, bf16[1024,1024]{1,0:T(8,128)(2,1)} %param.40), kind=kOutput, calls=%fused_computation.222 | convolution fusion | flops 4349492224 | bytes 18880512 | tf_op jit(solution)/shard_map/dot_general | solution.py:47
  618.2 44.5 %reduce-scatter.12.cloned.1.call-done = bf16[512,1024]{1,0:T(8,128)(2,1)} async-done(((bf16[2048,1024]{1,0:T(8,128)(2,1)}), bf16[512,1024]{1,0:T(8,128)(2,1)}) %reduce-scatter.12.cloned.1.call-update) | async-done | bytes 1048592 | tf_op jit(solution)/shard_map/reduce_scatter | solution.py:264
  681.5 25.1 %all-gather.22.cloned.1.call-done = bf16[2048,1024]{1,0:T(8,128)(2,1)} async-done(((bf16[512,1024]{1,0:T(8,128)(2,1)}), bf16[2048,1024]{1,0:T(8,128)(2,1)}) %all-gather.22.cloned.1.call-update) | async-done | bytes 4194320 | tf_op jit(solution)/shard_map/all_gather | solution.py:274
  715.1 180.9 %while.44 = (s32[]{:T(128)}, f32[3072,4,64]{0,2,1:T(8,128)}, f32[3072,4,64]{0,2,1:T(8,128)}, bf16[4,512,4,64]{1,0,3,2:T(4,128)(2,1)}, s32[4]{0:T(128)S(1)}, /*in...) while((s32[]{:T(128)}, f32[3072,4,64]{0,2,1:T(8,128)}, ...), condition=%wide.region_26.28_spmd, body=%wide.region_24.27_spmd.sunk | while | flops 2045378560 | bytes 163641856 | solution.py:135
  935.7 22.6 %all-reduce.5 = (bf16[2,3,64]{2,1,0:T(4,128)(2,1)S(1)}, bf16[1024]{0:T(1024)(128)(2,1)S(1)}) all-reduce(bf16[2,3,64]{2,1,0:T(4,128)(2,1)S(1)} %pad_maximum_fusion.2, bf16[1024]{0:T(1024)(128)(2,1)S(1)} %copy-done.54), channel_id=1, replica_groups=mesh['dp'=8,'mp'=4] {'dp'}, use_global_device_ids=true, to_apply=%region_38.40 | all-reduce | flops 1408 | bytes 5632 | tf_op jit(solution)/shard_map/psum | solution.py:317
  962.6 169.7 %all-reduce.9.cloned.1.call-done = (bf16[1024,2,5,64]{0,3,2,1:T(8,128)(2,1)}, bf16[2,2,64,1024]{3,2,1,0:T(8,128)(2,1)}, bf16[1024,1024]{1,0:T(8,128)(2,1)}, bf16[1024,1024]{1,0:T(8,128)(2,1)}) async-done(((bf16[1024,2,5,64]{0,3,2,1:T(8,128)(2,1)}, bf16[2,2,64,1024]{3,2,1,0:T(8,128)(2,1)}, bf16[1024,1024]{1,0:T(8,128)(2,1)}, bf16[1024,1024]{1,0:T(8,128)(2,1)}), (bf16[1024,2,5,64]{0,3,2,1:T(8,128)(2,1)}, ...) | async-done | bytes 6029328 | tf_op jit(solution)/shard_map/psum | solution.py:316
  1143.2 35.2 %reduce-scatter.14.cloned.1.call-done = bf16[512,1024]{1,0:T(8,128)(2,1)} async-done(((bf16[2048,1024]{1,0:T(8,128)(2,1)}), bf16[512,1024]{1,0:T(8,128)(2,1)}) %reduce-scatter.14.cloned.1.call-update) | async-done | bytes 1048592 | tf_op jit(solution)/shard_map/reduce_scatter | solution.py:299
  1181.7 39.9 %all-reduce.4 = (f32[1024]{0:T(1024)}, f32[1024]{0:T(1024)}, f32[1024]{0:T(1024)}, f32[1024]{0:T(1024)}, f32[1024]{0:T(1024)}, /*index=5*/f32[1024]{0:T(1024)}) all-reduce(f32[1024]{0:T(1024)S(1)} %get-tuple-element.386, f32[1024]{0:T(1024)S(1)} %get-tuple-element.390, ...), channel_id=1, replica_groups=mesh['dp'=8,'mp'=4] {'dp','mp'}, use_global_device_ids=true, to_apply=%region_32.34 | all-reduce | flops 6144 | bytes 49152 | tf_op jit(solution)/shard_map/psum | solution.py:323
  (423 shorter events, 451.9 us)
Async XLA Ops:
  7.2 296.0 %copy-start = (bf16[1024,1024]{1,0:T(8,128)(2,1)S(1)}, bf16[1024,1024]{1,0:T(8,128)(2,1)}, u32[]{:S(2)}) copy-start(bf16[1024,1024]{1,0:T(8,128)(2,1)} %param.38) | copy-start | bytes 6291460
  7.2 27.7 %all-gather.12.cloned.1.call-start = ((), (), s32[]{:S(2)}) async-start(), calls=%async_computation.6 | async-start | bytes 2621440 | tf_op jit(solution)/shard_map/all_gather | solution.py:174
  8.0 63.5 %all-gather.10.cloned.1.call-start = ((), (), s32[]{:S(2)}) async-start(), calls=%async_computation.5 | async-start | bytes 5242880 | tf_op jit(solution)/shard_map/all_gather | solution.py:183
  12.8 251.8 %reduce-scatter.6.cloned.1.call-start = ((), (), s32[]{:S(2)}) async-start(), calls=%async_computation.7 | async-start | bytes 5242880 | tf_op jit(solution)/shard_map/reduce_scatter | solution.py:198
  13.0 63.9 %copy-start.40 = (f32[2,2,64]{2,1,0:T(2,128)}, f32[2,2,64]{2,1,0:T(2,128)S(1)}, u32[]{:S(2)}) copy-start(f32[2,2,64]{2,1,0:T(2,128)S(1)} %copy.44) | copy-start | bytes 3076
  13.3 63.5 %copy-start.50 = (f32[2,64]{1,0:T(2,128)}, f32[2,64]{1,0:T(2,128)S(1)}, u32[]{:S(2)}) copy-start(f32[2,64]{1,0:T(2,128)S(1)} %slice_bitcast_fusion) | copy-start | bytes 1540
  219.9 47.1 %copy-start.29 = (f32[1024]{0:T(1024)S(1)}, f32[1024]{0:T(1024)}, u32[]{:S(2)}) copy-start(f32[1024]{0:T(1024)} %param.36) | copy-start | bytes 12292
  219.9 47.1 %copy-start.44 = (f32[1024]{0:T(1024)S(1)}, f32[1024]{0:T(1024)}, u32[]{:S(2)}) copy-start(f32[1024]{0:T(1024)} %param.37) | copy-start | bytes 12292
  219.9 83.3 %all-gather.14.cloned.1.call-start = ((), (), s32[]{:S(2)}) async-start(), calls=%async_computation.8 | async-start | bytes 5242880 | tf_op jit(solution)/shard_map/all_gather | solution.py:207
  268.6 92.3 %reduce-scatter.8.cloned.1.call-start = ((), (), s32[]{:S(2)}) async-start(), calls=%async_computation.9 | async-start | bytes 5242880 | tf_op jit(solution)/shard_map/reduce_scatter | solution.py:213
  316.2 49.7 %copy-start.32 = (f32[1024]{0:T(1024)S(1)}, f32[1024]{0:T(1024)}, u32[]{:S(2)}) copy-start(f32[1024]{0:T(1024)} %param.30) | copy-start | bytes 12292
  316.2 49.7 %copy-start.43 = (f32[1024]{0:T(1024)S(1)}, f32[1024]{0:T(1024)}, u32[]{:S(2)}) copy-start(f32[1024]{0:T(1024)} %param.31) | copy-start | bytes 12292
  316.2 85.8 %all-gather.16.cloned.1.call-start = ((), (), s32[]{:S(2)}) async-start(), calls=%async_computation.10 | async-start | bytes 5242880 | tf_op jit(solution)/shard_map/all_gather | solution.py:183
  367.3 152.2 %reduce-scatter.10.cloned.1.call-start = ((), (), s32[]{:S(2)}) async-start(), calls=%async_computation.11 | async-start | bytes 5242880 | tf_op jit(solution)/shard_map/reduce_scatter | solution.py:198
  474.8 47.1 %copy-start.30 = (f32[1024]{0:T(1024)S(1)}, f32[1024]{0:T(1024)}, u32[]{:S(2)}) copy-start(f32[1024]{0:T(1024)} %param.36) | copy-start | bytes 12292
  474.8 47.0 %copy-start.45 = (f32[1024]{0:T(1024)S(1)}, f32[1024]{0:T(1024)}, u32[]{:S(2)}) copy-start(f32[1024]{0:T(1024)} %param.37) | copy-start | bytes 12292
  474.8 83.3 %all-gather.18.cloned.1.call-start = ((), (), s32[]{:S(2)}) async-start(), calls=%async_computation.12 | async-start | bytes 5242880 | tf_op jit(solution)/shard_map/all_gather | solution.py:207
  523.5 70.7 %all-gather.20.cloned.1.call-start = ((), (), s32[]{:S(2)}) async-start(), calls=%async_computation.13 | async-start | bytes 5242880 | tf_op jit(solution)/shard_map/all_gather | solution.py:256
  524.2 70.0 %copy-start.61 = (f32[1024]{0:T(1024)S(1)}, f32[1024]{0:T(1024)}, u32[]{:S(2)}) copy-start(f32[1024]{0:T(1024)} %param.39) | copy-start | bytes 12292
  524.2 138.5 %reduce-scatter.12.cloned.1.call-start = ((), (), s32[]{:S(2)}) async-start(), calls=%async_computation.14 | async-start | bytes 5242880 | tf_op jit(solution)/shard_map/reduce_scatter | solution.py:264
  617.9 88.7 %all-gather.22.cloned.1.call-start = ((), (), s32[]{:S(2)}) async-start(), calls=%async_computation.15 | async-start | bytes 5242880 | tf_op jit(solution)/shard_map/all_gather | solution.py:274
  672.0 287.5 %all-gather.24.cloned.1.call-start = ((), (), s32[]{:S(2)}) async-start(), calls=%async_computation.17 | async-start | bytes 2621440 | tf_op jit(solution)/shard_map/all_gather | solution.py:308
  898.9 233.5 %all-reduce.9.cloned.1.call-start = ((), (), s32[]{:S(2)}) async-start(), calls=%async_computation.18 | async-start | bytes 12058624 | tf_op jit(solution)/shard_map/psum | solution.py:316
  924.0 254.4 %reduce-scatter.14.cloned.1.call-start = ((), (), s32[]{:S(2)}) async-start(), calls=%async_computation.16 | async-start | bytes 5242880 | tf_op jit(solution)/shard_map/reduce_scatter | solution.py:299
  (77 other events, 864.8 us)
Sparse Core Ops, SparseCore 0:
  9.6 25.2 all-gather.11
  37.0 34.4 all-gather.9
  220.0 44.5 reduce-scatter.5
  268.7 34.4 all-gather.13
  316.3 44.5 reduce-scatter.7
  367.5 34.4 all-gather.15
  474.9 44.5 reduce-scatter.9
  523.6 34.4 all-gather.17
  559.7 34.4 all-gather.19
  618.0 44.5 reduce-scatter.11
  672.1 34.4 all-gather.21
  899.0 22.5 all-gather.23
  927.4 204.9 all-reduce.8
  1134.7 43.6 reduce-scatter.13
where the time goes:
time: 1250 us; the launch traced here: 1230 us
  waiting for transfers between devices  594 us (48%)
  matrix products  280 us (22%)
  other arithmetic  162 us (13%)
  local copies, waits for them, and re-layouts  99.3 us (8%)
  blocking collectives  62.6 us (5%)
  loops' own time  16.7 us (1%)
  between operations  14.9 us (1%)
    psum x1, waiting for transfers between devices, body(): lax.psum(grad_qkv_weight.astype(jnp.bfloat16), 'dp').astype(jnp.float32)  170 us
    reduce_scatter x2, waiting for transfers between devices, run_forward(): lax.psum_scatter(jnp.dot(picked, out_flat, preferred_element_type=jnp.flo...  88.9 us
    dot_general x12, matrix products, one_block(): jnp.einsum('qhd,khd->hqk', query_blk, key_blk, preferred_element_type=jnp...  78.7 us
    all_gather x2, waiting for transfers between devices, run_forward(): rows_two = lax.all_gather(normed_two, 'mp', axis=0, tiled=True)  68.4 us
    all_gather x2, waiting for transfers between devices, run_forward(): rows_one = lax.all_gather(normed_one, 'mp', axis=0, tiled=True)  67.7 us
    sub x4, other arithmetic, one_block(): weights = jnp.exp(scores - top_score)  64.7 us
    dot_general x8, matrix products, one_block(): jnp.einsum('hqk,khd->qhd', probs, value_blk, preferred_element_type=jnp.f...  47.8 us
    reduce_scatter x1, waiting for transfers between devices, run_forward(): lax.psum_scatter(jnp.dot(picked, down_weight, preferred_element_type=jnp....  44.7 us
  transfers between devices with their start and end apart: 14, of which 13 were waited for; matrix products, arithmetic and copies ran while one was open for 6% of the time, Pallas kernels for 0%

commit v1 on v0

v1 whole, which is shorter than its diff:
```python
import functools

import jax
import jax.numpy as jnp
from jax import lax
from jax.experimental import pallas as pl
from jax.experimental.pallas import tpu as pltpu
from jax.sharding import PartitionSpec as P

SHORT = 512
QROWS = 256
LANES = 128
PACK = 6

EPSILON = 1e-05
MASKED = -1e30
GELU_C = 0.7978845608028654
BF16 = jnp.bfloat16
F32 = jnp.float32


def layer_norm(values, scale_gain, scale_bias):
    average = jnp.mean(values, axis=-1, keepdims=True)
    centered = values - average
    variance = jnp.mean(centered * centered, axis=-1, keepdims=True)
    return centered * lax.rsqrt(variance + EPSILON) * scale_gain + scale_bias


def gelu_tanh(values):
    return 0.5 * values * (1.0 + jnp.tanh(GELU_C * (values + 0.044715 * values * values * values)))


def rows_product(left, right):
    return lax.dot_general(left, right, (((0,), (0,)), ((), ())), preferred_element_type=F32)


def back_product(left, weight):
    return lax.dot_general(left, weight, (((1,), (1,)), ((), ())), preferred_element_type=F32)


def product(left, right):
    return jnp.dot(left, right, preferred_element_type=F32)


def opens_at(lengths, row):
    begin, opens = jnp.int32(0), jnp.int32(0)
    for slot in range(lengths.shape[0]):
        opens = jnp.maximum(opens, jnp.where(begin == row, 1, 0))
        begin = begin + lengths[slot]
    return opens


def head_lanes(head):
    lane = lax.broadcasted_iota(jnp.int32, (1, LANES), 1)
    return (lane < LANES // 2) if head == 0 else (lane >= LANES // 2)


def causal_tile():
    row = lax.broadcasted_iota(jnp.int32, (QROWS, QROWS), 0)
    column = lax.broadcasted_iota(jnp.int32, (QROWS, QROWS), 1)
    return column <= row


def pick_values(half, qkv_ref, first_ref, value_ref):
    held = first_ref[0]
    if held.shape[1] < LANES:
        turned = jnp.concatenate([held, held], axis=1)
    else:
        turned = jnp.concatenate([held[:, LANES // 2 :], held[:, : LANES // 2]], axis=1)
        turned = jnp.where(half == 1, held, turned)
    value_ref[...] = jnp.where(head_lanes(0), qkv_ref[:, 2 * LANES : 3 * LANES], turned)


def attend_forward_kernel(pairs, lengths, owner, place, qkv_ref, first_ref, mixed_ref, totals_ref, value_ref):
    pick_values(lax.rem(owner[place[0] * pairs + pl.program_id(0)], pairs), qkv_ref, first_ref, value_ref)
    blocks = qkv_ref.shape[0] // SHORT
    scale = (LANES // 2) ** (-0.5)

    def block(index, carried):
        base = pl.multiple_of(index * SHORT, SHORT)
        for half in range(SHORT // QROWS):
            first = base + half * QROWS

            def attend(with_previous):
                query = qkv_ref[pl.ds(first, QROWS), 0:LANES] * jnp.asarray(scale, BF16)
                spans = []
                if with_previous:
                    spans.append((base - SHORT, SHORT))
                if half:
                    spans.append((base, half * QROWS))
                spans.append((first, QROWS))
                mixed = jnp.zeros((QROWS, LANES), F32)
                totals = []
                for head in range(2):
                    chosen = head_lanes(head)
                    query_head = jnp.where(chosen, query, jnp.zeros_like(query))
                    scores = [
                        back_product(query_head, qkv_ref[pl.ds(at, size), LANES : 2 * LANES])
                        for at, size in spans
                    ]
                    scores[-1] = jnp.where(causal_tile(), scores[-1], MASKED)
                    top = scores[0].max(axis=1, keepdims=True)
                    for part in scores[1:]:
                        top = jnp.maximum(top, part.max(axis=1, keepdims=True))
                    total = jnp.zeros((QROWS, 1), F32)
                    gathered = jnp.zeros((QROWS, LANES), F32)
                    for (at, size), part in zip(spans, scores):
                        weights = jnp.exp(part - top)
                        total = total + weights.sum(axis=1, keepdims=True)
                        values = value_ref[pl.ds(at, size), :]
                        values = jnp.where(chosen, values, jnp.zeros_like(values))
                        gathered = gathered + product(weights.astype(BF16), values)
                    mixed = mixed + gathered / total
                    totals.append(top + jnp.log(total))
                mixed_ref[pl.ds(first, QROWS), :] = mixed.astype(BF16)
                totals_ref[pl.ds(first, QROWS), :] = jnp.where(
                    head_lanes(0), totals[0], totals[1]
                )

            @pl.when(opens_at(lengths, base) == 0)
            def _():
                attend(True)

            @pl.when(opens_at(lengths, base) == 1)
            def _():
                attend(False)

        return carried

    lax.fori_loop(0, blocks, block, 0)


def attend_backward_kernel(
    pairs, lengths, owner, place, qkv_ref, first_ref, grad_ref, totals_ref, out_ref, key_sum, value_sum, value_ref
):
    pick_values(lax.rem(owner[place[0] * pairs + pl.program_id(0)], pairs), qkv_ref, first_ref, value_ref)
    blocks = qkv_ref.shape[0] // SHORT
    scale = (LANES // 2) ** (-0.5)
    key_sum[...] = jnp.zeros_like(key_sum)
    value_sum[...] = jnp.zeros_like(value_sum)

    def block(index, carried):
        base = pl.multiple_of(index * SHORT, SHORT)
        for half in range(SHORT // QROWS):
            first = base + half * QROWS

            def attend(with_previous):
                query = qkv_ref[pl.ds(first, QROWS), 0:LANES] * jnp.asarray(scale, BF16)
                grad = grad_ref[pl.ds(first, QROWS), :]
                spans = []
                if with_previous:
                    spans.append((base - SHORT, SHORT))
                if half:
                    spans.append((base, half * QROWS))
                spans.append((first, QROWS))
                grad_query = jnp.zeros((QROWS, LANES), F32)
                for head in range(2):
                    chosen = head_lanes(head)
                    query_head = jnp.where(chosen, query, jnp.zeros_like(query))
                    grad_head = jnp.where(chosen, grad, jnp.zeros_like(grad))
                    at_lane = head * (LANES // 2)
                    totals = totals_ref[pl.ds(first, QROWS), at_lane : at_lane + 1]
                    probs, grads = [], []
                    inner = jnp.zeros((QROWS, 1), F32)
                    for at, size in spans:
                        keys = qkv_ref[pl.ds(at, size), LANES : 2 * LANES]
                        part = jnp.exp(back_product(query_head, keys) - totals)
                        if at is first:
                            part = jnp.where(causal_tile(), part, 0.0)
                        values = value_ref[pl.ds(at, size), :]
                        weighted = part * back_product(grad_head, values)
                        inner = inner + weighted.sum(axis=1, keepdims=True)
                        probs.append(part)
                        grads.append(weighted)
                    for (at, size), part, weighted in zip(spans, probs, grads):
                        keys = qkv_ref[pl.ds(at, size), LANES : 2 * LANES]
                        keys = jnp.where(chosen, keys, jnp.zeros_like(keys))
                        grad_scores = (weighted - part * inner).astype(BF16)
                        grad_query = grad_query + product(grad_scores, keys)
                        key_sum[pl.ds(at, size), :] += rows_product(grad_scores, query_head)
                        value_sum[pl.ds(at, size), :] += rows_product(part.astype(BF16), grad_head)
                out_ref[pl.ds(first, QROWS), 0:LANES] = (grad_query * scale).astype(BF16)

            @pl.when(opens_at(lengths, base) == 0)
            def _():
                attend(True)

            @pl.when(opens_at(lengths, base) == 1)
            def _():
                attend(False)

        return carried

    lax.fori_loop(0, blocks, block, 0)
    out_ref[:, LANES : 2 * LANES] = key_sum[...].astype(BF16)
    out_ref[:, 2 * LANES : 3 * LANES] = value_sum[...].astype(BF16)


def attend_forward(lengths, owner, place, packed, firsts):
    rows, pairs = packed.shape[0], packed.shape[1] // (3 * LANES)
    return pl.pallas_call(
        functools.partial(attend_forward_kernel, pairs),
        grid_spec=pltpu.PrefetchScalarGridSpec(
            num_scalar_prefetch=3,
            grid=(pairs,),
            in_specs=[
                pl.BlockSpec((rows, 3 * LANES), lambda p, c, o, m: (0, p)),
                pl.BlockSpec((1, rows, firsts.shape[2]), lambda p, c, o, m: (lax.div(o[m[0] * pairs + p], pairs), 0, 0)),
            ],
            out_specs=[
                pl.BlockSpec((rows, LANES), lambda p, c, o, m: (0, p)),
                pl.BlockSpec((rows, LANES), lambda p, c, o, m: (0, p)),
            ],
            scratch_shapes=[pltpu.VMEM((rows, LANES), BF16)],
        ),
        out_shape=[
            jax.ShapeDtypeStruct((rows, pairs * LANES), BF16),
            jax.ShapeDtypeStruct((rows, pairs * LANES), F32),
        ],
        cost_estimate=pl.CostEstimate(
            flops=rows * 1024 * 256 * 4 * pairs, bytes_accessed=8 << 20, transcendentals=rows * 2048
        ),
        name="attend_forward",
    )(lengths, owner, place, packed, firsts)


def attend_backward(lengths, owner, place, packed, firsts, grad, totals):
    rows, pairs = packed.shape[0], packed.shape[1] // (3 * LANES)
    return pl.pallas_call(
        functools.partial(attend_backward_kernel, pairs),
        grid_spec=pltpu.PrefetchScalarGridSpec(
            num_scalar_prefetch=3,
            grid=(pairs,),
            in_specs=[
                pl.BlockSpec((rows, 3 * LANES), lambda p, c, o, m: (0, p)),
                pl.BlockSpec((1, rows, firsts.shape[2]), lambda p, c, o, m: (lax.div(o[m[0] * pairs + p], pairs), 0, 0)),
                pl.BlockSpec((rows, LANES), lambda p, c, o, m: (0, p)),
                pl.BlockSpec((rows, LANES), lambda p, c, o, m: (0, p)),
            ],
            out_specs=pl.BlockSpec((rows, 3 * LANES), lambda p, c, o, m: (0, p)),
            scratch_shapes=[
                pltpu.VMEM((rows, LANES), F32),
                pltpu.VMEM((rows, LANES), F32),
                pltpu.VMEM((rows, LANES), BF16),
            ],
        ),
        out_shape=jax.ShapeDtypeStruct((rows, pairs * 3 * LANES), BF16),
        cost_estimate=pl.CostEstimate(
            flops=rows * 1024 * 256 * 10 * pairs, bytes_accessed=8 << 20, transcendentals=rows * 2048
        ),
        name="attend_backward",
    )(lengths, owner, place, packed, firsts, grad, totals)


def mesh_place(count):
    place = lax.axis_index("mp")
    core = lax.rem(place, 2)
    chip = lax.div(place, 2)
    chips = count // 2

    def across(step, other):
        return lax.rem(chip + step + chips, chips) * 2 + (1 - core if other else core)

    return place, place + 1 - 2 * core, across


def remote(source, target, sems, index, device):
    return pltpu.make_async_remote_copy(
        src_ref=source,
        dst_ref=target,
        send_sem=sems.at[(0, *index)],
        recv_sem=sems.at[(1, *index)],
        device_id={"mp": device},
        device_id_type=pl.DeviceIdType.MESH,
    )


def greet(count, copies=0):
    place, partner, across = mesh_place(count)
    barrier = pltpu.get_barrier_semaphore()
    for device in [partner] + [across(step, False) for step in range(1, count // 2)]:
        pl.semaphore_signal(
            barrier, inc=1, device_id={"mp": device}, device_id_type=pl.DeviceIdType.MESH
        )
    others = DpPlace(copies).greet(barrier) if copies else 0
    pl.semaphore_wait(barrier, count // 2 + others)


def each(count, step):
    def run(index, carried):
        step(index)
        return carried

    lax.fori_loop(0, count, run, 0)


class Gather:
    def __init__(self, count, out_ref, chunk, near, far, passed):
        self.count, self.out, self.chunk = count, out_ref, chunk
        self.near, self.far, self.passed = near, far, passed
        self.place, self.partner, self.across = mesh_place(count)

    def part(self, owner, index):
        return self.out.at[owner, pl.ds(pl.multiple_of(index * self.chunk, self.chunk), self.chunk), :]

    def send(self, index):
        own = self.part(self.place, index)
        for step in range(1, self.count // 2):
            remote(own, own, self.far, (step - 1, index), self.across(step, False)).start()
        remote(own, own, self.near, (index,), self.partner).start()

    def hand_on(self, index):
        for step in range(1, self.count // 2):
            got = self.part(self.across(-step, False), index)
            remote(got, got, self.far, (step - 1, index), self.across(step, False)).wait_recv()
            remote(got, got, self.passed, (step - 1, index), self.partner).start()

    def finish(self, index):
        own = self.part(self.place, index)
        near = self.part(self.partner, index)
        remote(own, near, self.near, (index,), self.partner).wait()
        for step in range(1, self.count // 2):
            remote(own, own, self.far, (step - 1, index), self.across(step, False)).wait_send()
            got = self.part(self.across(-step, True), index)
            remote(got, got, self.passed, (step - 1, index), self.partner).wait()


def gather_sems(count, chunks):
    far = max(count // 2 - 1, 1)
    return [
        pltpu.SemaphoreType.DMA((2, chunks)),
        pltpu.SemaphoreType.DMA((2, far, chunks)),
        pltpu.SemaphoreType.DMA((2, far, chunks)),
    ]


class RowSum:
    def __init__(self, count, rows, chunk, left, weight, flipped, buffers):
        self.count, self.rows, self.chunk = count, rows, chunk
        self.left, self.weight, self.flipped = left, weight, flipped
        (self.pair_out, self.pair_in, self.far_out, self.far_in, self.near_out, self.near_in) = buffers[:6]
        self.pair, self.far, self.near = buffers[6:]
        self.place, self.partner, self.across = mesh_place(count)

    def product(self, owner, index):
        at = pl.multiple_of(owner * self.rows + index * self.chunk, self.chunk)
        rows = self.left[pl.ds(at, self.chunk), :]
        return (back_product if self.flipped else product)(rows, self.weight[...])

    def pair_copy(self, step, index):
        return remote(
            self.pair_out.at[step - 1, index], self.pair_in.at[step - 1, index],
            self.pair, (step - 1, index), self.partner,
        )

    def far_copy(self, step, index):
        return remote(
            self.far_out.at[step - 1, index], self.far_in.at[step - 1, index],
            self.far, (step - 1, index), self.across(step, False),
        )

    def near_copy(self, index):
        return remote(self.near_out.at[index], self.near_in.at[index], self.near, (index,), self.partner)

    def send(self):
        chunks = self.rows // self.chunk

        def pair(index):
            for step in range(1, self.count // 2):
                self.pair_out[step - 1, index] = self.product(self.across(step, True), index).astype(BF16)
                self.pair_copy(step, index).start()

        def far(index):
            for step in range(1, self.count // 2):
                own = self.product(self.across(step, False), index)
                self.pair_copy(step, index).wait_recv()
                self.far_out[step - 1, index] = (own + self.pair_in[step - 1, index].astype(F32)).astype(BF16)
                self.far_copy(step, index).start()

        def near(index):
            self.near_out[index] = self.product(self.partner, index).astype(BF16)
            self.near_copy(index).start()

        each(chunks, pair)
        each(chunks, far)
        each(chunks, near)

    def total(self, index):
        rows = self.product(self.place, index)
        self.near_copy(index).wait_recv()
        rows = rows + self.near_in[index].astype(F32)
        for step in range(1, self.count // 2):
            self.far_copy(step, index).wait_recv()
            rows = rows + self.far_in[step - 1, index].astype(F32)
        return rows

    def finish(self, index):
        self.near_copy(index).wait_send()
        for step in range(1, self.count // 2):
            self.pair_copy(step, index).wait_send()
            self.far_copy(step, index).wait_send()


def split_copies(copies):
    inner = 1
    while (2 * inner) ** 2 <= copies:
        inner *= 2
    return copies // inner, inner


def dp_copy(source, target, send_sem, recv_sem, device):
    return pltpu.make_async_remote_copy(
        src_ref=source, dst_ref=target, send_sem=send_sem, recv_sem=recv_sem,
        device_id={"dp": device}, device_id_type=pl.DeviceIdType.MESH,
    )


class DpPlace:
    def __init__(self, copies):
        self.outer, self.inner = split_copies(copies)
        here = lax.axis_index("dp")
        self.z, self.y = lax.div(here, self.inner), lax.rem(here, self.inner)

    def along_y(self, step):
        return lax.rem(self.y + step + self.inner, self.inner)

    def along_z(self, step):
        return lax.rem(self.z + step + self.outer, self.outer)

    def device(self, z, y):
        return z * self.inner + y

    def greet(self, barrier):
        for step in range(1, self.inner):
            pl.semaphore_signal(
                barrier, inc=1, device_id={"dp": self.device(self.z, self.along_y(step))},
                device_id_type=pl.DeviceIdType.MESH,
            )
        for step in range(1, self.outer):
            pl.semaphore_signal(
                barrier, inc=1, device_id={"dp": self.device(self.along_z(step), self.y)},
                device_id_type=pl.DeviceIdType.MESH,
            )
        return self.inner + self.outer - 2


class DpReduce:
    def __init__(self, copies, source, y_in, z_out, z_in, y_sems, z_sems):
        self.at = DpPlace(copies)
        self.source, self.y_in, self.z_out, self.z_in = source, y_in, z_out, z_in
        self.y_sems, self.z_sems = y_sems, z_sems

    def y_copy(self, step, z):
        peer = self.at.along_y(step)
        return dp_copy(
            self.source.at[z, peer], self.y_in.at[step - 1, z],
            self.y_sems.at[0, step - 1, z], self.y_sems.at[1, step - 1, z], self.at.device(self.at.z, peer),
        )

    def z_copy(self, step):
        peer = self.at.along_z(step + 1)
        return dp_copy(
            self.z_out.at[step], self.z_in.at[step],
            self.z_sems.at[0, step], self.z_sems.at[1, step], self.at.device(peer, self.at.y),
        )

    def send(self):
        def start(step):
            for y_step in range(1, self.at.inner):
                self.y_copy(y_step, self.at.along_z(step + 1)).start()

        each(self.at.outer, start)

    def y_total(self, z):
        total = self.source[z, self.at.y].astype(F32)
        for y_step in range(1, self.at.inner):
            self.y_copy(y_step, z).wait_recv()
            total = total + self.y_in[y_step - 1, z].astype(F32)
        return total

    def pass_on(self, step):
        @pl.when(step < self.at.outer - 1)
        def _():
            self.z_out[step] = self.y_total(self.at.along_z(step + 1)).astype(BF16)
            self.z_copy(step).start()

    def total(self):
        total = self.y_total(self.at.z)
        for step in range(self.at.outer - 1):
            self.z_copy(step).wait_recv()
            total = total + self.z_in[step].astype(F32)
        for step in range(self.at.outer - 1):
            self.z_copy(step).wait_send()
        for y_step in range(1, self.at.inner):
            for z in range(self.at.outer):
                self.y_copy(y_step, z).wait_send()
        return total


def reduce_scratch(copies, array):
    outer, inner = split_copies(copies)
    slab = array.shape[2:]
    return [
        pltpu.VMEM((inner - 1, outer, *slab), BF16),
        pltpu.VMEM((outer - 1, *slab), BF16),
        pltpu.VMEM((outer - 1, *slab), BF16),
        pltpu.SemaphoreType.DMA((2, inner - 1, outer)),
        pltpu.SemaphoreType.DMA((2, outer - 1)),
    ]


class DpGather:
    def __init__(self, copies, slab, held, z_sems, y_sems):
        self.at = DpPlace(copies)
        self.slab, self.held, self.z_sems, self.y_sems = slab, held, z_sems, y_sems

    def z_copy(self, step, z):
        here = self.held.at[z, self.at.y]
        peer = self.at.device(self.at.along_z(step + 1), self.at.y)
        return dp_copy(here, here, self.z_sems.at[0, step], self.z_sems.at[1, step], peer)

    def y_copy(self, y_step, slot, z, y):
        here = self.held.at[z, y]
        peer = self.at.device(self.at.z, self.at.along_y(y_step))
        return dp_copy(
            here, here, self.y_sems.at[0, y_step - 1, slot], self.y_sems.at[1, y_step - 1, slot], peer
        )

    def send(self):
        self.held[self.at.z, self.at.y] = self.slab[...]
        for step in range(self.at.outer - 1):
            self.z_copy(step, self.at.z).start()
        for y_step in range(1, self.at.inner):
            self.y_copy(y_step, self.at.outer - 1, self.at.z, self.at.y).start()

    def pass_on(self, step):
        @pl.when(step < self.at.outer - 1)
        def _():
            source = self.at.along_z(-step - 1)
            self.z_copy(step, source).wait_recv()
            for y_step in range(1, self.at.inner):
                self.y_copy(y_step, step, source, self.at.y).start()

    def finish(self):
        for step in range(self.at.outer - 1):
            self.z_copy(step, self.at.z).wait_send()
        for y_step in range(1, self.at.inner):
            sender = self.at.along_y(-y_step)
            for slot in range(self.at.outer):
                source = self.at.along_z(-slot - 1)
                self.y_copy(y_step, slot, source, sender).wait_recv()
                self.y_copy(y_step, slot, source, self.at.y).wait_send()


def gather_scratch(copies, array):
    outer, inner = split_copies(copies)
    return [
        pltpu.VMEM(array.shape, BF16),
        pltpu.SemaphoreType.DMA((2, outer - 1)),
        pltpu.SemaphoreType.DMA((2, inner - 1, outer)),
    ]


def widen(source, target, outer):
    def one(z):
        for y in range(source.shape[1]):
            target[z, y] = source[z, y].astype(F32)

    each(outer, one)


def spread(index, chunks, copies, steps):
    outer = split_copies(copies)[0]
    turns = -(-outer // chunks)

    def turn(sub):
        for step in steps:
            step(index * turns + sub)

    each(turns, turn)


def row_sum_scratch(count, rows, chunk, width):
    far, chunks = max(count // 2 - 1, 1), rows // chunk
    wide = pltpu.VMEM((far, chunks, chunk, width), BF16)
    slim = pltpu.VMEM((chunks, chunk, width), BF16)
    return [
        wide, wide, wide, wide, slim, slim,
        pltpu.SemaphoreType.DMA((2, far, chunks)),
        pltpu.SemaphoreType.DMA((2, far, chunks)),
        pltpu.SemaphoreType.DMA((2, chunks)),
    ]


def rows_at(index, chunk):
    return pl.ds(pl.multiple_of(index * chunk, chunk), chunk)


def standardize(values):
    average = jnp.mean(values, axis=-1, keepdims=True)
    centered = values - average
    spread = lax.rsqrt(jnp.mean(centered * centered, axis=-1, keepdims=True) + EPSILON)
    return centered * spread, spread


def norm_backward(values, grad, gain):
    normed, spread = standardize(values)
    scaled = grad * gain
    inner = jnp.mean(scaled * normed, axis=-1, keepdims=True)
    back = (scaled - jnp.mean(scaled, axis=-1, keepdims=True) - normed * inner) * spread
    return back, grad * normed


def column_sum(values):
    return jnp.sum(values, axis=0, keepdims=True)


def open_kernel(count, chunk, x_ref, gain_ref, shift_ref, first_ref, rows_ref, all_ref, *sems):
    rows = x_ref.shape[0]
    place, _, _ = mesh_place(count)
    greet(count)
    chunks = rows // chunk
    main = Gather(count, rows_ref, chunk, *sems[:3])
    side_chunk = first_ref.shape[0] // 2
    side = Gather(count, all_ref, side_chunk, *sems[3:])

    def start(index):
        values = x_ref[rows_at(index, chunk), :].astype(F32)
        normed = standardize(values)[0] * gain_ref[...] + shift_ref[...]
        rows_ref[place, rows_at(index, chunk), :] = normed.astype(BF16)
        main.send(index)

    each(chunks, start)

    def side_start(index):
        all_ref[place, rows_at(index, side_chunk), :] = first_ref[rows_at(index, side_chunk), :]
        side.send(index)

    each(2, side_start)
    each(chunks, main.hand_on)
    each(2, side.hand_on)
    each(chunks, main.finish)
    each(2, side.finish)


def attend_out_kernel(
    count, chunk, left, weight, x_ref, bias_ref, gain_ref, shift_ref, rows_ref, residual_ref, *scratch
):
    rows = x_ref.shape[0]
    place, _, _ = mesh_place(count)
    greet(count)
    chunks = rows // chunk
    summed = RowSum(count, rows, chunk, left, weight, False, scratch[:9])
    main = Gather(count, rows_ref, chunk, *scratch[9:])
    summed.send()

    def close(index):
        at = rows_at(index, chunk)
        values = x_ref[at, :].astype(F32) + summed.total(index) + bias_ref[...]
        residual_ref[at, :] = values
        normed = standardize(values)[0] * gain_ref[...] + shift_ref[...]
        rows_ref[place, at, :] = normed.astype(BF16)
        main.send(index)

    each(chunks, close)
    each(chunks, main.hand_on)
    each(chunks, main.finish)
    each(chunks, summed.finish)


def mlp_back_kernel(
    count, copies, chunk, left, weight, residual_ref, dy_ref, gain_ref, up_ref, down_ref,
    rows_ref, grad_ref, sums_ref, up_slab, down_slab, *scratch
):
    rows = residual_ref.shape[0]
    place, _, _ = mesh_place(count)
    greet(count, copies)
    chunks = rows // chunk
    summed = RowSum(count, rows, chunk, left, weight, True, scratch[:9])
    main = Gather(count, rows_ref, chunk, *scratch[9:12])
    up = DpReduce(copies, up_ref, *scratch[12:17])
    down = DpReduce(copies, down_ref, *scratch[17:22])
    down.send()
    up.send()
    sums_ref[...] = jnp.zeros_like(sums_ref)
    summed.send()

    def close(index):
        at = rows_at(index, chunk)
        total = summed.total(index)
        dy = dy_ref[at, :].astype(F32)
        back, per_gain = norm_backward(residual_ref[at, :], total, gain_ref[...])
        grad = dy + back
        grad_ref[at, :] = grad
        rows_ref[place, at, :] = grad.astype(BF16)
        main.send(index)
        sums_ref[0:1, :] += column_sum(per_gain)
        sums_ref[1:2, :] += column_sum(total)
        sums_ref[2:3, :] += column_sum(grad)
        sums_ref[3:4, :] += column_sum(dy)
        spread(index, chunks, copies, [down.pass_on])

    def hand_on(index):
        main.hand_on(index)
        spread(index, chunks, copies, [up.pass_on])

    each(chunks, close)
    each(chunks, hand_on)
    down_slab[...] = down.total().astype(BF16)
    each(chunks, main.finish)
    each(chunks, summed.finish)
    up_slab[...] = up.total().astype(BF16)


def input_back_kernel(
    count, copies, chunk, left, weight, x_ref, grad_ref, gain_ref, skip_ref, up_slab, down_slab, qkv_ref, outw_ref,
    out_ref, all_ref, sums_ref, up_ref, down_ref, qkv_slab, outw_slab, *scratch
):
    rows = x_ref.shape[0]
    place, _, _ = mesh_place(count)
    greet(count, copies)
    chunks = rows // chunk
    summed = RowSum(count, rows, chunk, left, weight, True, scratch[:9])
    side_chunk = skip_ref.shape[0] // 2
    side = Gather(count, all_ref, side_chunk, *scratch[9:12])
    outw = DpReduce(copies, outw_ref, *scratch[12:17])
    qkv = DpReduce(copies, qkv_ref, *scratch[17:22])
    up = DpGather(copies, up_slab, *scratch[22:25])
    down = DpGather(copies, down_slab, *scratch[25:28])
    qkv.send()
    outw.send()
    down.send()
    up.send()
    sums_ref[...] = jnp.zeros_like(sums_ref)
    summed.send()

    def side_start(index):
        all_ref[place, rows_at(index, side_chunk), :] = skip_ref[rows_at(index, side_chunk), :]
        side.send(index)

    each(2, side_start)

    def close(index):
        at = rows_at(index, chunk)
        total = summed.total(index)
        back, per_gain = norm_backward(x_ref[at, :].astype(F32), total, gain_ref[...])
        out_ref[at, :] = (grad_ref[at, :] + back).astype(BF16)
        sums_ref[0:1, :] += column_sum(per_gain)
        sums_ref[1:2, :] += column_sum(total)
        spread(index, chunks, copies, [qkv.pass_on, outw.pass_on, down.pass_on, up.pass_on])

    each(chunks, close)
    each(2, side.hand_on)
    qkv_slab[...] = qkv.total().astype(BF16)
    outw_slab[...] = outw.total().astype(BF16)
    down.finish()
    widen(down.held, down_ref, down.at.outer)
    each(2, side.finish)
    each(chunks, summed.finish)
    up.finish()
    widen(up.held, up_ref, up.at.outer)


def mlp_out_kernel(
    count, copies, chunk, shared, left, weight, residual_ref, bias_ref, small_ref, qkv_slab, outw_slab,
    out_ref, small_out, qkv_ref, outw_ref, *scratch
):
    rows = residual_ref.shape[0]
    copy, place = lax.axis_index("dp"), lax.axis_index("mp")
    barrier = pltpu.get_barrier_semaphore()
    for step in range(1, copies):
        pl.semaphore_signal(
            barrier, inc=1, device_id={"dp": lax.rem(copy + step, copies)}, device_id_type=pl.DeviceIdType.MESH
        )
    for step in range(1, count):
        pl.semaphore_signal(
            barrier, inc=1, device_id={"mp": lax.rem(place + step, count)}, device_id_type=pl.DeviceIdType.MESH
        )
    pl.semaphore_wait(barrier, copies + count - 2)
    chunks = rows // chunk
    summed = RowSum(count, rows, chunk, left, weight, False, scratch[:9])
    qkv = DpGather(copies, qkv_slab, *scratch[9:12])
    outw = DpGather(copies, outw_slab, *scratch[12:15])
    copy_in, part_in, part_out, copy_sems, part_sems = scratch[15:]

    def small_copy(axis, own, size, source, slots, sems, step, slot):
        return pltpu.make_async_remote_copy(
            src_ref=source, dst_ref=slots.at[slot], send_sem=sems.at[0, step], recv_sem=sems.at[1, slot],
            device_id={axis: lax.rem(own + step, size)}, device_id_type=pl.DeviceIdType.MESH,
        )

    def small_start(axis, own, size, source, slots, sems):
        slots[own] = source[...]
        for step in range(1, size):
            small_copy(axis, own, size, source, slots, sems, step, own).start()

    def small_total(axis, own, size, source, slots, sems):
        for step in range(1, size):
            slot = lax.rem(own + size - step, size)
            small_copy(axis, own, size, source, slots, sems, step, slot).wait_recv()
            small_copy(axis, own, size, source, slots, sems, step, own).wait_send()
        total = slots[0]
        for slot in range(1, size):
            total = total + slots[slot]
        return total

    over_copies = ("dp", copy, copies, small_ref, copy_in, copy_sems)
    over_parts = ("mp", place, count, part_out, part_in, part_sems)
    small_start(*over_copies)
    qkv.send()
    outw.send()
    summed.send()
    part_out[...] = small_total(*over_copies)
    small_start(*over_parts)

    def close(index):
        at = rows_at(index, chunk)
        out_ref[at, :] = (residual_ref[at, :] + summed.total(index) + bias_ref[...]).astype(BF16)
        spread(index, chunks, copies, [qkv.pass_on, outw.pass_on])

    each(chunks, close)
    every = small_total(*over_parts)
    row = lax.broadcasted_iota(jnp.int32, every.shape, 0)
    small_out[...] = jnp.where(row < shared, every, part_out[...])
    qkv.finish()
    widen(qkv.held, qkv_ref, qkv.at.outer)
    outw.finish()
    widen(outw.held, outw_ref, outw.at.outer)
    each(chunks, summed.finish)


def call(kernel, name, number, inputs, outputs, scratch, flops):
    moved = sum(a.size * a.dtype.itemsize for a in (*inputs, *outputs))
    return pl.pallas_call(
        kernel,
        out_shape=outputs,
        in_specs=[pl.BlockSpec(memory_space=pltpu.VMEM)] * len(inputs),
        out_specs=[pl.BlockSpec(memory_space=pltpu.VMEM)] * len(outputs),
        scratch_shapes=scratch,
        compiler_params=pltpu.CompilerParams(collective_id=number, has_side_effects=True),
        cost_estimate=pl.CostEstimate(flops=flops, bytes_accessed=moved, transcendentals=0),
        name=name,
    )(*inputs)


def like(shape, kind):
    return jax.ShapeDtypeStruct(shape, kind)


def body(
    inputs,
    first_values,
    cotangent,
    seq_lengths,
    value_owner,
    attn_norm_gain,
    attn_norm_bias,
    qkv_weight,
    qv_bias,
    out_weight,
    out_bias,
    mlp_norm_gain,
    mlp_norm_bias,
    up_weight,
    up_bias,
    down_weight,
    down_bias,
):
    local_rows, model_width = inputs.shape
    group_rows = local_rows * lax.axis_size("mp")
    pairs_dev, head_size = qkv_weight.shape[1], qkv_weight.shape[3]
    all_pairs = value_owner.shape[0]
    seats = (seq_lengths, value_owner, lax.axis_index("mp").reshape(1).astype(jnp.int32))
    copies = lax.axis_size("dp")

    qkv_pack = jnp.pad(qkv_weight, ((0, 0), (0, 0), (0, 1), (0, 0)))
    qkv_pack = qkv_pack.reshape(model_width, pairs_dev * PACK * head_size)
    bias_pack = jnp.concatenate(
        [qv_bias[:, 0:2], jnp.zeros_like(qv_bias[:, 0:2]), qv_bias[:, 2:3], jnp.zeros_like(qv_bias[:, 2:3])],
        axis=1,
    ).reshape(1, pairs_dev * PACK * head_size)
    out_flat = out_weight.reshape(pairs_dev * 2 * head_size, model_width)

    count = lax.axis_size("mp")
    chunk = min(128, local_rows)
    chunks = local_rows // chunk
    row = (1, model_width)
    whole = (count, local_rows, model_width)
    slim = pairs_dev * head_size
    sum_scratch = row_sum_scratch(count, local_rows, chunk, model_width)
    main_sems, side_sems = gather_sems(count, chunks), gather_sems(count, 2)
    dense = 2 * group_rows * model_width

    rows_one, all_first = call(
        functools.partial(open_kernel, count, chunk), "open_rows", 0,
        (inputs, attn_norm_gain.reshape(row), attn_norm_bias.reshape(row), first_values.reshape(group_rows, slim)),
        [like(whole, BF16), like((count, group_rows, slim), BF16)],
        main_sems + side_sems, dense * 100,
    )
    rows_one = rows_one.reshape(group_rows, model_width)
    packed = (product(rows_one, qkv_pack) + bias_pack).astype(BF16)
    cotangent_late = lax.optimization_barrier((cotangent, rows_one))[0]
    with jax.named_scope("gradrows"):
        grad_rows = lax.all_gather(cotangent_late, "mp", axis=0, tiled=True)
    mixed, totals = attend_forward(*seats, packed, all_first)
    rows_two, residual = call(
        functools.partial(attend_out_kernel, count, chunk), "attend_out", 1,
        (mixed, out_flat, inputs, out_bias.reshape(row), mlp_norm_gain.reshape(row), mlp_norm_bias.reshape(row)),
        [like(whole, BF16), like(inputs.shape, F32)],
        sum_scratch + main_sems, dense * 256,
    )
    rows_two = rows_two.reshape(group_rows, model_width)
    hidden_pre = product(rows_two, up_weight) + up_bias
    hidden = gelu_tanh(hidden_pre).astype(BF16)
    grad_hidden = back_product(grad_rows, down_weight)
    grad_pre = jax.vjp(gelu_tanh, hidden_pre)[1](grad_hidden)[0].astype(BF16)
    grad_down_weight = rows_product(hidden, grad_rows).astype(BF16)
    grad_up_weight = rows_product(rows_two, grad_pre).astype(BF16)
    grad_up_bias = jnp.sum(grad_pre.astype(F32), axis=0)
    outer, inner = split_copies(copies)

    def sliced(values):
        return values.reshape(outer, inner, values.shape[0] // copies, values.shape[1])

    grad_up_weight, grad_down_weight = sliced(grad_up_weight), sliced(grad_down_weight)
    up_slab, down_slab = (like(part.shape[2:], BF16) for part in (grad_up_weight, grad_down_weight))
    resid_rows, grad_residual, sums_two, up_slab, down_slab = call(
        functools.partial(mlp_back_kernel, count, copies, chunk), "mlp_back", 2,
        (grad_pre, up_weight, residual, cotangent, mlp_norm_gain.reshape(row), grad_up_weight, grad_down_weight),
        [like(whole, BF16), like(inputs.shape, F32), like((8, model_width), F32), up_slab, down_slab],
        sum_scratch + main_sems + reduce_scratch(copies, grad_up_weight) + reduce_scratch(copies, grad_down_weight),
        dense * up_bias.shape[0],
    )
    resid_rows = resid_rows.reshape(group_rows, model_width)
    grad_mixed = back_product(resid_rows, out_flat).astype(BF16)
    grad_out_weight = rows_product(mixed, resid_rows).astype(BF16)
    grad_flat = attend_backward(*seats, packed, all_first, grad_mixed, totals)
    grad_pack = grad_flat.reshape(group_rows, pairs_dev, PACK, head_size)
    pack_sums = jnp.sum(grad_flat.astype(F32), axis=0).reshape(pairs_dev, PACK, head_size)
    grad_qv_bias = jnp.concatenate([pack_sums[:, 0:2], pack_sums[:, 4:5]], axis=1)
    grad_qkv_weight = sliced(rows_product(rows_one, grad_flat).astype(BF16))
    grad_out_weight = sliced(grad_out_weight)
    grad_inputs, every_skip, sums_one, up_sum, down_sum, qkv_slab, out_slab = call(
        functools.partial(input_back_kernel, count, copies, chunk), "input_back", 3,
        (grad_flat, qkv_pack, inputs, grad_residual, attn_norm_gain.reshape(row),
         grad_pack[:, :, 5].reshape(group_rows, slim), up_slab, down_slab, grad_qkv_weight, grad_out_weight),
        [like(inputs.shape, BF16), like((count, group_rows, slim), BF16), like((8, model_width), F32),
         like(grad_up_weight.shape, F32), like(grad_down_weight.shape, F32),
         like(grad_qkv_weight.shape[2:], BF16), like(grad_out_weight.shape[2:], BF16)],
        sum_scratch + side_sems + reduce_scratch(copies, grad_out_weight) + reduce_scratch(copies, grad_qkv_weight)
        + gather_scratch(copies, grad_up_weight) + gather_scratch(copies, grad_down_weight),
        dense * pairs_dev * PACK * head_size,
    )
    wide_bias = jnp.pad(grad_up_bias, (0, model_width - grad_up_bias.shape[0])).reshape(row)
    slim_bias = jnp.pad(grad_qv_bias.reshape(-1), (0, model_width - grad_qv_bias.size)).reshape(row)
    own_sums = jnp.concatenate([sums_two[0:4], sums_one[0:2], wide_bias, slim_bias], axis=0)
    block = pltpu.VMEM(own_sums.shape, F32)
    output, small, qkv_sum, out_sum = call(
        functools.partial(mlp_out_kernel, count, copies, chunk, 6), "mlp_out", 4,
        (hidden, down_weight, residual, down_bias.reshape(row), own_sums, qkv_slab, out_slab),
        [like(inputs.shape, BF16), like(own_sums.shape, F32),
         like(grad_qkv_weight.shape, F32), like(grad_out_weight.shape, F32)],
        sum_scratch + gather_scratch(copies, grad_qkv_weight) + gather_scratch(copies, grad_out_weight)
        + [pltpu.VMEM((copies, *own_sums.shape), F32), pltpu.VMEM((count, *own_sums.shape), F32), block,
           pltpu.SemaphoreType.DMA((2, copies)), pltpu.SemaphoreType.DMA((2, count))],
        dense * up_bias.shape[0],
    )
    qkv_sum = qkv_sum.reshape(model_width, pairs_dev, PACK, head_size)[:, :, 0:5]
    late_sums = (up_sum.reshape(up_weight.shape), down_sum.reshape(down_weight.shape), out_sum.reshape(out_weight.shape))
    owned = lax.axis_index("mp") * pairs_dev + jnp.arange(pairs_dev, dtype=jnp.int32)
    every_pair = jnp.arange(all_pairs, dtype=jnp.int32)
    inverse = jnp.sum(
        jnp.where(value_owner[None, :] == owned[:, None], every_pair[None, :], 0), axis=1
    )
    every_skip = every_skip.reshape(count, group_rows, pairs_dev, head_size)
    grad_first = jnp.stack(
        [every_skip[inverse[p] // pairs_dev, :, inverse[p] % pairs_dev] for p in range(pairs_dev)], axis=1
    )
    norm_sums = (small[4], small[5], small[2], small[0], small[1], small[3])
    bias_sums = (small[7, : grad_qv_bias.size].reshape(qv_bias.shape), small[6, : grad_up_bias.shape[0]])

    return (
        output,
        grad_inputs,
        grad_first,
        norm_sums[0],
        norm_sums[1],
        qkv_sum,
        bias_sums[0],
        late_sums[2],
        norm_sums[2],
        norm_sums[3],
        norm_sums[4],
        late_sums[0],
        bias_sums[1],
        late_sums[1],
        norm_sums[5],
    )


def solution(mesh):
    return jax.shard_map(
        body,
        mesh=mesh,
        in_specs=(
            P(("dp", "mp"), None),
            P("dp", "mp", None),
            P(("dp", "mp"), None),
            P("dp"),
            P(),
            P(),
            P(),
            P(None, "mp", None, None),
            P("mp", None, None),
            P("mp", None, None, None),
            P(),
            P(),
            P(),
            P(None, "mp"),
            P("mp"),
            P("mp", None),
            P(),
        ),
        out_specs=(
            P(("dp", "mp"), None),
            P(("dp", "mp"), None),
            P("dp", "mp", None),
            P(),
            P(),
            P(None, "mp", None, None),
            P("mp", None, None),
            P("mp", None, None, None),
            P(),
            P(),
            P(),
            P(None, "mp"),
            P("mp"),
            P("mp", None),
            P(),
        ),
        check_vma=False,
    )
```

time: 1250 us -> 480 us (0.38)
  waiting for transfers between devices: 594 us -> 0.02 us
  Pallas kernels: 0 us -> 349 us
  matrix products: 280 us -> 61.1 us
  other arithmetic: 162 us -> 2.92 us
  blocking collectives: 62.6 us -> 0 us
  local copies, waits for them, and re-layouts: 99.3 us -> 40.7 us
  loops' own time: 16.7 us -> 0 us
    pallas_call x0 -> x7, Pallas kernels: none -> 349 us  [the longest x5 301 us: call(): pl.pallas_call(kernel, out_shape=outputs, in_specs=[pl.BlockSpec(memory_s...]
    reduce_scatter x5 -> x0, waiting for transfers between devices: 213 us -> none  [the longest x2 88.9 us: run_forward(): lax.psum_scatter(jnp.dot(picked, out_flat, preferred_element_type=jnp.flo...]
    all_gather x8 -> x1, waiting for transfers between devices: 210 us -> 0.01 us  [body(): grad_rows = lax.all_gather(cotangent_late, 'mp', axis=0, tiled=True)]
    dot_general x42 -> x2, matrix products: 219 us -> 16.5 us  [product(): return jnp.dot(left, right, preferred_element_type=F32)]
    psum x1 -> x0, waiting for transfers between devices: 170 us -> none  [body(): lax.psum(grad_qkv_weight.astype(jnp.bfloat16), 'dp').astype(jnp.float32)]
    sub x5 -> x0, other arithmetic: 64.7 us -> none  [the longest x4 64.7 us: one_block(): weights = jnp.exp(scores - top_score)]
    psum x2 -> x0, blocking collectives: 62.6 us -> none  [the longest x1 39.9 us: body(): lax.psum((grad_attn_norm_gain, grad_attn_norm_bias, grad_out_bias, grad_m...]
    convert_element_type x20 -> x0, other arithmetic: 47.7 us -> none  [the longest x4 22.6 us: one_block(): grad_scores = (probs * (grad_probs - inner)).astype(jnp.bfloat16)]
  transfers between devices with their start and end apart: 14 -> 1, of which waited for: 13 -> 0; matrix products, arithmetic and copies ran while one was open for 6% -> 5% of each run, Pallas kernels for 0% -> 16%
where the time goes in v1:
time: 480 us; the launch traced here: 474 us
  Pallas kernels  349 us (73%)
  matrix products  61.1 us (13%)
  local copies, waits for them, and re-layouts  40.7 us (8%)
  between operations  19.9 us (4%)
    pallas_call x5, Pallas kernels, call(): pl.pallas_call(kernel, out_shape=outputs, in_specs=[pl.BlockSpec(memory_s...  301 us
    pallas_call x1, Pallas kernels, attend_backward(): pl.pallas_call(functools.partial(attend_backward_kernel, pairs), grid_spe...  29.7 us
    dot_general x4, matrix products, rows_product(): lax.dot_general(left, right, (((0,), (0,)), ((), ())), preferred_element_...  24.3 us
    dot_general x2, matrix products, back_product(): lax.dot_general(left, weight, (((1,), (1,)), ((), ())), preferred_element...  20.3 us
    pallas_call x1, Pallas kernels, attend_forward(): pl.pallas_call(functools.partial(attend_forward_kernel, pairs), grid_spec...  18.7 us
    dot_general x2, matrix products, product(): return jnp.dot(left, right, preferred_element_type=F32)  16.5 us
    unnamed x34, local copies, waits for them, and re-layouts  11.1 us
  transfers between devices with their start and end apart: 1, of which 0 were waited for; matrix products, arithmetic and copies ran while one was open for 5% of the time, Pallas kernels for 16%

profile of v1, /device:TPU:0, one launch (start us, length us, event | category | flops | bytes accessed | tf_op | source)
XLA Modules:
  0.0 473.8 jit_solution(230345766422065650)
XLA Ops:
  7.2 2.1 copy.47.first_ref
  9.4 43.8 %open_rows.1 = (bf16[4,512,1024]{2,1,0:T(8,128)(2,1)}, bf16[4,2048,128]{2,1,0:T(8,128)(2,1)}) custom-call(bf16[512,1024]{1,0:T(8,128)(2,1)} %x_ref.5, f32[1,1024]{1,0:T(1,128)} %bitcast.68, f32[1,1024]{1,0:T(1,128)} %bitcast.67, bf16[2048,128]{1,0:T(8,128)(2,1)} %copy.47.first_ref), custom_call_target="tpu_custom_call" | custom-call | flops 419430400 | bytes 7872512 | tf_op jit(solution)/shard_map/open_rows/pallas_call | solution.py:834
  63.4 7.5 %add_convert_fusion.qkv_ref = bf16[2048,768]{1,0:T(8,128)(2,1)} fusion(bf16[2048,1024]{1,0:T(8,128)(2,1)} %bitcast.78, bf16[1024,768]{0,1:T(8,128)(2,1)S(1)} %bitcast.58, f32[768]{0:T(1024)S(1)} %add.62), kind=kOutput, calls=%fused_computation.13 | convolution fusion | flops 3224371200 | bytes 8915968 | tf_op jit(solution)/shard_map/dot_general | solution.py:42
  70.9 18.7 %attend_forward.1 = (bf16[2048,256]{1,0:T(8,128)(2,1)}, f32[2048,256]{1,0:T(8,128)}) custom-call(s32[4]{0:T(128)} %lengths.3, s32[8]{0:T(128)} %owner.3, s32[1]{0:T(128)} %bitcast.place, bf16[2048,768]{1,0:T(8,128)(2,1)} %add_convert_fusion.qkv_ref, bf16[4,2048,128]{2,1,0:T(8,128)(2,1)} %get-tuple-element.39.first_ref), custom_call_target="tpu_custom_call" | custom-call | flops 4294967296 | bytes 8388608 | tf_op jit(solution)/shard_map/attend_forward/pallas_call | solution.py:201
  89.6 55.9 %attend_out.1 = (bf16[4,512,1024]{2,1,0:T(8,128)(2,1)}, f32[512,1024]{1,0:T(8,128)}) custom-call(bf16[2048,256]{1,0:T(8,128)(2,1)} %get-tuple-element.40.left, bf16[256,1024]{1,0:T(8,128)(2,1)} %bitcast.80, bf16[512,1024]{1,0:T(8,128)(2,1)} %x_ref.5, f32[1,1024]{1,0:T(1,128)} %bitcast.82, f32[1,1024]{1,0:T(1,128)} %bitcast.84, f32[1,1024]{1,0:T(1,128)} %bitcast.83), custom_call_target="tpu_custom_call" | custom-call | flops 1073741824 | bytes 8925184 | tf_op jit(solution)/shard_map/attend_out/pallas_call | solution.py:834
  145.5 9.0 %fusion.10 = f32[2048,1024]{1,0:T(8,128)} fusion(bf16[2048,1024]{1,0:T(8,128)(2,1)} %bitcast.89, bf16[1024,1024]{1,0:T(8,128)(2,1)S(1)} %copy-done.8), kind=kOutput, calls=%fused_computation.31 | convolution fusion | flops 4294967296 | bytes 14680064 | tf_op jit(solution)/shard_map/dot_general | solution.py:42
  154.5 15.8 %convert_reduce_fusion = (f32[1024]{0:T(1024)S(1)}, bf16[2048,1024]{1,0:T(8,128)(2,1)S(1)}, bf16[2048,1024]{1,0:T(8,128)(2,1)S(1)}) fusion(f32[2048,1024]{1,0:T(8,128)} %fusion.10, f32[1024]{0:T(1024)S(1)} %copy-done.10, bf16[2048,1024]{1,0:T(8,128)(2,1)} %all-gather.2.cloned.1.call-done, bf16[1024,1024]{1,0:T(8,128)(2,1)} %weight.3), kind=kOutput, calls=%fused_computation.10 | convolution fusion | flops 4355783680 | bytes 23076864 | tf_op jit(solution)/shard_map/dot_general | solution.py:38
  170.4 5.9 %convolution_convert_fusion.2 = bf16[1024,1024]{1,0:T(8,128)(2,1)} fusion(bf16[2048,1024]{1,0:T(8,128)(2,1)S(1)} %bitcast.90, bf16[2048,1024]{1,0:T(8,128)(2,1)S(1)} %get-tuple-element.107.left), kind=kOutput, calls=%fused_computation.16 | convolution fusion | flops 4296015872 | bytes 10485760 | tf_op jit(solution)/shard_map/dot_general | solution.py:34
  176.3 5.9 %convolution_convert_fusion.1 = bf16[1024,1024]{1,0:T(8,128)(2,1)} fusion(bf16[2048,1024]{1,0:T(8,128)(2,1)S(1)} %get-tuple-element.108.left, bf16[2048,1024]{1,0:T(8,128)(2,1)S(1)} %copy-done.7), kind=kOutput, calls=%fused_computation.15 | convolution fusion | flops 4296015872 | bytes 10485760 | tf_op jit(solution)/shard_map/dot_general | solution.py:34
  182.2 69.0 %mlp_back.1 = (bf16[4,512,1024]{2,1,0:T(8,128)(2,1)}, f32[512,1024]{1,0:T(8,128)}, f32[8,1024]{1,0:T(8,128)}, bf16[128,1024]{1,0:T(8,128)(2,1)}, bf16[128,1024]{1,0:T(8,128)(2,1)}) custom-call(bf16[2048,1024]{1,0:T(8,128)(2,1)} %copy-done.12, bf16[1024,1024]{1,0:T(8,128)(2,1)} %weight.2, f32[512,1024]{1,0:T(8,128)} %get-tuple-element.42.residual_ref, ...), custom_call_target="tpu_custom_call" | custom-call | flops 4294967296 | bytes 20484096 | tf_op jit(solution)/shard_map/mlp_back/pallas_call | solution.py:834
  251.2 4.5 convolution_convert_fusion.grad_ref
  255.7 29.7 %attend_backward.1.left = bf16[2048,768]{1,0:T(8,128)(2,1)} custom-call(s32[4]{0:T(128)} %lengths.3, s32[8]{0:T(128)} %owner.3, s32[1]{0:T(128)} %bitcast.place, bf16[2048,768]{1,0:T(8,128)(2,1)} %add_convert_fusion.qkv_ref, bf16[4,2048,128]{2,1,0:T(8,128)(2,1)} %get-tuple-element.39.first_ref, bf16[2048,256]{1,0:T(8,128)(2,1)} %convolution_convert_fusion.grad_ref, ...), custom_call_target="tpu_custom_call" | custom-call | flops 10737418240 | bytes 8388608 | tf_op jit(solution)/shard_map/attend_backward/pallas_call | solution.py:229
  285.4 8.0 %convolution_convert_fusion.3 = bf16[1024,768]{1,0:T(8,128)(2,1)} fusion(bf16[2048,1024]{1,0:T(8,128)(2,1)} %bitcast.79, bf16[2048,768]{1,0:T(8,128)(2,1)} %attend_backward.1.left), kind=kOutput, calls=%fused_computation.17 | convolution fusion | flops 3222011904 | bytes 8912896 | tf_op jit(solution)/shard_map/dot_general | solution.py:34
  293.3 3.2 copy.49
  296.5 4.6 convolution_convert_fusion.4
  303.8 82.8 %input_back.1 = (bf16[512,1024]{1,0:T(8,128)(2,1)}, bf16[4,2048,128]{2,1,0:T(8,128)(2,1)}, f32[8,1024]{1,0:T(8,128)}, f32[4,2,128,1024]{3,2,1,0:T(8,128)}, f32[4...) custom-call(bf16[2048,768]{1,0:T(8,128)(2,1)} %attend_backward.1.left, ...), custom_call_target="tpu_custom_call" | custom-call | flops 3221225472 | bytes 22843392 | tf_op jit(solution)/shard_map/input_back/pallas_call | solution.py:834
  388.1 49.2 %mlp_out.1 = (bf16[512,1024]{1,0:T(8,128)(2,1)}, f32[8,1024]{1,0:T(8,128)}, f32[4,2,128,768]{3,2,1,0:T(8,128)}, f32[4,2,32,1024]{3,2,1,0:T(8,128)}) custom-call(bf16[2048,1024]{1,0:T(8,128)(2,1)} %copy-done.13, bf16[1024,1024]{1,0:T(8,128)(2,1)} %weight.3, f32[512,1024]{1,0:T(8,128)} %get-tuple-element.42.residual_ref, f32[1,1024]{1,0:T(1,128)} %bitcast.86, ...), custom_call_target="tpu_custom_call" | custom-call | flops 4294967296 | bytes 13963264 | tf_op jit(solution)/shard_map/mlp_out/pallas_call | solution.py:834
  439.7 4.6 copy.53
  444.3 3.6 reshape.144
  447.9 3.6 slice.77
  451.5 3.0 copy.52
  456.0 2.8 copy.60
  460.8 2.1 copy.63
  464.5 2.0 copy.64
  (64 shorter events, 16.6 us)
Async XLA Ops:
  7.2 54.4 %copy-start.3 = (bf16[1024,2,5,64]{0,3,2,1:T(8,128)(2,1)S(1)}, bf16[1024,2,5,64]{0,3,2,1:T(8,128)(2,1)}, u32[]{:S(2)}) copy-start(bf16[1024,2,5,64]{0,3,2,1:T(8,128)(2,1)} %param.24) | copy-start | bytes 3932164
  7.2 147.3 %all-gather.2.cloned.1.call-start = ((), (), s32[]{:S(2)}) async-start(), calls=%async_computation | async-start | bytes 5242880 | tf_op jit(solution)/shard_map/gradrows/all_gather | solution.py:904
  70.9 74.6 %copy-start.8 = (bf16[1024,1024]{1,0:T(8,128)(2,1)S(1)}, bf16[1024,1024]{1,0:T(8,128)(2,1)}, u32[]{:S(2)}) copy-start(bf16[1024,1024]{1,0:T(8,128)(2,1)} %weight.2) | copy-start | bytes 6291460
  145.5 9.0 %copy-start.10 = (f32[1024]{0:T(1024)S(1)}, f32[1024]{0:T(1024)}, u32[]{:S(2)}) copy-start(f32[1024]{0:T(1024)} %param.31) | copy-start | bytes 12292
  154.5 15.8 %copy-start.11 = (bf16[4,512,1024]{2,1,0:T(8,128)(2,1)S(1)}, bf16[4,512,1024]{2,1,0:T(8,128)(2,1)}, u32[]{:S(2)}) copy-start(bf16[4,512,1024]{2,1,0:T(8,128)(2,1)} %get-tuple-element.41) | copy-start | bytes 12582916
  170.3 5.9 %copy-start.12 = (bf16[2048,1024]{1,0:T(8,128)(2,1)}, bf16[2048,1024]{1,0:T(8,128)(2,1)S(1)}, u32[]{:S(2)}) copy-start(bf16[2048,1024]{1,0:T(8,128)(2,1)S(1)} %get-tuple-element.107.left) | copy-start | bytes 12582916
  170.4 5.9 %copy-start.13 = (bf16[2048,1024]{1,0:T(8,128)(2,1)}, bf16[2048,1024]{1,0:T(8,128)(2,1)S(1)}, u32[]{:S(2)}) copy-start(bf16[2048,1024]{1,0:T(8,128)(2,1)S(1)} %get-tuple-element.108.left) | copy-start | bytes 12582916
  170.4 5.9 %copy-start.7 = (bf16[2048,1024]{1,0:T(8,128)(2,1)S(1)}, bf16[2048,1024]{1,0:T(8,128)(2,1)}, u32[]{:S(2)}) copy-start(bf16[2048,1024]{1,0:T(8,128)(2,1)} %all-gather.2.cloned.1.call-done) | copy-start | bytes 12582916
  182.2 69.1 %copy-start.9 = (bf16[2,2,64,1024]{3,2,1,0:T(8,128)(2,1)S(1)}, bf16[2,2,64,1024]{3,2,1,0:T(8,128)(2,1)}, u32[]{:S(2)}) copy-start(bf16[2,2,64,1024]{3,2,1,0:T(8,128)(2,1)} %param.26) | copy-start | bytes 1572868
  285.4 8.0 %copy-start = (bf16[2048,768]{1,0:T(8,128)(2,1)S(1)}, bf16[2048,768]{1,0:T(8,128)(2,1)}, u32[]{:S(2)}) copy-start(bf16[2048,768]{1,0:T(8,128)(2,1)} %attend_backward.1.left) | copy-start | bytes 9437188
  303.8 83.6 %copy-start.6 = (f32[8,1024]{1,0:T(8,128)S(1)}, f32[8,1024]{1,0:T(8,128)}, u32[]{:S(2)}) copy-start(f32[8,1024]{1,0:T(8,128)} %get-tuple-element.44) | copy-start | bytes 98308
  451.5 7.4 %copy-start.4 = (bf16[512,1024]{1,0:T(8,128)(2,1)S(1)}, bf16[512,1024]{1,0:T(8,128)(2,1)}, u32[]{:S(2)}) copy-start(bf16[512,1024]{1,0:T(8,128)(2,1)} %get-tuple-element.136) | copy-start | bytes 3145732
  454.6 5.3 %copy-start.5 = (f32[4,2,32,1024]{3,2,1,0:T(8,128)S(1)}, f32[4,2,32,1024]{3,2,1,0:T(8,128)}, u32[]{:S(2)}) copy-start(f32[4,2,32,1024]{3,2,1,0:T(8,128)} %get-tuple-element.58) | copy-start | bytes 3145732
  455.2 5.6 %copy-start.2 = (f32[4,2,128,1024]{3,2,1,0:T(8,128)S(1)}, f32[4,2,128,1024]{3,2,1,0:T(8,128)}, u32[]{:S(2)}) copy-start(f32[4,2,128,1024]{3,2,1,0:T(8,128)} %get-tuple-element.59) | copy-start | bytes 12582916
  460.8 3.7 copy-start.1
Sparse Core Ops, SparseCore 0:
  53.3 35.2 all-gather.1

commit v2 on v1

--- a/solution.py
+++ b/solution.py
@@ -7,6 +7,7 @@
 from jax.experimental.pallas import tpu as pltpu
 from jax.sharding import PartitionSpec as P
 
+
 SHORT = 512
 QROWS = 256
 LANES = 128
@@ -17,13 +18,6 @@
 GELU_C = 0.7978845608028654
 BF16 = jnp.bfloat16
 F32 = jnp.float32
-
-
-def layer_norm(values, scale_gain, scale_bias):
-    average = jnp.mean(values, axis=-1, keepdims=True)
-    centered = values - average
-    variance = jnp.mean(centered * centered, axis=-1, keepdims=True)
-    return centered * lax.rsqrt(variance + EPSILON) * scale_gain + scale_bias
 
 
 def gelu_tanh(values):
@@ -276,7 +270,7 @@
 
 
 def greet(count, copies=0):
-    place, partner, across = mesh_place(count)
+    _, partner, across = mesh_place(count)
     barrier = pltpu.get_barrier_semaphore()
     for device in [partner] + [across(step, False) for step in range(1, count // 2)]:
         pl.semaphore_signal(
@@ -338,8 +332,8 @@
     def __init__(self, count, rows, chunk, left, weight, flipped, buffers):
         self.count, self.rows, self.chunk = count, rows, chunk
         self.left, self.weight, self.flipped = left, weight, flipped
-        (self.pair_out, self.pair_in, self.far_out, self.far_in, self.near_out, self.near_in) = buffers[:6]
-        self.pair, self.far, self.near = buffers[6:]
+        (self.pair_out, self.pair_in, self.far_out, self.far_in, self.near_out, self.near_in, self.own) = buffers[:7]
+        self.pair, self.far, self.near = buffers[7:]
         self.place, self.partner, self.across = mesh_place(count)
 
     def product(self, owner, index):
@@ -363,32 +357,43 @@
         return remote(self.near_out.at[index], self.near_in.at[index], self.near, (index,), self.partner)
 
     def send(self):
-        chunks = self.rows // self.chunk
-
-        def pair(index):
-            for step in range(1, self.count // 2):
-                self.pair_out[step - 1, index] = self.product(self.across(step, True), index).astype(BF16)
+        chunks, far = self.rows // self.chunk, self.count // 2 - 1
+        core = lax.rem(self.place, 2)
+
+        def turn(number):
+            kind, index = lax.div(number, chunks), lax.rem(number, chunks)
+            step = lax.rem(kind, max(far, 1)) + 1
+            owner = lax.rem(lax.div(self.place, 2) + step, self.count // 2) * 2
+            owner = owner + jnp.where(kind < far, 1 - core, core)
+            owner = jnp.where(kind == 2 * far, self.partner, owner)
+            owner = jnp.where(kind > 2 * far, self.place, owner)
+            rows = self.product(owner, index)
+
+            @pl.when(kind < far)
+            def _():
+                self.pair_out[step - 1, index] = rows.astype(BF16)
                 self.pair_copy(step, index).start()
 
-        def far(index):
-            for step in range(1, self.count // 2):
-                own = self.product(self.across(step, False), index)
+            @pl.when((kind >= far) & (kind < 2 * far))
+            def _():
                 self.pair_copy(step, index).wait_recv()
-                self.far_out[step - 1, index] = (own + self.pair_in[step - 1, index].astype(F32)).astype(BF16)
+                self.far_out[step - 1, index] = (rows + self.pair_in[step - 1, index].astype(F32)).astype(BF16)
                 self.far_copy(step, index).start()
 
-        def near(index):
-            self.near_out[index] = self.product(self.partner, index).astype(BF16)
-            self.near_copy(index).start()
-
-        each(chunks, pair)
-        each(chunks, far)
-        each(chunks, near)
+            @pl.when(kind == 2 * far)
+            def _():
+                self.near_out[index] = rows.astype(BF16)
+                self.near_copy(index).start()
+
+            @pl.when(kind > 2 * far)
+            def _():
+                self.own[index] = rows
+
+        each((2 * far + 2) * chunks, turn)
 
     def total(self, index):
-        rows = self.product(self.place, index)
         self.near_copy(index).wait_recv()
-        rows = rows + self.near_in[index].astype(F32)
+        rows = self.own[index] + self.near_in[index].astype(F32)
         for step in range(1, self.count // 2):
             self.far_copy(step, index).wait_recv()
             rows = rows + self.far_in[step - 1, index].astype(F32)
@@ -552,21 +557,9 @@
                 self.y_copy(y_step, slot, source, self.at.y).wait_send()
 
 
-def gather_scratch(copies, array):
+def gather_scratch(copies):
     outer, inner = split_copies(copies)
-    return [
-        pltpu.VMEM(array.shape, BF16),
-        pltpu.SemaphoreType.DMA((2, outer - 1)),
-        pltpu.SemaphoreType.DMA((2, inner - 1, outer)),
-    ]
-
-
-def widen(source, target, outer):
-    def one(z):
-        for y in range(source.shape[1]):
-            target[z, y] = source[z, y].astype(F32)
-
-    each(outer, one)
+    return [pltpu.SemaphoreType.DMA((2, outer - 1)), pltpu.SemaphoreType.DMA((2, inner - 1, outer))]
 
 
 def spread(index, chunks, copies, steps):
@@ -585,7 +578,7 @@
     wide = pltpu.VMEM((far, chunks, chunk, width), BF16)
     slim = pltpu.VMEM((chunks, chunk, width), BF16)
     return [
-        wide, wide, wide, wide, slim, slim,
+        wide, wide, wide, wide, slim, slim, pltpu.VMEM((chunks, chunk, width), F32),
         pltpu.SemaphoreType.DMA((2, far, chunks)),
         pltpu.SemaphoreType.DMA((2, far, chunks)),
         pltpu.SemaphoreType.DMA((2, chunks)),
@@ -650,8 +643,8 @@
     place, _, _ = mesh_place(count)
     greet(count)
     chunks = rows // chunk
-    summed = RowSum(count, rows, chunk, left, weight, False, scratch[:9])
-    main = Gather(count, rows_ref, chunk, *scratch[9:])
+    summed = RowSum(count, rows, chunk, left, weight, False, scratch[:10])
+    main = Gather(count, rows_ref, chunk, *scratch[10:])
     summed.send()
 
     def close(index):
@@ -669,19 +662,14 @@
 
 
 def mlp_back_kernel(
-    count, copies, chunk, left, weight, residual_ref, dy_ref, gain_ref, up_ref, down_ref,
-    rows_ref, grad_ref, sums_ref, up_slab, down_slab, *scratch
+    count, chunk, left, weight, residual_ref, dy_ref, gain_ref, rows_ref, grad_ref, sums_ref, *scratch
 ):
     rows = residual_ref.shape[0]
     place, _, _ = mesh_place(count)
-    greet(count, copies)
+    greet(count)
     chunks = rows // chunk
-    summed = RowSum(count, rows, chunk, left, weight, True, scratch[:9])
-    main = Gather(count, rows_ref, chunk, *scratch[9:12])
-    up = DpReduce(copies, up_ref, *scratch[12:17])
-    down = DpReduce(copies, down_ref, *scratch[17:22])
-    down.send()
-    up.send()
+    summed = RowSum(count, rows, chunk, left, weight, True, scratch[:10])
+    main = Gather(count, rows_ref, chunk, *scratch[10:])
     sums_ref[...] = jnp.zeros_like(sums_ref)
     summed.send()
 
@@ -698,39 +686,28 @@
         sums_ref[1:2, :] += column_sum(total)
         sums_ref[2:3, :] += column_sum(grad)
         sums_ref[3:4, :] += column_sum(dy)
-        spread(index, chunks, copies, [down.pass_on])
-
-    def hand_on(index):
-        main.hand_on(index)
-        spread(index, chunks, copies, [up.pass_on])
 
     each(chunks, close)
-    each(chunks, hand_on)
-    down_slab[...] = down.total().astype(BF16)
+    each(chunks, main.hand_on)
     each(chunks, main.finish)
     each(chunks, summed.finish)
-    up_slab[...] = up.total().astype(BF16)
 
 
 def input_back_kernel(
-    count, copies, chunk, left, weight, x_ref, grad_ref, gain_ref, skip_ref, up_slab, down_slab, qkv_ref, outw_ref,
-    out_ref, all_ref, sums_ref, up_ref, down_ref, qkv_slab, outw_slab, *scratch
+    count, copies, chunk, left, weight, x_ref, grad_ref, gain_ref, skip_ref, qkv_ref, outw_ref,
+    out_ref, all_ref, sums_ref, qkv_slab, outw_slab, *scratch
 ):
     rows = x_ref.shape[0]
     place, _, _ = mesh_place(count)
     greet(count, copies)
     chunks = rows // chunk
-    summed = RowSum(count, rows, chunk, left, weight, True, scratch[:9])
+    summed = RowSum(count, rows, chunk, left, weight, True, scratch[:10])
     side_chunk = skip_ref.shape[0] // 2
-    side = Gather(count, all_ref, side_chunk, *scratch[9:12])
-    outw = DpReduce(copies, outw_ref, *scratch[12:17])
-    qkv = DpReduce(copies, qkv_ref, *scratch[17:22])
-    up = DpGather(copies, up_slab, *scratch[22:25])
-    down = DpGather(copies, down_slab, *scratch[25:28])
+    side = Gather(count, all_ref, side_chunk, *scratch[10:13])
+    outw = DpReduce(copies, outw_ref, *scratch[13:18])
+    qkv = DpReduce(copies, qkv_ref, *scratch[18:23])
     qkv.send()
     outw.send()
-    down.send()
-    up.send()
     sums_ref[...] = jnp.zeros_like(sums_ref)
     summed.send()
 
@@ -747,18 +724,14 @@
         out_ref[at, :] = (grad_ref[at, :] + back).astype(BF16)
         sums_ref[0:1, :] += column_sum(per_gain)
         sums_ref[1:2, :] += column_sum(total)
-        spread(index, chunks, copies, [qkv.pass_on, outw.pass_on, down.pass_on, up.pass_on])
+        spread(index, chunks, copies, [qkv.pass_on, outw.pass_on])
 
     each(chunks, close)
     each(2, side.hand_on)
     qkv_slab[...] = qkv.total().astype(BF16)
     outw_slab[...] = outw.total().astype(BF16)
-    down.finish()
-    widen(down.held, down_ref, down.at.outer)
     each(2, side.finish)
     each(chunks, summed.finish)
-    up.finish()
-    widen(up.held, up_ref, up.at.outer)
 
 
 def mlp_out_kernel(
@@ -778,10 +751,10 @@
         )
     pl.semaphore_wait(barrier, copies + count - 2)
     chunks = rows // chunk
-    summed = RowSum(count, rows, chunk, left, weight, False, scratch[:9])
-    qkv = DpGather(copies, qkv_slab, *scratch[9:12])
-    outw = DpGather(copies, outw_slab, *scratch[12:15])
-    copy_in, part_in, part_out, copy_sems, part_sems = scratch[15:]
+    summed = RowSum(count, rows, chunk, left, weight, False, scratch[:10])
+    qkv = DpGather(copies, qkv_slab, qkv_ref, *scratch[10:12])
+    outw = DpGather(copies, outw_slab, outw_ref, *scratch[12:14])
+    copy_in, part_in, part_out, copy_sems, part_sems = scratch[14:]
 
     def small_copy(axis, own, size, source, slots, sems, step, slot):
         return pltpu.make_async_remote_copy(
@@ -823,13 +796,50 @@
     row = lax.broadcasted_iota(jnp.int32, every.shape, 0)
     small_out[...] = jnp.where(row < shared, every, part_out[...])
     qkv.finish()
-    widen(qkv.held, qkv_ref, qkv.at.outer)
     outw.finish()
-    widen(outw.held, outw_ref, outw.at.outer)
     each(chunks, summed.finish)
 
 
-def call(kernel, name, number, inputs, outputs, scratch, flops):
+def user_of(owner, head):
+    user = jnp.int32(0)
+    for pair in range(owner.shape[0]):
+        user = user + jnp.where(owner[pair] == head, pair, 0)
+    return user
+
+
+def pick_gradient(owner, place, every, pairs):
+    _, rows, slim = every.shape
+    width = slim // pairs
+
+    def kernel(owner, place, *refs):
+        for slot in range(pairs):
+            held = refs[slot][0]
+            user = lax.rem(user_of(owner, place[0] * pairs + slot), pairs)
+            value = held[:, 0:width]
+            for part in range(1, pairs):
+                value = jnp.where(user == part, held[:, part * width : (part + 1) * width], value)
+            refs[-1][:, slot * width : (slot + 1) * width] = value
+
+    def block(slot):
+        return pl.BlockSpec(
+            (1, rows // 4, slim),
+            lambda g, o, m: (lax.div(user_of(o, m[0] * pairs + slot), pairs), g, 0),
+        )
+
+    return pl.pallas_call(
+        kernel,
+        grid_spec=pltpu.PrefetchScalarGridSpec(
+            num_scalar_prefetch=2,
+            grid=(4,),
+            in_specs=[block(slot) for slot in range(pairs)],
+            out_specs=pl.BlockSpec((rows // 4, slim), lambda g, o, m: (g, 0)),
+        ),
+        out_shape=jax.ShapeDtypeStruct((rows, slim), BF16),
+        name="pick_gradient",
+    )(owner, place, *([every] * pairs))
+
+
+def call(kernel, number, inputs, outputs, scratch, flops):
     moved = sum(a.size * a.dtype.itemsize for a in (*inputs, *outputs))
     return pl.pallas_call(
         kernel,
@@ -839,7 +849,6 @@
         scratch_shapes=scratch,
         compiler_params=pltpu.CompilerParams(collective_id=number, has_side_effects=True),
         cost_estimate=pl.CostEstimate(flops=flops, bytes_accessed=moved, transcendentals=0),
-        name=name,
     )(*inputs)
 
 
@@ -869,7 +878,6 @@
     local_rows, model_width = inputs.shape
     group_rows = local_rows * lax.axis_size("mp")
     pairs_dev, head_size = qkv_weight.shape[1], qkv_weight.shape[3]
-    all_pairs = value_owner.shape[0]
     seats = (seq_lengths, value_owner, lax.axis_index("mp").reshape(1).astype(jnp.int32))
     copies = lax.axis_size("dp")
 
@@ -892,7 +900,7 @@
     dense = 2 * group_rows * model_width
 
     rows_one, all_first = call(
-        functools.partial(open_kernel, count, chunk), "open_rows", 0,
+        functools.partial(open_kernel, count, chunk), 0,
         (inputs, attn_norm_gain.reshape(row), attn_norm_bias.reshape(row), first_values.reshape(group_rows, slim)),
         [like(whole, BF16), like((count, group_rows, slim), BF16)],
         main_sems + side_sems, dense * 100,
@@ -900,11 +908,10 @@
     rows_one = rows_one.reshape(group_rows, model_width)
     packed = (product(rows_one, qkv_pack) + bias_pack).astype(BF16)
     cotangent_late = lax.optimization_barrier((cotangent, rows_one))[0]
-    with jax.named_scope("gradrows"):
-        grad_rows = lax.all_gather(cotangent_late, "mp", axis=0, tiled=True)
+    grad_rows = lax.all_gather(cotangent_late, "mp", axis=0, tiled=True)
     mixed, totals = attend_forward(*seats, packed, all_first)
     rows_two, residual = call(
-        functools.partial(attend_out_kernel, count, chunk), "attend_out", 1,
+        functools.partial(attend_out_kernel, count, chunk), 1,
         (mixed, out_flat, inputs, out_bias.reshape(row), mlp_norm_gain.reshape(row), mlp_norm_bias.reshape(row)),
         [like(whole, BF16), like(inputs.shape, F32)],
         sum_scratch + main_sems, dense * 256,
@@ -922,14 +929,14 @@
     def sliced(values):
         return values.reshape(outer, inner, values.shape[0] // copies, values.shape[1])
 
-    grad_up_weight, grad_down_weight = sliced(grad_up_weight), sliced(grad_down_weight)
-    up_slab, down_slab = (like(part.shape[2:], BF16) for part in (grad_up_weight, grad_down_weight))
-    resid_rows, grad_residual, sums_two, up_slab, down_slab = call(
-        functools.partial(mlp_back_kernel, count, copies, chunk), "mlp_back", 2,
-        (grad_pre, up_weight, residual, cotangent, mlp_norm_gain.reshape(row), grad_up_weight, grad_down_weight),
-        [like(whole, BF16), like(inputs.shape, F32), like((8, model_width), F32), up_slab, down_slab],
-        sum_scratch + main_sems + reduce_scratch(copies, grad_up_weight) + reduce_scratch(copies, grad_down_weight),
-        dense * up_bias.shape[0],
+    late = (grad_up_weight, grad_down_weight)
+    grad_pre, late = lax.optimization_barrier((grad_pre, late))
+    late_sums = lax.psum(late, "dp")
+    resid_rows, grad_residual, sums_two = call(
+        functools.partial(mlp_back_kernel, count, chunk), 2,
+        (grad_pre, up_weight, residual, cotangent, mlp_norm_gain.reshape(row)),
+        [like(whole, BF16), like(inputs.shape, F32), like((8, model_width), F32)],
+        sum_scratch + main_sems, dense * up_bias.shape[0],
     )
     resid_rows = resid_rows.reshape(group_rows, model_width)
     grad_mixed = back_product(resid_rows, out_flat).astype(BF16)
@@ -940,15 +947,13 @@
     grad_qv_bias = jnp.concatenate([pack_sums[:, 0:2], pack_sums[:, 4:5]], axis=1)
     grad_qkv_weight = sliced(rows_product(rows_one, grad_flat).astype(BF16))
     grad_out_weight = sliced(grad_out_weight)
-    grad_inputs, every_skip, sums_one, up_sum, down_sum, qkv_slab, out_slab = call(
-        functools.partial(input_back_kernel, count, copies, chunk), "input_back", 3,
+    grad_inputs, every_skip, sums_one, qkv_slab, out_slab = call(
+        functools.partial(input_back_kernel, count, copies, chunk), 3,
         (grad_flat, qkv_pack, inputs, grad_residual, attn_norm_gain.reshape(row),
-         grad_pack[:, :, 5].reshape(group_rows, slim), up_slab, down_slab, grad_qkv_weight, grad_out_weight),
+         grad_pack[:, :, 5].reshape(group_rows, slim), grad_qkv_weight, grad_out_weight),
         [like(inputs.shape, BF16), like((count, group_rows, slim), BF16), like((8, model_width), F32),
-         like(grad_up_weight.shape, F32), like(grad_down_weight.shape, F32),
          like(grad_qkv_weight.shape[2:], BF16), like(grad_out_weight.shape[2:], BF16)],
-        sum_scratch + side_sems + reduce_scratch(copies, grad_out_weight) + reduce_scratch(copies, grad_qkv_weight)
-        + gather_scratch(copies, grad_up_weight) + gather_scratch(copies, grad_down_weight),
+        sum_scratch + side_sems + reduce_scratch(copies, grad_out_weight) + reduce_scratch(copies, grad_qkv_weight),
         dense * pairs_dev * PACK * head_size,
     )
     wide_bias = jnp.pad(grad_up_bias, (0, model_width - grad_up_bias.shape[0])).reshape(row)
@@ -956,26 +961,18 @@
     own_sums = jnp.concatenate([sums_two[0:4], sums_one[0:2], wide_bias, slim_bias], axis=0)
     block = pltpu.VMEM(own_sums.shape, F32)
     output, small, qkv_sum, out_sum = call(
-        functools.partial(mlp_out_kernel, count, copies, chunk, 6), "mlp_out", 4,
+        functools.partial(mlp_out_kernel, count, copies, chunk, 6), 4,
         (hidden, down_weight, residual, down_bias.reshape(row), own_sums, qkv_slab, out_slab),
         [like(inputs.shape, BF16), like(own_sums.shape, F32),
-         like(grad_qkv_weight.shape, F32), like(grad_out_weight.shape, F32)],
-        sum_scratch + gather_scratch(copies, grad_qkv_weight) + gather_scratch(copies, grad_out_weight)
+         like(grad_qkv_weight.shape, BF16), like(grad_out_weight.shape, BF16)],
+        sum_scratch + gather_scratch(copies) + gather_scratch(copies)
         + [pltpu.VMEM((copies, *own_sums.shape), F32), pltpu.VMEM((count, *own_sums.shape), F32), block,
            pltpu.SemaphoreType.DMA((2, copies)), pltpu.SemaphoreType.DMA((2, count))],
         dense * up_bias.shape[0],
     )
-    qkv_sum = qkv_sum.reshape(model_width, pairs_dev, PACK, head_size)[:, :, 0:5]
-    late_sums = (up_sum.reshape(up_weight.shape), down_sum.reshape(down_weight.shape), out_sum.reshape(out_weight.shape))
-    owned = lax.axis_index("mp") * pairs_dev + jnp.arange(pairs_dev, dtype=jnp.int32)
-    every_pair = jnp.arange(all_pairs, dtype=jnp.int32)
-    inverse = jnp.sum(
-        jnp.where(value_owner[None, :] == owned[:, None], every_pair[None, :], 0), axis=1
-    )
-    every_skip = every_skip.reshape(count, group_rows, pairs_dev, head_size)
-    grad_first = jnp.stack(
-        [every_skip[inverse[p] // pairs_dev, :, inverse[p] % pairs_dev] for p in range(pairs_dev)], axis=1
-    )
+    qkv_sum = qkv_sum.reshape(model_width, pairs_dev, PACK, head_size)[:, :, 0:5].astype(F32)
+    late_sums = (*(part.astype(F32) for part in late_sums), out_sum.reshape(out_weight.shape).astype(F32))
+    grad_first = pick_gradient(*seats[1:], every_skip, pairs_dev).reshape(group_rows, pairs_dev, head_size)
     norm_sums = (small[4], small[5], small[2], small[0], small[1], small[3])
     bias_sums = (small[7, : grad_qv_bias.size].reshape(qv_bias.shape), small[6, : grad_up_bias.shape[0]])
 

time: 480 us -> 444 us (0.925)
  the two profiles are of different devices: /device:TPU:0 before, /device:TPU:16 now
where the time goes in v2:
time: 444 us; the launch traced here: 435 us
  Pallas kernels  327 us (74%)
  matrix products  58.5 us (13%)
  local copies, waits for them, and re-layouts  22.2 us (5%)
  between operations  14.5 us (3%)
  other arithmetic  12.9 us (3%)
    pallas_call x5, Pallas kernels, call(): pl.pallas_call(kernel, out_shape=outputs, in_specs=[pl.BlockSpec(memory_s...  278 us
    pallas_call x1, Pallas kernels, attend_backward(): pl.pallas_call(functools.partial(attend_backward_kernel, pairs), grid_spe...  27.1 us
    dot_general x4, matrix products, rows_product(): lax.dot_general(left, right, (((0,), (0,)), ((), ())), preferred_element_...  21.1 us
    dot_general x2, matrix products, back_product(): lax.dot_general(left, weight, (((1,), (1,)), ((), ())), preferred_element...  21 us
    pallas_call x1, Pallas kernels, attend_forward(): pl.pallas_call(functools.partial(attend_forward_kernel, pairs), grid_spec...  17.4 us
    dot_general x2, matrix products, product(): return jnp.dot(left, right, preferred_element_type=F32)  16.4 us
  transfers between devices with their start and end apart: 2, of which 0 were waited for; matrix products, arithmetic and copies ran while one was open for 13% of the time, Pallas kernels for 65%

profile of v2, /device:TPU:16, one launch (start us, length us, event | category | flops | bytes accessed | tf_op | source)
XLA Modules:
  0.0 435.0 jit_solution(8990851747261121418)
XLA Ops:
  7.2 2.1 copy.38.first_ref
  9.4 42.3 %shard_map.280 = (bf16[4,512,1024]{2,1,0:T(8,128)(2,1)}, bf16[4,2048,128]{2,1,0:T(8,128)(2,1)}) custom-call(bf16[512,1024]{1,0:T(8,128)(2,1)} %x_ref.5, f32[1,1024]{1,0:T(1,128)} %bitcast.57, f32[1,1024]{1,0:T(1,128)} %bitcast.56, bf16[2048,128]{1,0:T(8,128)(2,1)} %copy.38.first_ref), custom_call_target="tpu_custom_call" | custom-call | flops 419430400 | bytes 7872512 | tf_op jit(solution)/shard_map/pallas_call | solution.py:844
  55.3 7.4 %add_convert_fusion.qkv_ref = bf16[2048,768]{1,0:T(8,128)(2,1)} fusion(bf16[2048,1024]{1,0:T(8,128)(2,1)} %bitcast.67, bf16[1024,768]{0,1:T(8,128)(2,1)S(1)} %bitcast.49, f32[768]{0:T(1024)S(1)} %add.35), kind=kOutput, calls=%fused_computation.13 | convolution fusion | flops 3224371200 | bytes 8915968 | tf_op jit(solution)/shard_map/dot_general | solution.py:36
  62.7 17.4 %attend_forward.1 = (bf16[2048,256]{1,0:T(8,128)(2,1)}, f32[2048,256]{1,0:T(8,128)}) custom-call(s32[4]{0:T(128)} %lengths.3, s32[8]{0:T(128)} %owner.5, s32[1]{0:T(128)} %bitcast.place, bf16[2048,768]{1,0:T(8,128)(2,1)} %add_convert_fusion.qkv_ref, bf16[4,2048,128]{2,1,0:T(8,128)(2,1)} %get-tuple-element.38.first_ref), custom_call_target="tpu_custom_call" | custom-call | flops 4294967296 | bytes 8388608 | tf_op jit(solution)/shard_map/attend_forward/pallas_call | solution.py:195
  80.0 55.7 %shard_map.281 = (bf16[4,512,1024]{2,1,0:T(8,128)(2,1)}, f32[512,1024]{1,0:T(8,128)}) custom-call(bf16[2048,256]{1,0:T(8,128)(2,1)} %get-tuple-element.39.left, bf16[256,1024]{1,0:T(8,128)(2,1)} %bitcast.69, bf16[512,1024]{1,0:T(8,128)(2,1)} %x_ref.5, f32[1,1024]{1,0:T(1,128)} %bitcast.71, f32[1,1024]{1,0:T(1,128)} %bitcast.73, f32[1,1024]{1,0:T(1,128)} %bitcast.72), custom_call_target="tpu_custom_call" | custom-call | flops 1073741824 | bytes 8925184 | tf_op jit(solution)/shard_map/pallas_call | solution.py:844
  135.8 9.0 %fusion.8 = f32[2048,1024]{1,0:T(8,128)} fusion(bf16[2048,1024]{1,0:T(8,128)(2,1)} %bitcast.78, bf16[1024,1024]{1,0:T(8,128)(2,1)S(1)} %copy-done.11), kind=kOutput, calls=%fused_computation.25 | convolution fusion | flops 4294967296 | bytes 14680064 | tf_op jit(solution)/shard_map/dot_general | solution.py:36
  144.8 16.2 %convert_reduce_fusion = (f32[1024]{0:T(1024)S(1)}, bf16[2048,1024]{1,0:T(8,128)(2,1)S(1)}, bf16[2048,1024]{1,0:T(8,128)(2,1)S(1)}) fusion(f32[2048,1024]{1,0:T(8,128)} %fusion.8, f32[1024]{0:T(1024)S(1)} %copy-done.13, bf16[2048,1024]{1,0:T(8,128)(2,1)} %all-gather.2.cloned.1.call-done, bf16[1024,1024]{1,0:T(8,128)(2,1)} %weight.3), kind=kOutput, calls=%fused_computation.10 | convolution fusion | flops 4355783680 | bytes 23076864 | tf_op jit(solution)/shard_map/dot_general | solution.py:32
  161.0 5.9 %convolution_convert_fusion.2 = bf16[1024,1024]{1,0:T(8,128)(2,1)} fusion(bf16[2048,1024]{1,0:T(8,128)(2,1)S(1)} %bitcast.79, bf16[2048,1024]{1,0:T(8,128)(2,1)S(1)} %get-tuple-element.43.left), kind=kOutput, calls=%fused_computation.16 | convolution fusion | flops 4296015872 | bytes 10485760 | tf_op jit(solution)/shard_map/dot_general | solution.py:28
  166.9 5.8 %convolution_convert_fusion.1 = bf16[1024,1024]{1,0:T(8,128)(2,1)} fusion(bf16[2048,1024]{1,0:T(8,128)(2,1)S(1)} %get-tuple-element.93.left, bf16[2048,1024]{1,0:T(8,128)(2,1)S(1)} %copy-done.10), kind=kOutput, calls=%fused_computation.15 | convolution fusion | flops 4296015872 | bytes 10485760 | tf_op jit(solution)/shard_map/dot_general | solution.py:28
  172.8 60.3 %shard_map.282 = (bf16[4,512,1024]{2,1,0:T(8,128)(2,1)}, f32[512,1024]{1,0:T(8,128)}, f32[8,1024]{1,0:T(8,128)}) custom-call(bf16[2048,1024]{1,0:T(8,128)(2,1)} %copy-done.15, bf16[1024,1024]{1,0:T(8,128)(2,1)} %weight.2, f32[512,1024]{1,0:T(8,128)} %get-tuple-element.41.residual_ref, bf16[512,1024]{1,0:T(8,128)(2,1)} %dy_ref.1, f32[1,1024]{1,0:T(1,128)} %bitcast.74), custom_call_target="tpu_custom_call" | custom-call | flops 4294967296 | bytes 15765504 | tf_op jit(solution)/shard_map/pallas_call | solution.py:844
  233.1 4.8 %convolution_convert_fusion.grad_ref = bf16[2048,256]{1,0:T(8,128)(2,1)} fusion(bf16[2048,1024]{1,0:T(8,128)(2,1)} %bitcast.76, bf16[256,1024]{1,0:T(8,128)(2,1)S(1)} %bitcast.70), kind=kOutput, calls=%fused_computation.14 | convolution fusion | flops 1074266112 | bytes 5767168 | tf_op jit(solution)/shard_map/dot_general | solution.py:32
  237.9 27.1 %attend_backward.1.left = bf16[2048,768]{1,0:T(8,128)(2,1)} custom-call(s32[4]{0:T(128)} %lengths.3, s32[8]{0:T(128)} %owner.5, s32[1]{0:T(128)} %bitcast.place, bf16[2048,768]{1,0:T(8,128)(2,1)} %add_convert_fusion.qkv_ref, bf16[4,2048,128]{2,1,0:T(8,128)(2,1)} %get-tuple-element.38.first_ref, bf16[2048,256]{1,0:T(8,128)(2,1)} %convolution_convert_fusion.grad_ref, ...), custom_call_target="tpu_custom_call" | custom-call | flops 10737418240 | bytes 8388608 | tf_op jit(solution)/shard_map/attend_backward/pallas_call | solution.py:223
  265.0 2.6 convert_reduce_fusion.1
  267.8 2.9 copy.40
  270.9 1.9 slice.64
  272.7 2.0 copy.42.skip_ref
  274.8 4.7 %convolution_convert_fusion.4 = bf16[256,1024]{1,0:T(8,128)(2,1)} fusion(bf16[2048,256]{1,0:T(8,128)(2,1)} %get-tuple-element.39.left, bf16[2048,1024]{1,0:T(8,128)(2,1)} %bitcast.77), kind=kOutput, calls=%fused_computation.19 | convolution fusion | flops 1074003968 | bytes 5767168 | tf_op jit(solution)/shard_map/dot_general | solution.py:28
  279.5 4.7 %convolution_convert_fusion.3 = bf16[1024,768]{1,0:T(8,128)(2,1)} fusion(bf16[2048,1024]{1,0:T(8,128)(2,1)S(1)} %bitcast.68, bf16[2048,768]{1,0:T(8,128)(2,1)S(1)} %copy-done), kind=kOutput, calls=%fused_computation.17 | convolution fusion | flops 3222011904 | bytes 8912896 | tf_op jit(solution)/shard_map/dot_general | solution.py:28
  284.2 67.6 %shard_map.283 = (bf16[512,1024]{1,0:T(8,128)(2,1)}, bf16[4,2048,128]{2,1,0:T(8,128)(2,1)}, f32[8,1024]{1,0:T(8,128)}, bf16[128,768]{1,0:T(8,128)(2,1)}, bf16[32,1024]{1,0:T(8,128)(2,1)}) custom-call(bf16[2048,768]{1,0:T(8,128)(2,1)} %attend_backward.1.left, bf16[1024,768]{1,0:T(8,128)(2,1)} %copy.41.weight, bf16[512,1024]{1,0:T(8,128)(2,1)} %x_ref.5, ...), custom_call_target="tpu_custom_call" | custom-call | flops 3221225472 | bytes 13930496 | tf_op jit(solution)/shard_map/pallas_call | solution.py:844
  353.2 52.0 %shard_map.284 = (bf16[512,1024]{1,0:T(8,128)(2,1)}, f32[8,1024]{1,0:T(8,128)}, bf16[4,2,128,768]{3,2,1,0:T(8,128)(2,1)}, bf16[4,2,32,1024]{3,2,1,0:T(8,128)(2,1)}) custom-call(bf16[2048,1024]{1,0:T(8,128)(2,1)} %copy-done.16, bf16[1024,1024]{1,0:T(8,128)(2,1)} %weight.3, f32[512,1024]{1,0:T(8,128)} %get-tuple-element.41.residual_ref, f32[1,1024]{1,0:T(1,128)} %bitcast.75, ...), custom_call_target="tpu_custom_call" | custom-call | flops 4294967296 | bytes 11866112 | tf_op jit(solution)/shard_map/pallas_call | solution.py:844
  406.7 4.5 %pick_gradient.1 = bf16[2048,128]{1,0:T(8,128)(2,1)} custom-call(s32[8]{0:T(128)} %owner.5, s32[1]{0:T(128)} %bitcast.place, bf16[4,2048,128]{2,1,0:T(8,128)(2,1)} %get-tuple-element.53.refs_0_.refs_1_, bf16[4,2048,128]{2,1,0:T(8,128)(2,1)} %get-tuple-element.53.refs_0_.refs_1_), custom_call_target="tpu_custom_call" | custom-call | tf_op jit(solution)/shard_map/pick_gradient/pallas_call | solution.py:829
  411.2 2.0 copy.43
  419.3 4.2 convert_element_type.62
  423.5 2.5 convert_element_type.63
  (69 shorter events, 14.9 us)
Async XLA Ops:
  7.2 46.3 %copy-start.3 = (bf16[1024,2,5,64]{0,3,2,1:T(8,128)(2,1)S(1)}, bf16[1024,2,5,64]{0,3,2,1:T(8,128)(2,1)}, u32[]{:S(2)}) copy-start(bf16[1024,2,5,64]{0,3,2,1:T(8,128)(2,1)} %param.24) | copy-start | bytes 3932164
  7.2 137.6 %all-gather.2.cloned.1.call-start = ((), (), s32[]{:S(2)}) async-start(), calls=%async_computation | async-start | bytes 5242880 | tf_op jit(solution)/shard_map/all_gather | solution.py:911
  51.7 367.6 %all-reduce.5.cloned.1.call-start = ((), (), s32[]{:S(2)}) async-start(), calls=%async_computation.1 | async-start | bytes 8388608 | tf_op jit(solution)/shard_map/psum | solution.py:934
  62.7 73.1 %copy-start.11 = (bf16[1024,1024]{1,0:T(8,128)(2,1)S(1)}, bf16[1024,1024]{1,0:T(8,128)(2,1)}, u32[]{:S(2)}) copy-start(bf16[1024,1024]{1,0:T(8,128)(2,1)} %weight.2) | copy-start | bytes 6291460
  135.7 9.0 %copy-start.13 = (f32[1024]{0:T(1024)S(1)}, f32[1024]{0:T(1024)}, u32[]{:S(2)}) copy-start(f32[1024]{0:T(1024)} %param.31) | copy-start | bytes 12292
  144.8 16.2 %copy-start.14 = (bf16[4,512,1024]{2,1,0:T(8,128)(2,1)S(1)}, bf16[4,512,1024]{2,1,0:T(8,128)(2,1)}, u32[]{:S(2)}) copy-start(bf16[4,512,1024]{2,1,0:T(8,128)(2,1)} %get-tuple-element.40) | copy-start | bytes 12582916
  161.0 5.9 %copy-start.15 = (bf16[2048,1024]{1,0:T(8,128)(2,1)}, bf16[2048,1024]{1,0:T(8,128)(2,1)S(1)}, u32[]{:S(2)}) copy-start(bf16[2048,1024]{1,0:T(8,128)(2,1)S(1)} %get-tuple-element.43.left) | copy-start | bytes 12582916
  161.0 5.9 %copy-start.16 = (bf16[2048,1024]{1,0:T(8,128)(2,1)}, bf16[2048,1024]{1,0:T(8,128)(2,1)S(1)}, u32[]{:S(2)}) copy-start(bf16[2048,1024]{1,0:T(8,128)(2,1)S(1)} %get-tuple-element.93.left) | copy-start | bytes 12582916
  161.0 5.9 %copy-start.10 = (bf16[2048,1024]{1,0:T(8,128)(2,1)S(1)}, bf16[2048,1024]{1,0:T(8,128)(2,1)}, u32[]{:S(2)}) copy-start(bf16[2048,1024]{1,0:T(8,128)(2,1)} %all-gather.2.cloned.1.call-done) | copy-start | bytes 12582916
  172.8 60.3 %copy-start.12 = (bf16[2,2,64,1024]{3,2,1,0:T(8,128)(2,1)S(1)}, bf16[2,2,64,1024]{3,2,1,0:T(8,128)(2,1)}, u32[]{:S(2)}) copy-start(bf16[2,2,64,1024]{3,2,1,0:T(8,128)(2,1)} %param.26) | copy-start | bytes 1572868
  265.0 2.9 copy-start
  265.0 5.8 %copy-start.8 = (f32[8,1024]{1,0:T(8,128)S(1)}, f32[8,1024]{1,0:T(8,128)}, u32[]{:S(2)}) copy-start(f32[8,1024]{1,0:T(8,128)} %get-tuple-element.44) | copy-start | bytes 98308
  274.8 4.7 %copy-start.9 = (bf16[4,512,1024]{2,1,0:T(8,128)(2,1)S(1)}, bf16[4,512,1024]{2,1,0:T(8,128)(2,1)}, u32[]{:S(2)}) copy-start(bf16[4,512,1024]{2,1,0:T(8,128)(2,1)} %get-tuple-element.37) | copy-start | bytes 12582916
  405.1 8.1 %copy-start.6 = (bf16[4,2,32,1024]{3,2,1,0:T(8,128)(2,1)S(1)}, bf16[4,2,32,1024]{3,2,1,0:T(8,128)(2,1)}, u32[]{:S(2)}) copy-start(bf16[4,2,32,1024]{3,2,1,0:T(8,128)(2,1)} %get-tuple-element.56) | copy-start | bytes 1572868
  405.1 9.2 %copy-start.2 = (bf16[4,2,128,768]{3,2,1,0:T(8,128)(2,1)S(1)}, bf16[4,2,128,768]{3,2,1,0:T(8,128)(2,1)}, u32[]{:S(2)}) copy-start(bf16[4,2,128,768]{3,2,1,0:T(8,128)(2,1)} %get-tuple-element.55) | copy-start | bytes 4718596
  413.2 3.6 copy-start.7
  419.3 4.2 copy-start.1
  423.5 2.5 copy-start.5
  423.5 3.5 copy-start.4
Sparse Core Ops, SparseCore 0:
  51.9 35.2 all-gather.1
  172.9 173.0 all-reduce.4

commit v3 on v2

--- a/solution.py
+++ b/solution.py
@@ -55,18 +55,18 @@
     return column <= row
 
 
-def pick_values(half, qkv_ref, first_ref, value_ref):
-    held = first_ref[0]
+def pick_values(half, fresh, held, value_ref):
     if held.shape[1] < LANES:
         turned = jnp.concatenate([held, held], axis=1)
     else:
         turned = jnp.concatenate([held[:, LANES // 2 :], held[:, : LANES // 2]], axis=1)
         turned = jnp.where(half == 1, held, turned)
-    value_ref[...] = jnp.where(head_lanes(0), qkv_ref[:, 2 * LANES : 3 * LANES], turned)
+    value_ref[...] = jnp.where(head_lanes(0), fresh, turned)
 
 
 def attend_forward_kernel(pairs, lengths, owner, place, qkv_ref, first_ref, mixed_ref, totals_ref, value_ref):
-    pick_values(lax.rem(owner[place[0] * pairs + pl.program_id(0)], pairs), qkv_ref, first_ref, value_ref)
+    half = lax.rem(owner[place[0] * pairs + pl.program_id(0)], pairs)
+    pick_values(half, qkv_ref[:, 2 * LANES : 3 * LANES], first_ref[0], value_ref)
     blocks = qkv_ref.shape[0] // SHORT
     scale = (LANES // 2) ** (-0.5)
 
@@ -125,22 +125,37 @@
 
 
 def attend_backward_kernel(
-    pairs, lengths, owner, place, qkv_ref, first_ref, grad_ref, totals_ref, out_ref, key_sum, value_sum, value_ref
+    count, chunk, pairs, lengths, owner, qkv_ref, first_ref, grad_ref, totals_ref, left, weight, residual_ref, shift_ref,
+    out_ref, skip_ref, sums_ref, layer_ref, key_sum, value_sum, value_ref, *scratch
 ):
-    pick_values(lax.rem(owner[place[0] * pairs + pl.program_id(0)], pairs), qkv_ref, first_ref, value_ref)
     blocks = qkv_ref.shape[0] // SHORT
     scale = (LANES // 2) ** (-0.5)
-    key_sum[...] = jnp.zeros_like(key_sum)
-    value_sum[...] = jnp.zeros_like(value_sum)
-
-    def block(index, carried):
-        base = pl.multiple_of(index * SHORT, SHORT)
-        for half in range(SHORT // QROWS):
-            first = base + half * QROWS
-
-            def attend(with_previous):
-                query = qkv_ref[pl.ds(first, QROWS), 0:LANES] * jnp.asarray(scale, BF16)
-                grad = grad_ref[pl.ds(first, QROWS), :]
+    place, _, _ = mesh_place(count)
+    greet(count)
+    rows = residual_ref.shape[0]
+    chunks = rows // chunk
+    summed = RowSum(count, rows, chunk, left, weight, False, scratch)
+    sums_ref[...] = jnp.zeros_like(sums_ref)
+    summed.send()
+
+    def one_pair(pair):
+        column = pl.multiple_of(pair * 3 * LANES, LANES)
+        side = pl.multiple_of(pair * LANES, LANES)
+        query_at, key_at, fresh_at = (pl.ds(column + part * LANES, LANES) for part in range(3))
+        used = owner[place * pairs + pair]
+        held = first_ref[lax.div(used, pairs)]
+        pick_values(lax.rem(used, pairs), qkv_ref[:, fresh_at], held, value_ref)
+        key_sum[...] = jnp.zeros_like(key_sum)
+        value_sum[...] = jnp.zeros_like(value_sum)
+
+        def block(index):
+            base = pl.multiple_of(index * SHORT, SHORT)
+            joined = opens_at(lengths, base) == 0
+
+            def attend(half, with_previous):
+                first = base + half * QROWS
+                query = qkv_ref[pl.ds(first, QROWS), query_at] * jnp.asarray(scale, BF16)
+                grad = grad_ref[pl.ds(first, QROWS), pl.ds(side, LANES)]
                 spans = []
                 if with_previous:
                     spans.append((base - SHORT, SHORT))
@@ -148,46 +163,67 @@
                     spans.append((base, half * QROWS))
                 spans.append((first, QROWS))
                 grad_query = jnp.zeros((QROWS, LANES), F32)
+                both = totals_ref[pl.ds(first, QROWS), pl.ds(side, LANES)]
                 for head in range(2):
                     chosen = head_lanes(head)
                     query_head = jnp.where(chosen, query, jnp.zeros_like(query))
                     grad_head = jnp.where(chosen, grad, jnp.zeros_like(grad))
                     at_lane = head * (LANES // 2)
-                    totals = totals_ref[pl.ds(first, QROWS), at_lane : at_lane + 1]
+                    totals = both[:, at_lane : at_lane + 1]
                     probs, grads = [], []
                     inner = jnp.zeros((QROWS, 1), F32)
-                    for at, size in spans:
-                        keys = qkv_ref[pl.ds(at, size), LANES : 2 * LANES]
+                    for number, (at, size) in enumerate(spans):
+                        keys = qkv_ref[pl.ds(at, size), key_at]
                         part = jnp.exp(back_product(query_head, keys) - totals)
-                        if at is first:
+                        if number == len(spans) - 1:
                             part = jnp.where(causal_tile(), part, 0.0)
+                        elif with_previous and number == 0:
+                            part = jnp.where(joined, part, 0.0)
                         values = value_ref[pl.ds(at, size), :]
                         weighted = part * back_product(grad_head, values)
                         inner = inner + weighted.sum(axis=1, keepdims=True)
                         probs.append(part)
                         grads.append(weighted)
                     for (at, size), part, weighted in zip(spans, probs, grads):
-                        keys = qkv_ref[pl.ds(at, size), LANES : 2 * LANES]
+                        keys = qkv_ref[pl.ds(at, size), key_at]
                         keys = jnp.where(chosen, keys, jnp.zeros_like(keys))
                         grad_scores = (weighted - part * inner).astype(BF16)
                         grad_query = grad_query + product(grad_scores, keys)
                         key_sum[pl.ds(at, size), :] += rows_product(grad_scores, query_head)
                         value_sum[pl.ds(at, size), :] += rows_product(part.astype(BF16), grad_head)
-                out_ref[pl.ds(first, QROWS), 0:LANES] = (grad_query * scale).astype(BF16)
-
-            @pl.when(opens_at(lengths, base) == 0)
+                out_ref[pl.ds(first, QROWS), query_at] = (grad_query * scale).astype(BF16)
+
+            for half in range(SHORT // QROWS):
+
+                @pl.when(index > 0)
+                def _():
+                    attend(half, True)
+
+                @pl.when(index == 0)
+                def _():
+                    attend(half, False)
+
+        each(blocks, block)
+        out_ref[:, key_at] = key_sum[...].astype(BF16)
+        out_ref[:, fresh_at] = value_sum[...].astype(BF16)
+        for slot in range(pairs):
+
+            @pl.when(pair == slot)
             def _():
-                attend(True)
-
-            @pl.when(opens_at(lengths, base) == 1)
-            def _():
-                attend(False)
-
-        return carried
-
-    lax.fori_loop(0, blocks, block, 0)
-    out_ref[:, LANES : 2 * LANES] = key_sum[...].astype(BF16)
-    out_ref[:, 2 * LANES : 3 * LANES] = value_sum[...].astype(BF16)
+                width = LANES // 2
+                skip_ref[:, slot * width : (slot + 1) * width] = value_sum[:, width:].astype(BF16)
+
+        for at in (query_at, fresh_at):
+            sums_ref[0:1, at] = column_sum(out_ref[:, at].astype(F32))
+
+    each(pairs, one_pair)
+
+    def close(index):
+        at = rows_at(index, chunk)
+        layer_ref[at, :] = (residual_ref[at, :] + summed.total(index) + shift_ref[...]).astype(BF16)
+
+    each(chunks, close)
+    each(chunks, summed.finish)
 
 
 def attend_forward(lengths, owner, place, packed, firsts):
@@ -218,34 +254,6 @@
     )(lengths, owner, place, packed, firsts)
 
 
-def attend_backward(lengths, owner, place, packed, firsts, grad, totals):
-    rows, pairs = packed.shape[0], packed.shape[1] // (3 * LANES)
-    return pl.pallas_call(
-        functools.partial(attend_backward_kernel, pairs),
-        grid_spec=pltpu.PrefetchScalarGridSpec(
-            num_scalar_prefetch=3,
-            grid=(pairs,),
-            in_specs=[
-                pl.BlockSpec((rows, 3 * LANES), lambda p, c, o, m: (0, p)),
-                pl.BlockSpec((1, rows, firsts.shape[2]), lambda p, c, o, m: (lax.div(o[m[0] * pairs + p], pairs), 0, 0)),
-                pl.BlockSpec((rows, LANES), lambda p, c, o, m: (0, p)),
-                pl.BlockSpec((rows, LANES), lambda p, c, o, m: (0, p)),
-            ],
-            out_specs=pl.BlockSpec((rows, 3 * LANES), lambda p, c, o, m: (0, p)),
-            scratch_shapes=[
-                pltpu.VMEM((rows, LANES), F32),
-                pltpu.VMEM((rows, LANES), F32),
-                pltpu.VMEM((rows, LANES), BF16),
-            ],
-        ),
-        out_shape=jax.ShapeDtypeStruct((rows, pairs * 3 * LANES), BF16),
-        cost_estimate=pl.CostEstimate(
-            flops=rows * 1024 * 256 * 10 * pairs, bytes_accessed=8 << 20, transcendentals=rows * 2048
-        ),
-        name="attend_backward",
-    )(lengths, owner, place, packed, firsts, grad, totals)
-
-
 def mesh_place(count):
     place = lax.axis_index("mp")
     core = lax.rem(place, 2)
@@ -694,28 +702,19 @@
 
 
 def input_back_kernel(
-    count, copies, chunk, left, weight, x_ref, grad_ref, gain_ref, skip_ref, qkv_ref, outw_ref,
-    out_ref, all_ref, sums_ref, qkv_slab, outw_slab, *scratch
+    count, copies, chunk, left, weight, x_ref, grad_ref, gain_ref, qkv_ref, outw_ref,
+    out_ref, sums_ref, qkv_slab, outw_slab, *scratch
 ):
     rows = x_ref.shape[0]
-    place, _, _ = mesh_place(count)
     greet(count, copies)
     chunks = rows // chunk
     summed = RowSum(count, rows, chunk, left, weight, True, scratch[:10])
-    side_chunk = skip_ref.shape[0] // 2
-    side = Gather(count, all_ref, side_chunk, *scratch[10:13])
-    outw = DpReduce(copies, outw_ref, *scratch[13:18])
-    qkv = DpReduce(copies, qkv_ref, *scratch[18:23])
+    outw = DpReduce(copies, outw_ref, *scratch[10:15])
+    qkv = DpReduce(copies, qkv_ref, *scratch[15:20])
     qkv.send()
     outw.send()
     sums_ref[...] = jnp.zeros_like(sums_ref)
     summed.send()
-
-    def side_start(index):
-        all_ref[place, rows_at(index, side_chunk), :] = skip_ref[rows_at(index, side_chunk), :]
-        side.send(index)
-
-    each(2, side_start)
 
     def close(index):
         at = rows_at(index, chunk)
@@ -727,18 +726,15 @@
         spread(index, chunks, copies, [qkv.pass_on, outw.pass_on])
 
     each(chunks, close)
-    each(2, side.hand_on)
     qkv_slab[...] = qkv.total().astype(BF16)
     outw_slab[...] = outw.total().astype(BF16)
-    each(2, side.finish)
     each(chunks, summed.finish)
 
 
-def mlp_out_kernel(
-    count, copies, chunk, shared, left, weight, residual_ref, bias_ref, small_ref, qkv_slab, outw_slab,
-    out_ref, small_out, qkv_ref, outw_ref, *scratch
+def closing_kernel(
+    count, copies, shared, small_ref, skip_ref, qkv_slab, outw_slab,
+    small_out, all_ref, qkv_ref, outw_ref, *scratch
 ):
-    rows = residual_ref.shape[0]
     copy, place = lax.axis_index("dp"), lax.axis_index("mp")
     barrier = pltpu.get_barrier_semaphore()
     for step in range(1, copies):
@@ -750,11 +746,11 @@
             barrier, inc=1, device_id={"mp": lax.rem(place + step, count)}, device_id_type=pl.DeviceIdType.MESH
         )
     pl.semaphore_wait(barrier, copies + count - 2)
-    chunks = rows // chunk
-    summed = RowSum(count, rows, chunk, left, weight, False, scratch[:10])
-    qkv = DpGather(copies, qkv_slab, qkv_ref, *scratch[10:12])
-    outw = DpGather(copies, outw_slab, outw_ref, *scratch[12:14])
-    copy_in, part_in, part_out, copy_sems, part_sems = scratch[14:]
+    side_chunk = skip_ref.shape[0] // 2
+    side = Gather(count, all_ref, side_chunk, *scratch[0:3])
+    qkv = DpGather(copies, qkv_slab, qkv_ref, *scratch[3:5])
+    outw = DpGather(copies, outw_slab, outw_ref, *scratch[5:7])
+    copy_in, part_in, part_out, copy_sems, part_sems = scratch[7:]
 
     def small_copy(axis, own, size, source, slots, sems, step, slot):
         return pltpu.make_async_remote_copy(
@@ -782,22 +778,27 @@
     small_start(*over_copies)
     qkv.send()
     outw.send()
-    summed.send()
+
+    def side_start(index):
+        all_ref[place, rows_at(index, side_chunk), :] = skip_ref[rows_at(index, side_chunk), :]
+        side.send(index)
+
+    each(2, side_start)
     part_out[...] = small_total(*over_copies)
     small_start(*over_parts)
-
-    def close(index):
-        at = rows_at(index, chunk)
-        out_ref[at, :] = (residual_ref[at, :] + summed.total(index) + bias_ref[...]).astype(BF16)
-        spread(index, chunks, copies, [qkv.pass_on, outw.pass_on])
-
-    each(chunks, close)
     every = small_total(*over_parts)
     row = lax.broadcasted_iota(jnp.int32, every.shape, 0)
     small_out[...] = jnp.where(row < shared, every, part_out[...])
+
+    def pass_on(index):
+        qkv.pass_on(index)
+        outw.pass_on(index)
+
+    each(qkv.at.outer, pass_on)
+    each(2, side.hand_on)
+    outw.finish()
     qkv.finish()
-    outw.finish()
-    each(chunks, summed.finish)
+    each(2, side.finish)
 
 
 def user_of(owner, head):
@@ -839,12 +840,13 @@
     )(owner, place, *([every] * pairs))
 
 
-def call(kernel, number, inputs, outputs, scratch, flops):
+def call(kernel, number, inputs, outputs, scratch, flops, scalars=0):
     moved = sum(a.size * a.dtype.itemsize for a in (*inputs, *outputs))
     return pl.pallas_call(
         kernel,
         out_shape=outputs,
-        in_specs=[pl.BlockSpec(memory_space=pltpu.VMEM)] * len(inputs),
+        in_specs=[pl.BlockSpec(memory_space=pltpu.SMEM)] * scalars
+        + [pl.BlockSpec(memory_space=pltpu.VMEM)] * (len(inputs) - scalars),
         out_specs=[pl.BlockSpec(memory_space=pltpu.VMEM)] * len(outputs),
         scratch_shapes=scratch,
         compiler_params=pltpu.CompilerParams(collective_id=number, has_side_effects=True),
@@ -941,34 +943,42 @@
     resid_rows = resid_rows.reshape(group_rows, model_width)
     grad_mixed = back_product(resid_rows, out_flat).astype(BF16)
     grad_out_weight = rows_product(mixed, resid_rows).astype(BF16)
-    grad_flat = attend_backward(*seats, packed, all_first, grad_mixed, totals)
-    grad_pack = grad_flat.reshape(group_rows, pairs_dev, PACK, head_size)
-    pack_sums = jnp.sum(grad_flat.astype(F32), axis=0).reshape(pairs_dev, PACK, head_size)
+    packs = pairs_dev * PACK * head_size
+    grad_flat, grad_skip, pack_sums, output = call(
+        functools.partial(attend_backward_kernel, count, chunk, pairs_dev), 5,
+        (seq_lengths, value_owner, packed, all_first, grad_mixed, totals, hidden, down_weight, residual,
+         down_bias.reshape(row)),
+        [like((group_rows, packs), BF16), like((group_rows, slim), BF16), like((8, packs), F32),
+         like(inputs.shape, BF16)],
+        [pltpu.VMEM((group_rows, LANES), F32), pltpu.VMEM((group_rows, LANES), F32),
+         pltpu.VMEM((group_rows, LANES), BF16)] + sum_scratch,
+        group_rows * 1024 * 256 * 10 * pairs_dev, scalars=2,
+    )
+    pack_sums = pack_sums[0].reshape(pairs_dev, PACK, head_size)
     grad_qv_bias = jnp.concatenate([pack_sums[:, 0:2], pack_sums[:, 4:5]], axis=1)
     grad_qkv_weight = sliced(rows_product(rows_one, grad_flat).astype(BF16))
     grad_out_weight = sliced(grad_out_weight)
-    grad_inputs, every_skip, sums_one, qkv_slab, out_slab = call(
+    grad_inputs, sums_one, qkv_slab, out_slab = call(
         functools.partial(input_back_kernel, count, copies, chunk), 3,
-        (grad_flat, qkv_pack, inputs, grad_residual, attn_norm_gain.reshape(row),
-         grad_pack[:, :, 5].reshape(group_rows, slim), grad_qkv_weight, grad_out_weight),
-        [like(inputs.shape, BF16), like((count, group_rows, slim), BF16), like((8, model_width), F32),
+        (grad_flat, qkv_pack, inputs, grad_residual, attn_norm_gain.reshape(row), grad_qkv_weight, grad_out_weight),
+        [like(inputs.shape, BF16), like((8, model_width), F32),
          like(grad_qkv_weight.shape[2:], BF16), like(grad_out_weight.shape[2:], BF16)],
-        sum_scratch + side_sems + reduce_scratch(copies, grad_out_weight) + reduce_scratch(copies, grad_qkv_weight),
-        dense * pairs_dev * PACK * head_size,
+        sum_scratch + reduce_scratch(copies, grad_out_weight) + reduce_scratch(copies, grad_qkv_weight),
+        dense * packs,
     )
     wide_bias = jnp.pad(grad_up_bias, (0, model_width - grad_up_bias.shape[0])).reshape(row)
     slim_bias = jnp.pad(grad_qv_bias.reshape(-1), (0, model_width - grad_qv_bias.size)).reshape(row)
     own_sums = jnp.concatenate([sums_two[0:4], sums_one[0:2], wide_bias, slim_bias], axis=0)
     block = pltpu.VMEM(own_sums.shape, F32)
-    output, small, qkv_sum, out_sum = call(
-        functools.partial(mlp_out_kernel, count, copies, chunk, 6), 4,
-        (hidden, down_weight, residual, down_bias.reshape(row), own_sums, qkv_slab, out_slab),
-        [like(inputs.shape, BF16), like(own_sums.shape, F32),
+    small, every_skip, qkv_sum, out_sum = call(
+        functools.partial(closing_kernel, count, copies, 6), 4,
+        (own_sums, grad_skip, qkv_slab, out_slab),
+        [like(own_sums.shape, F32), like((count, group_rows, slim), BF16),
          like(grad_qkv_weight.shape, BF16), like(grad_out_weight.shape, BF16)],
-        sum_scratch + gather_scratch(copies) + gather_scratch(copies)
+        side_sems + gather_scratch(copies) + gather_scratch(copies)
         + [pltpu.VMEM((copies, *own_sums.shape), F32), pltpu.VMEM((count, *own_sums.shape), F32), block,
            pltpu.SemaphoreType.DMA((2, copies)), pltpu.SemaphoreType.DMA((2, count))],
-        dense * up_bias.shape[0],
+        own_sums.size * (copies + count),
     )
     qkv_sum = qkv_sum.reshape(model_width, pairs_dev, PACK, head_size)[:, :, 0:5].astype(F32)
     late_sums = (*(part.astype(F32) for part in late_sums), out_sum.reshape(out_weight.shape).astype(F32))

time: 444 us -> 440 us (level)
  local copies, waits for them, and re-layouts: 22.2 us -> 15.2 us
  Pallas kernels: 327 us -> 333 us
    pallas_call x5 -> x6, Pallas kernels: 278 us -> 311 us  [call(): pl.pallas_call(kernel, out_shape=outputs, in_specs=[pl.BlockSpec(memory_s...]
    pallas_call x1 -> x0, Pallas kernels: 27.1 us -> none  [attend_backward(): pl.pallas_call(functools.partial(attend_backward_kernel, pairs), grid_spe...]
  transfers between devices with their start and end apart: 2 -> 2, of which waited for: 0 -> 0; matrix products, arithmetic and copies ran while one was open for 13% -> 11% of each run, Pallas kernels for 65% -> 67%
where the time goes in v3:
time: 440 us; the launch traced here: 431 us
  Pallas kernels  333 us (76%)
  matrix products  58.6 us (13%)
  local copies, waits for them, and re-layouts  15.2 us (3%)
  between operations  14.5 us (3%)
  other arithmetic  10.3 us (2%)
    pallas_call x6, Pallas kernels, call(): pl.pallas_call(kernel, out_shape=outputs, in_specs=[pl.BlockSpec(memory_s...  311 us
    dot_general x4, matrix products, rows_product(): lax.dot_general(left, right, (((0,), (0,)), ((), ())), preferred_element_...  21.2 us
    dot_general x2, matrix products, back_product(): lax.dot_general(left, weight, (((1,), (1,)), ((), ())), preferred_element...  21 us
    pallas_call x1, Pallas kernels, attend_forward(): pl.pallas_call(functools.partial(attend_forward_kernel, pairs), grid_spec...  17.3 us
    dot_general x2, matrix products, product(): return jnp.dot(left, right, preferred_element_type=F32)  16.4 us
  transfers between devices with their start and end apart: 2, of which 0 were waited for; matrix products, arithmetic and copies ran while one was open for 11% of the time, Pallas kernels for 67%

profile of v3, /device:TPU:16, one launch (start us, length us, event | category | flops | bytes accessed | tf_op | source)
XLA Modules:
  0.0 431.3 jit_solution(2201976980888158151)
XLA Ops:
  7.2 2.1 copy.37.first_ref
  9.4 42.3 %shard_map.280 = (bf16[4,512,1024]{2,1,0:T(8,128)(2,1)}, bf16[4,2048,128]{2,1,0:T(8,128)(2,1)}) custom-call(bf16[512,1024]{1,0:T(8,128)(2,1)} %x_ref.5, f32[1,1024]{1,0:T(1,128)} %bitcast.53, f32[1,1024]{1,0:T(1,128)} %bitcast.52, bf16[2048,128]{1,0:T(8,128)(2,1)} %copy.37.first_ref), custom_call_target="tpu_custom_call" | custom-call | flops 419430400 | bytes 7872512 | tf_op jit(solution)/shard_map/pallas_call | solution.py:845
  53.7 1.6 copy.39.weight
  55.3 7.4 %add_convert_fusion.qkv_ref = bf16[2048,768]{1,0:T(8,128)(2,1)} fusion(bf16[2048,1024]{1,0:T(8,128)(2,1)} %bitcast.63, bf16[1024,768]{0,1:T(8,128)(2,1)S(1)} %bitcast.47, f32[768]{0:T(1024)S(1)} %add.35), kind=kOutput, calls=%fused_computation.12 | convolution fusion | flops 3224371200 | bytes 8915968 | tf_op jit(solution)/shard_map/dot_general | solution.py:36
  62.7 17.3 %attend_forward.1 = (bf16[2048,256]{1,0:T(8,128)(2,1)}, f32[2048,256]{1,0:T(8,128)}) custom-call(s32[4]{0:T(128)} %lengths.3, s32[8]{0:T(128)} %owner.5, s32[1]{0:T(128)} %bitcast.5.place, bf16[2048,768]{1,0:T(8,128)(2,1)} %add_convert_fusion.qkv_ref, bf16[4,2048,128]{2,1,0:T(8,128)(2,1)} %get-tuple-element.41.first_ref), custom_call_target="tpu_custom_call" | custom-call | flops 4294967296 | bytes 8388608 | tf_op jit(solution)/shard_map/attend_forward/pallas_call | solution.py:231
  80.0 55.6 %shard_map.281 = (bf16[4,512,1024]{2,1,0:T(8,128)(2,1)}, f32[512,1024]{1,0:T(8,128)}) custom-call(bf16[2048,256]{1,0:T(8,128)(2,1)} %get-tuple-element.42.left, bf16[256,1024]{1,0:T(8,128)(2,1)} %bitcast.65, bf16[512,1024]{1,0:T(8,128)(2,1)} %x_ref.5, f32[1,1024]{1,0:T(1,128)} %bitcast.67, f32[1,1024]{1,0:T(1,128)} %bitcast.69, f32[1,1024]{1,0:T(1,128)} %bitcast.68), custom_call_target="tpu_custom_call" | custom-call | flops 1073741824 | bytes 8925184 | tf_op jit(solution)/shard_map/pallas_call | solution.py:845
  135.7 9.0 %fusion.8 = f32[2048,1024]{1,0:T(8,128)} fusion(bf16[2048,1024]{1,0:T(8,128)(2,1)} %bitcast.74, bf16[1024,1024]{1,0:T(8,128)(2,1)S(1)} %copy-done.10), kind=kOutput, calls=%fused_computation.25 | convolution fusion | flops 4294967296 | bytes 14680064 | tf_op jit(solution)/shard_map/dot_general | solution.py:36
  144.7 16.2 %convert_reduce_fusion = (f32[1024]{0:T(1024)S(1)}, bf16[2048,1024]{1,0:T(8,128)(2,1)S(1)}, bf16[2048,1024]{1,0:T(8,128)(2,1)S(1)}) fusion(f32[2048,1024]{1,0:T(8,128)} %fusion.8, f32[1024]{0:T(1024)S(1)} %copy-done.12, bf16[2048,1024]{1,0:T(8,128)(2,1)} %all-gather.2.cloned.1.call-done, bf16[1024,1024]{1,0:T(8,128)(2,1)} %weight.3), kind=kOutput, calls=%fused_computation.10 | convolution fusion | flops 4355783680 | bytes 23076864 | tf_op jit(solution)/shard_map/dot_general | solution.py:32
  160.9 5.9 %convolution_convert_fusion.2 = bf16[1024,1024]{1,0:T(8,128)(2,1)} fusion(bf16[2048,1024]{1,0:T(8,128)(2,1)S(1)} %bitcast.75, bf16[2048,1024]{1,0:T(8,128)(2,1)S(1)} %get-tuple-element.45.left), kind=kOutput, calls=%fused_computation.15 | convolution fusion | flops 4296015872 | bytes 10485760 | tf_op jit(solution)/shard_map/dot_general | solution.py:28
  166.8 5.8 %convolution_convert_fusion.1 = bf16[1024,1024]{1,0:T(8,128)(2,1)} fusion(bf16[2048,1024]{1,0:T(8,128)(2,1)S(1)} %get-tuple-element.99.left, bf16[2048,1024]{1,0:T(8,128)(2,1)S(1)} %copy-done.9), kind=kOutput, calls=%fused_computation.14 | convolution fusion | flops 4296015872 | bytes 10485760 | tf_op jit(solution)/shard_map/dot_general | solution.py:28
  172.6 60.3 %shard_map.282 = (bf16[4,512,1024]{2,1,0:T(8,128)(2,1)}, f32[512,1024]{1,0:T(8,128)}, f32[8,1024]{1,0:T(8,128)}) custom-call(bf16[2048,1024]{1,0:T(8,128)(2,1)} %copy-done.15, bf16[1024,1024]{1,0:T(8,128)(2,1)} %weight.2, f32[512,1024]{1,0:T(8,128)} %get-tuple-element.46.residual_ref, bf16[512,1024]{1,0:T(8,128)(2,1)} %dy_ref.1, f32[1,1024]{1,0:T(1,128)} %bitcast.70), custom_call_target="tpu_custom_call" | custom-call | flops 4294967296 | bytes 15765504 | tf_op jit(solution)/shard_map/pallas_call | solution.py:845
  232.9 4.8 %convolution_convert_fusion.grad_ref = bf16[2048,256]{1,0:T(8,128)(2,1)} fusion(bf16[2048,1024]{1,0:T(8,128)(2,1)} %bitcast.72, bf16[256,1024]{1,0:T(8,128)(2,1)S(1)} %bitcast.66), kind=kOutput, calls=%fused_computation.13 | convolution fusion | flops 1074266112 | bytes 5767168 | tf_op jit(solution)/shard_map/dot_general | solution.py:32
  237.7 47.9 %shard_map.283 = (bf16[2048,768]{1,0:T(8,128)(2,1)}, bf16[2048,128]{1,0:T(8,128)(2,1)}, f32[8,768]{1,0:T(8,128)}, bf16[512,1024]{1,0:T(8,128)(2,1)}) custom-call(s32[4]{0:T(128)} %lengths.3, s32[8]{0:T(128)} %owner.5, bf16[2048,768]{1,0:T(8,128)(2,1)} %add_convert_fusion.qkv_ref, bf16[4,2048,128]{2,1,0:T(8,128)(2,1)} %get-tuple-element.41.first_ref, ...), custom_call_target="tpu_custom_call" | custom-call | flops 10737418240 | bytes 21524528 | tf_op jit(solution)/shard_map/pallas_call | solution.py:845
  286.8 4.8 %convolution_convert_fusion.4 = bf16[256,1024]{1,0:T(8,128)(2,1)} fusion(bf16[2048,256]{1,0:T(8,128)(2,1)} %get-tuple-element.42.left, bf16[2048,1024]{1,0:T(8,128)(2,1)} %bitcast.73), kind=kOutput, calls=%fused_computation.18 | convolution fusion | flops 1074003968 | bytes 5767168 | tf_op jit(solution)/shard_map/dot_general | solution.py:28
  291.6 4.7 %convolution_convert_fusion.3 = bf16[1024,768]{1,0:T(8,128)(2,1)} fusion(bf16[2048,1024]{1,0:T(8,128)(2,1)S(1)} %bitcast.64, bf16[2048,768]{1,0:T(8,128)(2,1)S(1)} %copy-done.14), kind=kOutput, calls=%fused_computation.16 | convolution fusion | flops 3222011904 | bytes 8912896 | tf_op jit(solution)/shard_map/dot_general | solution.py:28
  296.3 54.6 %shard_map.284 = (bf16[512,1024]{1,0:T(8,128)(2,1)}, f32[8,1024]{1,0:T(8,128)}, bf16[128,768]{1,0:T(8,128)(2,1)}, bf16[32,1024]{1,0:T(8,128)(2,1)}) custom-call(bf16[2048,768]{1,0:T(8,128)(2,1)} %get-tuple-element.50.left, bf16[1024,768]{1,0:T(8,128)(2,1)} %copy.39.weight, bf16[512,1024]{1,0:T(8,128)(2,1)} %x_ref.5, f32[512,1024]{1,0:T(8,128)} %get-tuple-element.51.grad_ref, ...), custom_call_target="tpu_custom_call" | custom-call | flops 3221225472 | bytes 11309056 | tf_op jit(solution)/shard_map/pallas_call | solution.py:845
  352.3 49.8 %shard_map.285 = (f32[8,1024]{1,0:T(8,128)}, bf16[4,2048,128]{2,1,0:T(8,128)(2,1)}, bf16[4,2,128,768]{3,2,1,0:T(8,128)(2,1)}, bf16[4,2,32,1024]{3,2,1,0:T(8,128)(2,1)}) custom-call(f32[8,1024]{1,0:T(8,128)} %pad_maximum_fusion.small_ref, bf16[2048,128]{1,0:T(8,128)(2,1)} %get-tuple-element.56.skip_ref, bf16[128,768]{1,0:T(8,128)(2,1)} %get-tuple-element.57.qkv_slab, ...), custom_call_target="tpu_custom_call" | custom-call | flops 98304 | bytes 5046272 | tf_op jit(solution)/shard_map/pallas_call | solution.py:845
  402.2 4.6 %pick_gradient.1 = bf16[2048,128]{1,0:T(8,128)(2,1)} custom-call(s32[8]{0:T(128)} %owner.5, s32[1]{0:T(128)} %bitcast.5.place, bf16[4,2048,128]{2,1,0:T(8,128)(2,1)} %get-tuple-element.59.refs_0_.refs_1_, bf16[4,2048,128]{2,1,0:T(8,128)(2,1)} %get-tuple-element.59.refs_0_.refs_1_), custom_call_target="tpu_custom_call" | custom-call | tf_op jit(solution)/shard_map/pick_gradient/pallas_call | solution.py:830
  406.8 2.0 copy.40
  410.6 1.4 copy.41
  412.0 1.1 reshape.117
  413.8 1.8 slice_convert_fusion
  415.6 4.2 convert_element_type.58
  419.8 2.5 convert_element_type.59
  (66 shorter events, 8.9 us)
Async XLA Ops:
  7.2 46.3 %copy-start.2 = (bf16[1024,2,5,64]{0,3,2,1:T(8,128)(2,1)S(1)}, bf16[1024,2,5,64]{0,3,2,1:T(8,128)(2,1)}, u32[]{:S(2)}) copy-start(bf16[1024,2,5,64]{0,3,2,1:T(8,128)(2,1)} %param.24) | copy-start | bytes 3932164
  7.2 137.5 %all-gather.2.cloned.1.call-start = ((), (), s32[]{:S(2)}) async-start(), calls=%async_computation | async-start | bytes 5242880 | tf_op jit(solution)/shard_map/all_gather | solution.py:913
  51.7 363.9 %all-reduce.5.cloned.1.call-start = ((), (), s32[]{:S(2)}) async-start(), calls=%async_computation.1 | async-start | bytes 8388608 | tf_op jit(solution)/shard_map/psum | solution.py:936
  62.7 73.0 %copy-start.10 = (bf16[1024,1024]{1,0:T(8,128)(2,1)S(1)}, bf16[1024,1024]{1,0:T(8,128)(2,1)}, u32[]{:S(2)}) copy-start(bf16[1024,1024]{1,0:T(8,128)(2,1)} %weight.2) | copy-start | bytes 6291460
  135.7 9.0 %copy-start.12 = (f32[1024]{0:T(1024)S(1)}, f32[1024]{0:T(1024)}, u32[]{:S(2)}) copy-start(f32[1024]{0:T(1024)} %param.31) | copy-start | bytes 12292
  144.7 16.2 %copy-start.13 = (bf16[4,512,1024]{2,1,0:T(8,128)(2,1)S(1)}, bf16[4,512,1024]{2,1,0:T(8,128)(2,1)}, u32[]{:S(2)}) copy-start(bf16[4,512,1024]{2,1,0:T(8,128)(2,1)} %get-tuple-element.43) | copy-start | bytes 12582916
  160.8 5.9 %copy-start.15 = (bf16[2048,1024]{1,0:T(8,128)(2,1)}, bf16[2048,1024]{1,0:T(8,128)(2,1)S(1)}, u32[]{:S(2)}) copy-start(bf16[2048,1024]{1,0:T(8,128)(2,1)S(1)} %get-tuple-element.45.left) | copy-start | bytes 12582916
  160.8 5.9 %copy-start.16 = (bf16[2048,1024]{1,0:T(8,128)(2,1)}, bf16[2048,1024]{1,0:T(8,128)(2,1)S(1)}, u32[]{:S(2)}) copy-start(bf16[2048,1024]{1,0:T(8,128)(2,1)S(1)} %get-tuple-element.99.left) | copy-start | bytes 12582916
  160.9 5.9 %copy-start.9 = (bf16[2048,1024]{1,0:T(8,128)(2,1)S(1)}, bf16[2048,1024]{1,0:T(8,128)(2,1)}, u32[]{:S(2)}) copy-start(bf16[2048,1024]{1,0:T(8,128)(2,1)} %all-gather.2.cloned.1.call-done) | copy-start | bytes 12582916
  172.6 60.3 %copy-start.11 = (bf16[2,2,64,1024]{3,2,1,0:T(8,128)(2,1)S(1)}, bf16[2,2,64,1024]{3,2,1,0:T(8,128)(2,1)}, u32[]{:S(2)}) copy-start(bf16[2,2,64,1024]{3,2,1,0:T(8,128)(2,1)} %param.26) | copy-start | bytes 1572868
  285.7 5.9 %copy-start.14 = (bf16[2048,768]{1,0:T(8,128)(2,1)S(1)}, bf16[2048,768]{1,0:T(8,128)(2,1)}, u32[]{:S(2)}) copy-start(bf16[2048,768]{1,0:T(8,128)(2,1)} %get-tuple-element.50.left) | copy-start | bytes 9437188
  286.8 4.8 %copy-start.8 = (bf16[4,512,1024]{2,1,0:T(8,128)(2,1)S(1)}, bf16[4,512,1024]{2,1,0:T(8,128)(2,1)}, u32[]{:S(2)}) copy-start(bf16[4,512,1024]{2,1,0:T(8,128)(2,1)} %get-tuple-element.40) | copy-start | bytes 12582916
  296.3 55.4 %copy-start.7 = (f32[8,1024]{1,0:T(8,128)S(1)}, f32[8,1024]{1,0:T(8,128)}, u32[]{:S(2)}) copy-start(f32[8,1024]{1,0:T(8,128)} %get-tuple-element.53) | copy-start | bytes 98308
  402.1 6.7 %copy-start.6 = (f32[8,1024]{1,0:T(8,128)S(1)}, f32[8,1024]{1,0:T(8,128)}, u32[]{:S(2)}) copy-start(f32[8,1024]{1,0:T(8,128)} %get-tuple-element.60) | copy-start | bytes 98308
  402.2 7.4 %copy-start.5 = (bf16[4,2,32,1024]{3,2,1,0:T(8,128)(2,1)S(1)}, bf16[4,2,32,1024]{3,2,1,0:T(8,128)(2,1)}, u32[]{:S(2)}) copy-start(bf16[4,2,32,1024]{3,2,1,0:T(8,128)(2,1)} %get-tuple-element.62) | copy-start | bytes 1572868
  402.2 8.5 %copy-start.1 = (bf16[4,2,128,768]{3,2,1,0:T(8,128)(2,1)S(1)}, bf16[4,2,128,768]{3,2,1,0:T(8,128)(2,1)}, u32[]{:S(2)}) copy-start(bf16[4,2,128,768]{3,2,1,0:T(8,128)(2,1)} %get-tuple-element.61) | copy-start | bytes 4718596
  415.6 4.2 copy-start
  419.8 2.5 copy-start.3
  419.8 3.5 copy-start.4
Sparse Core Ops, SparseCore 0:
  51.9 35.2 all-gather.1
  172.7 169.2 all-reduce.4

commit v4 on v3

--- a/solution.py
+++ b/solution.py
@@ -317,6 +317,43 @@
             remote(got, got, self.far, (step - 1, index), self.across(step, False)).wait_recv()
             remote(got, got, self.passed, (step - 1, index), self.partner).start()
 
+    def consume(self, chunks, use):
+        far = self.count // 2 - 1
+        chip, core = lax.div(self.place, 2), lax.rem(self.place, 2)
+
+        def turn(number):
+            kind, index = lax.div(number, chunks), lax.rem(number, chunks)
+            step = lax.rem(kind + 2 * far - 2, max(far, 1)) + 1
+            owner = lax.rem(chip - step + self.count // 2, self.count // 2) * 2
+            owner = owner + jnp.where(kind < far + 2, core, 1 - core)
+            owner = jnp.where(kind == 0, self.place, jnp.where(kind == 1, self.partner, owner))
+            got = self.part(owner, index)
+
+            @pl.when(kind == 1)
+            def _():
+                remote(got, got, self.near, (index,), self.partner).wait_recv()
+
+            @pl.when((kind >= 2) & (kind < far + 2))
+            def _():
+                remote(got, got, self.far, (step - 1, index), self.across(step, False)).wait_recv()
+                remote(got, got, self.passed, (step - 1, index), self.partner).start()
+
+            @pl.when(kind >= far + 2)
+            def _():
+                remote(got, got, self.passed, (step - 1, index), self.partner).wait_recv()
+
+            use(owner, index)
+
+        each((2 * far + 2) * chunks, turn)
+
+    def sent(self, index):
+        own = self.part(self.place, index)
+        remote(own, own, self.near, (index,), self.partner).wait_send()
+        for step in range(1, self.count // 2):
+            remote(own, own, self.far, (step - 1, index), self.across(step, False)).wait_send()
+            got = self.part(self.across(-step, False), index)
+            remote(got, got, self.passed, (step - 1, index), self.partner).wait_send()
+
     def finish(self, index):
         own = self.part(self.place, index)
         near = self.part(self.partner, index)
@@ -616,7 +653,9 @@
     return jnp.sum(values, axis=0, keepdims=True)
 
 
-def open_kernel(count, chunk, x_ref, gain_ref, shift_ref, first_ref, rows_ref, all_ref, *sems):
+def open_kernel(
+    count, chunk, x_ref, gain_ref, shift_ref, first_ref, weight, bias_ref, rows_ref, all_ref, packed_ref, *sems
+):
     rows = x_ref.shape[0]
     place, _, _ = mesh_place(count)
     greet(count)
@@ -638,14 +677,21 @@
         side.send(index)
 
     each(2, side_start)
-    each(chunks, main.hand_on)
+
+    def use(owner, index):
+        got = rows_ref[owner, rows_at(index, chunk), :]
+        at = pl.ds(pl.multiple_of(owner * rows + index * chunk, chunk), chunk)
+        packed_ref[at, :] = (back_product(got, weight[...]) + bias_ref[...]).astype(BF16)
+
+    main.consume(chunks, use)
     each(2, side.hand_on)
-    each(chunks, main.finish)
+    each(chunks, main.sent)
     each(2, side.finish)
 
 
 def attend_out_kernel(
-    count, chunk, left, weight, x_ref, bias_ref, gain_ref, shift_ref, rows_ref, residual_ref, *scratch
+    count, chunk, left, weight, x_ref, bias_ref, gain_ref, shift_ref, up_ref, up_bias_ref,
+    rows_ref, residual_ref, pre_ref, hidden_ref, *scratch
 ):
     rows = x_ref.shape[0]
     place, _, _ = mesh_place(count)
@@ -664,13 +710,22 @@
         main.send(index)
 
     each(chunks, close)
-    each(chunks, main.hand_on)
-    each(chunks, main.finish)
+
+    def use(owner, index):
+        got = rows_ref[owner, rows_at(index, chunk), :]
+        at = pl.ds(pl.multiple_of(owner * rows + index * chunk, chunk), chunk)
+        pre = product(got, up_ref[...]) + up_bias_ref[...]
+        pre_ref[at, :] = pre
+        hidden_ref[at, :] = gelu_tanh(pre).astype(BF16)
+
+    main.consume(chunks, use)
+    each(chunks, main.sent)
     each(chunks, summed.finish)
 
 
 def mlp_back_kernel(
-    count, chunk, left, weight, residual_ref, dy_ref, gain_ref, rows_ref, grad_ref, sums_ref, *scratch
+    count, chunk, left, weight, residual_ref, dy_ref, gain_ref, out_weight_ref, mixed_ref,
+    grad_ref, sums_ref, mixed_grad_ref, weight_grad_ref, rows_ref, weight_sum, *scratch
 ):
     rows = residual_ref.shape[0]
     place, _, _ = mesh_place(count)
@@ -696,8 +751,17 @@
         sums_ref[3:4, :] += column_sum(dy)
 
     each(chunks, close)
-    each(chunks, main.hand_on)
-    each(chunks, main.finish)
+    weight_sum[...] = jnp.zeros_like(weight_sum)
+
+    def use(owner, index):
+        got = rows_ref[owner, rows_at(index, chunk), :]
+        at = pl.ds(pl.multiple_of(owner * rows + index * chunk, chunk), chunk)
+        mixed_grad_ref[at, :] = back_product(got, out_weight_ref[...]).astype(BF16)
+        weight_sum[...] += rows_product(mixed_ref[at, :], got)
+
+    main.consume(chunks, use)
+    weight_grad_ref[...] = weight_sum[...].astype(BF16)
+    each(chunks, main.sent)
     each(chunks, summed.finish)
 
 
@@ -708,7 +772,7 @@
     rows = x_ref.shape[0]
     greet(count, copies)
     chunks = rows // chunk
-    summed = RowSum(count, rows, chunk, left, weight, True, scratch[:10])
+    summed = RowSum(count, rows, chunk, left, weight, False, scratch[:10])
     outw = DpReduce(copies, outw_ref, *scratch[10:15])
     qkv = DpReduce(copies, qkv_ref, *scratch[15:20])
     qkv.send()
@@ -732,8 +796,8 @@
 
 
 def closing_kernel(
-    count, copies, shared, small_ref, skip_ref, qkv_slab, outw_slab,
-    small_out, all_ref, qkv_ref, outw_ref, *scratch
+    count, copies, shared, pairs, owner, small_ref, skip_ref, qkv_slab, outw_slab,
+    small_out, first_ref, qkv_ref, outw_ref, all_ref, *scratch
 ):
     copy, place = lax.axis_index("dp"), lax.axis_index("mp")
     barrier = pltpu.get_barrier_semaphore()
@@ -778,66 +842,42 @@
     small_start(*over_copies)
     qkv.send()
     outw.send()
+    part_out[...] = small_total(*over_copies)
+    small_start(*over_parts)
 
     def side_start(index):
         all_ref[place, rows_at(index, side_chunk), :] = skip_ref[rows_at(index, side_chunk), :]
         side.send(index)
 
     each(2, side_start)
-    part_out[...] = small_total(*over_copies)
-    small_start(*over_parts)
+
+    def pass_on(index):
+        qkv.pass_on(index)
+        outw.pass_on(index)
+
+    each(qkv.at.outer, pass_on)
+    each(2, side.hand_on)
     every = small_total(*over_parts)
     row = lax.broadcasted_iota(jnp.int32, every.shape, 0)
     small_out[...] = jnp.where(row < shared, every, part_out[...])
-
-    def pass_on(index):
-        qkv.pass_on(index)
-        outw.pass_on(index)
-
-    each(qkv.at.outer, pass_on)
-    each(2, side.hand_on)
+    each(2, side.finish)
+    width = skip_ref.shape[1] // pairs
+    for slot in range(pairs):
+        user = user_of(owner, place * pairs + slot)
+        held = all_ref[lax.div(user, pairs)]
+        value = held[:, 0:width]
+        for part in range(1, pairs):
+            value = jnp.where(lax.rem(user, pairs) == part, held[:, part * width : (part + 1) * width], value)
+        first_ref[:, slot * width : (slot + 1) * width] = value
     outw.finish()
     qkv.finish()
-    each(2, side.finish)
 
 
 def user_of(owner, head):
     user = jnp.int32(0)
     for pair in range(owner.shape[0]):
-        user = user + jnp.where(owner[pair] == head, pair, 0)
+        user = jnp.maximum(user, jnp.where(owner[pair] == head, pair, 0))
     return user
-
-
-def pick_gradient(owner, place, every, pairs):
-    _, rows, slim = every.shape
-    width = slim // pairs
-
-    def kernel(owner, place, *refs):
-        for slot in range(pairs):
-            held = refs[slot][0]
-            user = lax.rem(user_of(owner, place[0] * pairs + slot), pairs)
-            value = held[:, 0:width]
-            for part in range(1, pairs):
-                value = jnp.where(user == part, held[:, part * width : (part + 1) * width], value)
-            refs[-1][:, slot * width : (slot + 1) * width] = value
-
-    def block(slot):
-        return pl.BlockSpec(
-            (1, rows // 4, slim),
-            lambda g, o, m: (lax.div(user_of(o, m[0] * pairs + slot), pairs), g, 0),
-        )
-
-    return pl.pallas_call(
-        kernel,
-        grid_spec=pltpu.PrefetchScalarGridSpec(
-            num_scalar_prefetch=2,
-            grid=(4,),
-            in_specs=[block(slot) for slot in range(pairs)],
-            out_specs=pl.BlockSpec((rows // 4, slim), lambda g, o, m: (g, 0)),
-        ),
-        out_shape=jax.ShapeDtypeStruct((rows, slim), BF16),
-        name="pick_gradient",
-    )(owner, place, *([every] * pairs))
 
 
 def call(kernel, number, inputs, outputs, scratch, flops, scalars=0):
@@ -883,8 +923,8 @@
     seats = (seq_lengths, value_owner, lax.axis_index("mp").reshape(1).astype(jnp.int32))
     copies = lax.axis_size("dp")
 
-    qkv_pack = jnp.pad(qkv_weight, ((0, 0), (0, 0), (0, 1), (0, 0)))
-    qkv_pack = qkv_pack.reshape(model_width, pairs_dev * PACK * head_size)
+    qkv_pack = jnp.pad(jnp.transpose(qkv_weight, (1, 2, 3, 0)), ((0, 0), (0, 1), (0, 0), (0, 0)))
+    qkv_pack = qkv_pack.reshape(pairs_dev * PACK * head_size, model_width)
     bias_pack = jnp.concatenate(
         [qv_bias[:, 0:2], jnp.zeros_like(qv_bias[:, 0:2]), qv_bias[:, 2:3], jnp.zeros_like(qv_bias[:, 2:3])],
         axis=1,
@@ -901,26 +941,27 @@
     main_sems, side_sems = gather_sems(count, chunks), gather_sems(count, 2)
     dense = 2 * group_rows * model_width
 
-    rows_one, all_first = call(
+    packs = pairs_dev * PACK * head_size
+    rows_one, all_first, packed = call(
         functools.partial(open_kernel, count, chunk), 0,
-        (inputs, attn_norm_gain.reshape(row), attn_norm_bias.reshape(row), first_values.reshape(group_rows, slim)),
-        [like(whole, BF16), like((count, group_rows, slim), BF16)],
-        main_sems + side_sems, dense * 100,
+        (inputs, attn_norm_gain.reshape(row), attn_norm_bias.reshape(row), first_values.reshape(group_rows, slim),
+         qkv_pack, bias_pack),
+        [like(whole, BF16), like((count, group_rows, slim), BF16), like((group_rows, packs), BF16)],
+        main_sems + side_sems, dense * packs,
     )
     rows_one = rows_one.reshape(group_rows, model_width)
-    packed = (product(rows_one, qkv_pack) + bias_pack).astype(BF16)
     cotangent_late = lax.optimization_barrier((cotangent, rows_one))[0]
     grad_rows = lax.all_gather(cotangent_late, "mp", axis=0, tiled=True)
     mixed, totals = attend_forward(*seats, packed, all_first)
-    rows_two, residual = call(
+    units = up_bias.shape[0]
+    rows_two, residual, hidden_pre, hidden = call(
         functools.partial(attend_out_kernel, count, chunk), 1,
-        (mixed, out_flat, inputs, out_bias.reshape(row), mlp_norm_gain.reshape(row), mlp_norm_bias.reshape(row)),
-        [like(whole, BF16), like(inputs.shape, F32)],
-        sum_scratch + main_sems, dense * 256,
+        (mixed, out_flat, inputs, out_bias.reshape(row), mlp_norm_gain.reshape(row), mlp_norm_bias.reshape(row),
+         up_weight, up_bias.reshape(1, units)),
+        [like(whole, BF16), like(inputs.shape, F32), like((group_rows, units), F32), like((group_rows, units), BF16)],
+        sum_scratch + main_sems, dense * (256 + units),
     )
     rows_two = rows_two.reshape(group_rows, model_width)
-    hidden_pre = product(rows_two, up_weight) + up_bias
-    hidden = gelu_tanh(hidden_pre).astype(BF16)
     grad_hidden = back_product(grad_rows, down_weight)
     grad_pre = jax.vjp(gelu_tanh, hidden_pre)[1](grad_hidden)[0].astype(BF16)
     grad_down_weight = rows_product(hidden, grad_rows).astype(BF16)
@@ -934,16 +975,13 @@
     late = (grad_up_weight, grad_down_weight)
     grad_pre, late = lax.optimization_barrier((grad_pre, late))
     late_sums = lax.psum(late, "dp")
-    resid_rows, grad_residual, sums_two = call(
+    grad_residual, sums_two, grad_mixed, grad_out_weight = call(
         functools.partial(mlp_back_kernel, count, chunk), 2,
-        (grad_pre, up_weight, residual, cotangent, mlp_norm_gain.reshape(row)),
-        [like(whole, BF16), like(inputs.shape, F32), like((8, model_width), F32)],
-        sum_scratch + main_sems, dense * up_bias.shape[0],
+        (grad_pre, up_weight, residual, cotangent, mlp_norm_gain.reshape(row), out_flat, mixed),
+        [like(inputs.shape, F32), like((8, model_width), F32), like(mixed.shape, BF16), like(out_flat.shape, BF16)],
+        [pltpu.VMEM(whole, BF16), pltpu.VMEM(out_flat.shape, F32)] + sum_scratch + main_sems,
+        dense * up_bias.shape[0],
     )
-    resid_rows = resid_rows.reshape(group_rows, model_width)
-    grad_mixed = back_product(resid_rows, out_flat).astype(BF16)
-    grad_out_weight = rows_product(mixed, resid_rows).astype(BF16)
-    packs = pairs_dev * PACK * head_size
     grad_flat, grad_skip, pack_sums, output = call(
         functools.partial(attend_backward_kernel, count, chunk, pairs_dev), 5,
         (seq_lengths, value_owner, packed, all_first, grad_mixed, totals, hidden, down_weight, residual,
@@ -956,7 +994,9 @@
     )
     pack_sums = pack_sums[0].reshape(pairs_dev, PACK, head_size)
     grad_qv_bias = jnp.concatenate([pack_sums[:, 0:2], pack_sums[:, 4:5]], axis=1)
-    grad_qkv_weight = sliced(rows_product(rows_one, grad_flat).astype(BF16))
+    grad_qkv_weight = rows_product(grad_flat, rows_one).astype(BF16)
+    grad_qkv_weight = grad_qkv_weight.reshape(pairs_dev, PACK, head_size, model_width)[:, 0:5]
+    grad_qkv_weight = sliced(grad_qkv_weight.reshape(pairs_dev * 5 * head_size, model_width))
     grad_out_weight = sliced(grad_out_weight)
     grad_inputs, sums_one, qkv_slab, out_slab = call(
         functools.partial(input_back_kernel, count, copies, chunk), 3,
@@ -970,19 +1010,21 @@
     slim_bias = jnp.pad(grad_qv_bias.reshape(-1), (0, model_width - grad_qv_bias.size)).reshape(row)
     own_sums = jnp.concatenate([sums_two[0:4], sums_one[0:2], wide_bias, slim_bias], axis=0)
     block = pltpu.VMEM(own_sums.shape, F32)
-    small, every_skip, qkv_sum, out_sum = call(
-        functools.partial(closing_kernel, count, copies, 6), 4,
-        (own_sums, grad_skip, qkv_slab, out_slab),
-        [like(own_sums.shape, F32), like((count, group_rows, slim), BF16),
+    small, grad_first, qkv_sum, out_sum = call(
+        functools.partial(closing_kernel, count, copies, 6, pairs_dev), 4,
+        (value_owner, own_sums, grad_skip, qkv_slab, out_slab),
+        [like(own_sums.shape, F32), like((group_rows, slim), BF16),
          like(grad_qkv_weight.shape, BF16), like(grad_out_weight.shape, BF16)],
-        side_sems + gather_scratch(copies) + gather_scratch(copies)
+        [pltpu.VMEM((count, group_rows, slim), BF16)]
+        + side_sems + gather_scratch(copies) + gather_scratch(copies)
         + [pltpu.VMEM((copies, *own_sums.shape), F32), pltpu.VMEM((count, *own_sums.shape), F32), block,
            pltpu.SemaphoreType.DMA((2, copies)), pltpu.SemaphoreType.DMA((2, count))],
-        own_sums.size * (copies + count),
+        own_sums.size * (copies + count), scalars=1,
     )
-    qkv_sum = qkv_sum.reshape(model_width, pairs_dev, PACK, head_size)[:, :, 0:5].astype(F32)
+    qkv_sum = qkv_sum.reshape(pairs_dev, 5, head_size, model_width).astype(F32)
+    qkv_sum = jnp.transpose(qkv_sum, (3, 0, 1, 2))
     late_sums = (*(part.astype(F32) for part in late_sums), out_sum.reshape(out_weight.shape).astype(F32))
-    grad_first = pick_gradient(*seats[1:], every_skip, pairs_dev).reshape(group_rows, pairs_dev, head_size)
+    grad_first = grad_first.reshape(group_rows, pairs_dev, head_size)
     norm_sums = (small[4], small[5], small[2], small[0], small[1], small[3])
     bias_sums = (small[7, : grad_qv_bias.size].reshape(qv_bias.shape), small[6, : grad_up_bias.shape[0]])
 

time: 440 us -> 419 us (0.952)
  the two profiles are of different devices: /device:TPU:16 before, /device:TPU:0 now
where the time goes in v4:
time: 419 us; the launch traced here: 415 us
  Pallas kernels  339 us (81%)
  matrix products  32.3 us (8%)
  local copies, waits for them, and re-layouts  17 us (4%)
  between operations  14.2 us (3%)
  other arithmetic  12.7 us (3%)
    pallas_call x6, Pallas kernels, call(): pl.pallas_call(kernel, out_shape=outputs, in_specs=[pl.BlockSpec(memory_s...  322 us
    dot_general x3, matrix products, rows_product(): lax.dot_general(left, right, (((0,), (0,)), ((), ())), preferred_element_...  18.7 us
    pallas_call x1, Pallas kernels, attend_forward(): pl.pallas_call(functools.partial(attend_forward_kernel, pairs), grid_spec...  17.2 us
    dot_general x1, matrix products, back_product(): lax.dot_general(left, weight, (((1,), (1,)), ((), ())), preferred_element...  13.6 us
  transfers between devices with their start and end apart: 2, of which 0 were waited for; matrix products, arithmetic and copies ran while one was open for 5% of the time, Pallas kernels for 71%

profile of v4, /device:TPU:0, one launch (start us, length us, event | category | flops | bytes accessed | tf_op | source)
XLA Modules:
  0.0 415.2 jit_solution(4180717850842542464)
XLA Ops:
  9.5 2.0 copy.37.first_ref
  11.5 2.7 pad.8
  14.2 45.4 %shard_map.280 = (bf16[4,512,1024]{2,1,0:T(8,128)(2,1)}, bf16[4,2048,128]{2,1,0:T(8,128)(2,1)}, bf16[2048,768]{1,0:T(8,128)(2,1)}) custom-call(bf16[512,1024]{1,0:T(8,128)(2,1)} %x_ref.5, f32[1,1024]{1,0:T(1,128)} %bitcast.69, f32[1,1024]{1,0:T(1,128)} %bitcast.62, bf16[2048,128]{1,0:T(8,128)(2,1)} %copy.37.first_ref, bf16[768,1024]{1,0:T(8,128)(2,1)} %bitcast.42, ...), custom_call_target="tpu_custom_call" | custom-call | flops 3221225472 | bytes 12594176 | tf_op jit(solution)/shard_map/pallas_call | solution.py:885
  59.7 17.2 %attend_forward.1 = (bf16[2048,256]{1,0:T(8,128)(2,1)}, f32[2048,256]{1,0:T(8,128)}) custom-call(s32[4]{0:T(128)} %lengths.3, s32[8]{0:T(128)} %owner.5, s32[1]{0:T(128)} %bitcast.5.place, bf16[2048,768]{1,0:T(8,128)(2,1)} %get-tuple-element.44.qkv_ref, bf16[4,2048,128]{2,1,0:T(8,128)(2,1)} %get-tuple-element.45.first_ref), custom_call_target="tpu_custom_call" | custom-call | flops 4294967296 | bytes 8388608 | tf_op jit(solution)/shard_map/attend_forward/pallas_call | solution.py:231
  76.9 71.0 %shard_map.281 = (bf16[4,512,1024]{2,1,0:T(8,128)(2,1)}, f32[512,1024]{1,0:T(8,128)}, f32[2048,1024]{1,0:T(8,128)}, bf16[2048,1024]{1,0:T(8,128)(2,1)}) custom-call(bf16[2048,256]{1,0:T(8,128)(2,1)} %get-tuple-element.46.left.mixed_ref, bf16[256,1024]{1,0:T(8,128)(2,1)} %bitcast.60, bf16[512,1024]{1,0:T(8,128)(2,1)} %x_ref.5, f32[1,1024]{1,0:T(1,128)} %bitcast.63, ...), custom_call_target="tpu_custom_call" | custom-call | flops 5368709120 | bytes 23609344 | tf_op jit(solution)/shard_map/pallas_call | solution.py:885
  147.9 13.6 %convert_reduce_fusion = (f32[1024]{0:T(1024)S(1)}, bf16[2048,1024]{1,0:T(8,128)(2,1)S(1)}) fusion(f32[2048,1024]{1,0:T(8,128)} %get-tuple-element.47, bf16[2048,1024]{1,0:T(8,128)(2,1)} %all-gather.2.cloned.1.call-done, bf16[1024,1024]{1,0:T(8,128)(2,1)S(1)} %copy-done.5), kind=kOutput, calls=%fused_computation.10 | convolution fusion | flops 4349492224 | bytes 18878464 | tf_op jit(solution)/shard_map/dot_general | solution.py:32
  161.6 5.8 %convolution_convert_fusion.1 = bf16[1024,1024]{1,0:T(8,128)(2,1)} fusion(bf16[2048,1024]{1,0:T(8,128)(2,1)S(1)} %bitcast.72, bf16[2048,1024]{1,0:T(8,128)(2,1)S(1)} %get-tuple-element.52.left), kind=kOutput, calls=%fused_computation.13 | convolution fusion | flops 4296015872 | bytes 10485760 | tf_op jit(solution)/shard_map/dot_general | solution.py:28
  167.3 6.0 %convolution_convert_fusion = bf16[1024,1024]{1,0:T(8,128)(2,1)} fusion(bf16[2048,1024]{1,0:T(8,128)(2,1)S(1)} %copy-done.8, bf16[2048,1024]{1,0:T(8,128)(2,1)S(1)} %copy-done.4), kind=kOutput, calls=%fused_computation.12 | convolution fusion | flops 4296015872 | bytes 10485760 | tf_op jit(solution)/shard_map/dot_general | solution.py:28
  173.4 60.7 %shard_map.282 = (f32[512,1024]{1,0:T(8,128)}, f32[8,1024]{1,0:T(8,128)}, bf16[2048,256]{1,0:T(8,128)(2,1)}, bf16[256,1024]{1,0:T(8,128)(2,1)}) custom-call(bf16[2048,1024]{1,0:T(8,128)(2,1)} %copy-done.7, bf16[1024,1024]{1,0:T(8,128)(2,1)} %weight.2, f32[512,1024]{1,0:T(8,128)} %get-tuple-element.53.residual_ref, bf16[512,1024]{1,0:T(8,128)(2,1)} %dy_ref.1, ...), custom_call_target="tpu_custom_call" | custom-call | flops 4294967296 | bytes 14716928 | tf_op jit(solution)/shard_map/pallas_call | solution.py:885
  234.1 47.3 %shard_map.283 = (bf16[2048,768]{1,0:T(8,128)(2,1)}, bf16[2048,128]{1,0:T(8,128)(2,1)}, f32[8,768]{1,0:T(8,128)}, bf16[512,1024]{1,0:T(8,128)(2,1)}) custom-call(s32[4]{0:T(128)} %lengths.3, s32[8]{0:T(128)} %owner.5, bf16[2048,768]{1,0:T(8,128)(2,1)} %get-tuple-element.44.qkv_ref, bf16[4,2048,128]{2,1,0:T(8,128)(2,1)} %get-tuple-element.45.first_ref, ...), custom_call_target="tpu_custom_call" | custom-call | flops 10737418240 | bytes 21524528 | tf_op jit(solution)/shard_map/pallas_call | solution.py:885
  281.4 0.8 slice_reduce_fusion
  282.3 6.9 %convolution_convert_fusion.2 = bf16[768,1024]{1,0:T(8,128)(2,1)S(1)} fusion(bf16[2048,768]{1,0:T(8,128)(2,1)} %get-tuple-element.57.left, bf16[2048,1024]{1,0:T(8,128)(2,1)} %bitcast.71), kind=kOutput, calls=%fused_computation.14 | convolution fusion | flops 3222011904 | bytes 8912896 | tf_op jit(solution)/shard_map/dot_general | solution.py:28
  289.2 1.2 slice.64
  290.5 51.3 %shard_map.284 = (bf16[512,1024]{1,0:T(8,128)(2,1)}, f32[8,1024]{1,0:T(8,128)}, bf16[80,1024]{1,0:T(8,128)(2,1)}, bf16[32,1024]{1,0:T(8,128)(2,1)}) custom-call(bf16[2048,768]{1,0:T(8,128)(2,1)} %get-tuple-element.57.left, bf16[768,1024]{1,0:T(8,128)(2,1)} %bitcast.43, bf16[512,1024]{1,0:T(8,128)(2,1)} %x_ref.5, f32[512,1024]{1,0:T(8,128)} %get-tuple-element.58.grad_ref, ...), custom_call_target="tpu_custom_call" | custom-call | flops 3221225472 | bytes 11014144 | tf_op jit(solution)/shard_map/pallas_call | solution.py:885
  341.8 0.8 slice.52
  343.2 46.0 %shard_map.285 = (f32[8,1024]{1,0:T(8,128)}, bf16[2048,128]{1,0:T(8,128)(2,1)}, bf16[4,2,80,1024]{3,2,1,0:T(8,128)(2,1)}, bf16[4,2,32,1024]{3,2,1,0:T(8,128)(2,1)}) custom-call(s32[8]{0:T(128)} %owner.5, f32[8,1024]{1,0:T(8,128)} %pad_maximum_fusion.small_ref, bf16[2048,128]{1,0:T(8,128)(2,1)} %get-tuple-element.64.skip_ref, ...), custom_call_target="tpu_custom_call" | custom-call | flops 98304 | bytes 3178528 | tf_op jit(solution)/shard_map/pallas_call | solution.py:885
  389.2 2.0 copy.38
  392.7 2.1 convert.4
  394.8 1.8 fusion.7
  396.6 3.1 convert_bitcast_fusion
  399.7 4.2 %convert_element_type.43 = f32[1024,1024]{1,0:T(8,128)} convert(bf16[1024,1024]{1,0:T(8,128)(2,1)} %get-tuple-element.103) | non-fusion elementwise | flops 1048576 | bytes 6291456 | tf_op jit(solution)/shard_map/convert_element_type | solution.py:1026
  403.9 2.5 convert_element_type.44
  406.4 1.0 copy.44
  407.4 1.0 copy.45
  (43 shorter events, 4.6 us)
Async XLA Ops:
  7.2 140.7 %all-gather.2.cloned.1.call-start = ((), (), s32[]{:S(2)}) async-start(), calls=%async_computation | async-start | bytes 5242880 | tf_op jit(solution)/shard_map/all_gather | solution.py:954
  59.6 340.1 %all-reduce.5.cloned.1.call-start = ((), (), s32[]{:S(2)}) async-start(), calls=%async_computation.1 | async-start | bytes 8388608 | tf_op jit(solution)/shard_map/psum | solution.py:977
  76.9 71.0 %copy-start.5 = (bf16[1024,1024]{1,0:T(8,128)(2,1)S(1)}, bf16[1024,1024]{1,0:T(8,128)(2,1)}, u32[]{:S(2)}) copy-start(bf16[1024,1024]{1,0:T(8,128)(2,1)} %weight.3) | copy-start | bytes 6291460
  147.9 13.6 %copy-start.6 = (bf16[4,512,1024]{2,1,0:T(8,128)(2,1)S(1)}, bf16[4,512,1024]{2,1,0:T(8,128)(2,1)}, u32[]{:S(2)}) copy-start(bf16[4,512,1024]{2,1,0:T(8,128)(2,1)} %get-tuple-element.50) | copy-start | bytes 12582916
  161.5 5.8 %copy-start.7 = (bf16[2048,1024]{1,0:T(8,128)(2,1)}, bf16[2048,1024]{1,0:T(8,128)(2,1)S(1)}, u32[]{:S(2)}) copy-start(bf16[2048,1024]{1,0:T(8,128)(2,1)S(1)} %get-tuple-element.52.left) | copy-start | bytes 12582916
  161.5 5.8 %copy-start.4 = (bf16[2048,1024]{1,0:T(8,128)(2,1)S(1)}, bf16[2048,1024]{1,0:T(8,128)(2,1)}, u32[]{:S(2)}) copy-start(bf16[2048,1024]{1,0:T(8,128)(2,1)} %all-gather.2.cloned.1.call-done) | copy-start | bytes 12582916
  161.6 5.8 %copy-start.8 = (bf16[2048,1024]{1,0:T(8,128)(2,1)S(1)}, bf16[2048,1024]{1,0:T(8,128)(2,1)}, u32[]{:S(2)}) copy-start(bf16[2048,1024]{1,0:T(8,128)(2,1)} %get-tuple-element.51.left) | copy-start | bytes 12582916
  290.5 52.1 %copy-start.3 = (f32[8,1024]{1,0:T(8,128)S(1)}, f32[8,1024]{1,0:T(8,128)}, u32[]{:S(2)}) copy-start(f32[8,1024]{1,0:T(8,128)} %get-tuple-element.61) | copy-start | bytes 98308
  399.7 4.2 %copy-start = (bf16[1024,1024]{1,0:T(8,128)(2,1)S(1)}, bf16[1024,1024]{1,0:T(8,128)(2,1)}, u32[]{:S(2)}) copy-start(bf16[1024,1024]{1,0:T(8,128)(2,1)} %get-tuple-element.104) | copy-start | bytes 6291460
  403.9 2.5 copy-start.1
  403.9 3.5 copy-start.2
Sparse Core Ops, SparseCore 0:
  59.7 44.6 all-gather.1
  173.5 174.2 all-reduce.4

commit v5 on v4

--- a/solution.py
+++ b/solution.py
@@ -654,7 +654,7 @@
 
 
 def open_kernel(
-    count, chunk, x_ref, gain_ref, shift_ref, first_ref, weight, bias_ref, rows_ref, all_ref, packed_ref, *sems
+    count, chunk, x_ref, gain_ref, shift_ref, first_ref, weight, bias_ref, rows_ref, all_ref, packed_ref, pack_ref, *sems
 ):
     rows = x_ref.shape[0]
     place, _, _ = mesh_place(count)
@@ -678,10 +678,16 @@
 
     each(2, side_start)
 
+    held = weight.shape[1]
+    span = pack_ref.shape[0] // weight.shape[0]
+    for pair in range(weight.shape[0]):
+        pack_ref[pair * span : pair * span + held, :] = weight[pair]
+        pack_ref[pair * span + held : (pair + 1) * span, :] = jnp.zeros((span - held, weight.shape[2]), BF16)
+
     def use(owner, index):
         got = rows_ref[owner, rows_at(index, chunk), :]
         at = pl.ds(pl.multiple_of(owner * rows + index * chunk, chunk), chunk)
-        packed_ref[at, :] = (back_product(got, weight[...]) + bias_ref[...]).astype(BF16)
+        packed_ref[at, :] = (back_product(got, pack_ref[...]) + bias_ref[...]).astype(BF16)
 
     main.consume(chunks, use)
     each(2, side.hand_on)
@@ -766,38 +772,8 @@
 
 
 def input_back_kernel(
-    count, copies, chunk, left, weight, x_ref, grad_ref, gain_ref, qkv_ref, outw_ref,
-    out_ref, sums_ref, qkv_slab, outw_slab, *scratch
-):
-    rows = x_ref.shape[0]
-    greet(count, copies)
-    chunks = rows // chunk
-    summed = RowSum(count, rows, chunk, left, weight, False, scratch[:10])
-    outw = DpReduce(copies, outw_ref, *scratch[10:15])
-    qkv = DpReduce(copies, qkv_ref, *scratch[15:20])
-    qkv.send()
-    outw.send()
-    sums_ref[...] = jnp.zeros_like(sums_ref)
-    summed.send()
-
-    def close(index):
-        at = rows_at(index, chunk)
-        total = summed.total(index)
-        back, per_gain = norm_backward(x_ref[at, :].astype(F32), total, gain_ref[...])
-        out_ref[at, :] = (grad_ref[at, :] + back).astype(BF16)
-        sums_ref[0:1, :] += column_sum(per_gain)
-        sums_ref[1:2, :] += column_sum(total)
-        spread(index, chunks, copies, [qkv.pass_on, outw.pass_on])
-
-    each(chunks, close)
-    qkv_slab[...] = qkv.total().astype(BF16)
-    outw_slab[...] = outw.total().astype(BF16)
-    each(chunks, summed.finish)
-
-
-def closing_kernel(
-    count, copies, shared, pairs, owner, small_ref, skip_ref, qkv_slab, outw_slab,
-    small_out, first_ref, qkv_ref, outw_ref, all_ref, *scratch
+    count, copies, chunk, shared, pairs, owner, left, weight, x_ref, grad_ref, gain_ref, small_ref, skip_ref,
+    qkv_ref, outw_ref, out_ref, small_out, first_ref, qkv_all, outw_all, *scratch
 ):
     copy, place = lax.axis_index("dp"), lax.axis_index("mp")
     barrier = pltpu.get_barrier_semaphore()
@@ -810,11 +786,17 @@
             barrier, inc=1, device_id={"mp": lax.rem(place + step, count)}, device_id_type=pl.DeviceIdType.MESH
         )
     pl.semaphore_wait(barrier, copies + count - 2)
+    rows = x_ref.shape[0]
+    chunks = rows // chunk
+    summed = RowSum(count, rows, chunk, left, weight, False, scratch[:10])
+    outw = DpReduce(copies, outw_ref, *scratch[10:15])
+    qkv = DpReduce(copies, qkv_ref, *scratch[15:20])
+    all_ref, qkv_slab, outw_slab, own_small = scratch[20:24]
     side_chunk = skip_ref.shape[0] // 2
-    side = Gather(count, all_ref, side_chunk, *scratch[0:3])
-    qkv = DpGather(copies, qkv_slab, qkv_ref, *scratch[3:5])
-    outw = DpGather(copies, outw_slab, outw_ref, *scratch[5:7])
-    copy_in, part_in, part_out, copy_sems, part_sems = scratch[7:]
+    side = Gather(count, all_ref, side_chunk, *scratch[24:27])
+    qkv_back = DpGather(copies, qkv_slab, qkv_all, *scratch[27:29])
+    outw_back = DpGather(copies, outw_slab, outw_all, *scratch[29:31])
+    copy_in, part_in, part_out, copy_sems, part_sems = scratch[31:]
 
     def small_copy(axis, own, size, source, slots, sems, step, slot):
         return pltpu.make_async_remote_copy(
@@ -837,13 +819,12 @@
             total = total + slots[slot]
         return total
 
-    over_copies = ("dp", copy, copies, small_ref, copy_in, copy_sems)
+    over_copies = ("dp", copy, copies, own_small, copy_in, copy_sems)
     over_parts = ("mp", place, count, part_out, part_in, part_sems)
-    small_start(*over_copies)
     qkv.send()
     outw.send()
-    part_out[...] = small_total(*over_copies)
-    small_start(*over_parts)
+    own_small[...] = small_ref[...]
+    summed.send()
 
     def side_start(index):
         all_ref[place, rows_at(index, side_chunk), :] = skip_ref[rows_at(index, side_chunk), :]
@@ -851,15 +832,30 @@
 
     each(2, side_start)
 
+    def close(index):
+        at = rows_at(index, chunk)
+        total = summed.total(index)
+        back, per_gain = norm_backward(x_ref[at, :].astype(F32), total, gain_ref[...])
+        out_ref[at, :] = (grad_ref[at, :] + back).astype(BF16)
+        own_small[4:5, :] += column_sum(per_gain)
+        own_small[5:6, :] += column_sum(total)
+        spread(index, chunks, copies, [qkv.pass_on, outw.pass_on])
+
+    each(chunks, close)
+    small_start(*over_copies)
+    qkv_slab[...] = qkv.total().astype(BF16)
+    qkv_back.send()
+    outw_slab[...] = outw.total().astype(BF16)
+    outw_back.send()
+    each(2, side.hand_on)
+    part_out[...] = small_total(*over_copies)
+    small_start(*over_parts)
+
     def pass_on(index):
-        qkv.pass_on(index)
-        outw.pass_on(index)
+        qkv_back.pass_on(index)
+        outw_back.pass_on(index)
 
     each(qkv.at.outer, pass_on)
-    each(2, side.hand_on)
-    every = small_total(*over_parts)
-    row = lax.broadcasted_iota(jnp.int32, every.shape, 0)
-    small_out[...] = jnp.where(row < shared, every, part_out[...])
     each(2, side.finish)
     width = skip_ref.shape[1] // pairs
     for slot in range(pairs):
@@ -869,8 +865,12 @@
         for part in range(1, pairs):
             value = jnp.where(lax.rem(user, pairs) == part, held[:, part * width : (part + 1) * width], value)
         first_ref[:, slot * width : (slot + 1) * width] = value
-    outw.finish()
-    qkv.finish()
+    every = small_total(*over_parts)
+    row = lax.broadcasted_iota(jnp.int32, every.shape, 0)
+    small_out[...] = jnp.where(row < shared, every, part_out[...])
+    each(chunks, summed.finish)
+    outw_back.finish()
+    qkv_back.finish()
 
 
 def user_of(owner, head):
@@ -923,8 +923,7 @@
     seats = (seq_lengths, value_owner, lax.axis_index("mp").reshape(1).astype(jnp.int32))
     copies = lax.axis_size("dp")
 
-    qkv_pack = jnp.pad(jnp.transpose(qkv_weight, (1, 2, 3, 0)), ((0, 0), (0, 1), (0, 0), (0, 0)))
-    qkv_pack = qkv_pack.reshape(pairs_dev * PACK * head_size, model_width)
+    qkv_rows = jnp.transpose(qkv_weight, (1, 2, 3, 0)).reshape(pairs_dev, 5 * head_size, model_width)
     bias_pack = jnp.concatenate(
         [qv_bias[:, 0:2], jnp.zeros_like(qv_bias[:, 0:2]), qv_bias[:, 2:3], jnp.zeros_like(qv_bias[:, 2:3])],
         axis=1,
@@ -942,11 +941,12 @@
     dense = 2 * group_rows * model_width
 
     packs = pairs_dev * PACK * head_size
-    rows_one, all_first, packed = call(
+    rows_one, all_first, packed, qkv_pack = call(
         functools.partial(open_kernel, count, chunk), 0,
         (inputs, attn_norm_gain.reshape(row), attn_norm_bias.reshape(row), first_values.reshape(group_rows, slim),
-         qkv_pack, bias_pack),
-        [like(whole, BF16), like((count, group_rows, slim), BF16), like((group_rows, packs), BF16)],
+         qkv_rows, bias_pack),
+        [like(whole, BF16), like((count, group_rows, slim), BF16), like((group_rows, packs), BF16),
+         like((packs, model_width), BF16)],
         main_sems + side_sems, dense * packs,
     )
     rows_one = rows_one.reshape(group_rows, model_width)
@@ -998,28 +998,23 @@
     grad_qkv_weight = grad_qkv_weight.reshape(pairs_dev, PACK, head_size, model_width)[:, 0:5]
     grad_qkv_weight = sliced(grad_qkv_weight.reshape(pairs_dev * 5 * head_size, model_width))
     grad_out_weight = sliced(grad_out_weight)
-    grad_inputs, sums_one, qkv_slab, out_slab = call(
-        functools.partial(input_back_kernel, count, copies, chunk), 3,
-        (grad_flat, qkv_pack, inputs, grad_residual, attn_norm_gain.reshape(row), grad_qkv_weight, grad_out_weight),
-        [like(inputs.shape, BF16), like((8, model_width), F32),
-         like(grad_qkv_weight.shape[2:], BF16), like(grad_out_weight.shape[2:], BF16)],
-        sum_scratch + reduce_scratch(copies, grad_out_weight) + reduce_scratch(copies, grad_qkv_weight),
-        dense * packs,
-    )
     wide_bias = jnp.pad(grad_up_bias, (0, model_width - grad_up_bias.shape[0])).reshape(row)
     slim_bias = jnp.pad(grad_qv_bias.reshape(-1), (0, model_width - grad_qv_bias.size)).reshape(row)
-    own_sums = jnp.concatenate([sums_two[0:4], sums_one[0:2], wide_bias, slim_bias], axis=0)
+    own_sums = jnp.concatenate([sums_two[0:4], jnp.zeros((2, model_width), F32), wide_bias, slim_bias], axis=0)
     block = pltpu.VMEM(own_sums.shape, F32)
-    small, grad_first, qkv_sum, out_sum = call(
-        functools.partial(closing_kernel, count, copies, 6, pairs_dev), 4,
-        (value_owner, own_sums, grad_skip, qkv_slab, out_slab),
-        [like(own_sums.shape, F32), like((group_rows, slim), BF16),
+    grad_inputs, small, grad_first, qkv_sum, out_sum = call(
+        functools.partial(input_back_kernel, count, copies, chunk, 6, pairs_dev), 3,
+        (value_owner, grad_flat, qkv_pack, inputs, grad_residual, attn_norm_gain.reshape(row), own_sums, grad_skip,
+         grad_qkv_weight, grad_out_weight),
+        [like(inputs.shape, BF16), like(own_sums.shape, F32), like((group_rows, slim), BF16),
          like(grad_qkv_weight.shape, BF16), like(grad_out_weight.shape, BF16)],
-        [pltpu.VMEM((count, group_rows, slim), BF16)]
+        sum_scratch + reduce_scratch(copies, grad_out_weight) + reduce_scratch(copies, grad_qkv_weight)
+        + [pltpu.VMEM((count, group_rows, slim), BF16), pltpu.VMEM(grad_qkv_weight.shape[2:], BF16),
+           pltpu.VMEM(grad_out_weight.shape[2:], BF16), block]
         + side_sems + gather_scratch(copies) + gather_scratch(copies)
         + [pltpu.VMEM((copies, *own_sums.shape), F32), pltpu.VMEM((count, *own_sums.shape), F32), block,
            pltpu.SemaphoreType.DMA((2, copies)), pltpu.SemaphoreType.DMA((2, count))],
-        own_sums.size * (copies + count), scalars=1,
+        dense * packs, scalars=1,
     )
     qkv_sum = qkv_sum.reshape(pairs_dev, 5, head_size, model_width).astype(F32)
     qkv_sum = jnp.transpose(qkv_sum, (3, 0, 1, 2))

time: 419 us -> 409 us (0.976)
    pallas_call x6 -> x5, Pallas kernels: 322 us -> 318 us  [call(): pl.pallas_call(kernel, out_shape=outputs, in_specs=[pl.BlockSpec(memory_s...]
where the time goes in v5:
time: 409 us; the launch traced here: 408 us
  Pallas kernels  335 us (82%)
  matrix products  32.2 us (8%)
  between operations  14.2 us (3%)
  local copies, waits for them, and re-layouts  13.5 us (3%)
  other arithmetic  12.7 us (3%)
    pallas_call x5, Pallas kernels, call(): pl.pallas_call(kernel, out_shape=outputs, in_specs=[pl.BlockSpec(memory_s...  318 us
    dot_general x3, matrix products, rows_product(): lax.dot_general(left, right, (((0,), (0,)), ((), ())), preferred_element_...  18.7 us
    pallas_call x1, Pallas kernels, attend_forward(): pl.pallas_call(functools.partial(attend_forward_kernel, pairs), grid_spec...  17.2 us
    dot_general x1, matrix products, back_product(): lax.dot_general(left, weight, (((1,), (1,)), ((), ())), preferred_element...  13.6 us
  transfers between devices with their start and end apart: 2, of which 0 were waited for; matrix products, arithmetic and copies ran while one was open for 5% of the time, Pallas kernels for 71%

profile of v5, /device:TPU:0, one launch (start us, length us, event | category | flops | bytes accessed | tf_op | source)
XLA Modules:
  0.0 407.7 jit_solution(4406516323456466627)
XLA Ops:
  7.2 0.7 slice.46
  9.5 2.0 copy.37.first_ref
  11.5 45.7 %shard_map.280 = (bf16[4,512,1024]{2,1,0:T(8,128)(2,1)}, bf16[4,2048,128]{2,1,0:T(8,128)(2,1)}, bf16[2048,768]{1,0:T(8,128)(2,1)}, bf16[768,1024]{1,0:T(8,128)(2,1)}) custom-call(bf16[512,1024]{1,0:T(8,128)(2,1)} %x_ref.5, f32[1,1024]{1,0:T(1,128)} %bitcast.68, f32[1,1024]{1,0:T(1,128)} %bitcast.61, bf16[2048,128]{1,0:T(8,128)(2,1)} %copy.37.first_ref, ...), custom_call_target="tpu_custom_call" | custom-call | flops 3221225472 | bytes 13904896 | tf_op jit(solution)/shard_map/pallas_call | solution.py:885
  57.3 17.2 %attend_forward.1 = (bf16[2048,256]{1,0:T(8,128)(2,1)}, f32[2048,256]{1,0:T(8,128)}) custom-call(s32[4]{0:T(128)} %lengths.3, s32[8]{0:T(128)} %owner.5, s32[1]{0:T(128)} %bitcast.5.place, bf16[2048,768]{1,0:T(8,128)(2,1)} %get-tuple-element.42.qkv_ref, bf16[4,2048,128]{2,1,0:T(8,128)(2,1)} %get-tuple-element.43.first_ref), custom_call_target="tpu_custom_call" | custom-call | flops 4294967296 | bytes 8388608 | tf_op jit(solution)/shard_map/attend_forward/pallas_call | solution.py:231
  74.5 71.0 %shard_map.281 = (bf16[4,512,1024]{2,1,0:T(8,128)(2,1)}, f32[512,1024]{1,0:T(8,128)}, f32[2048,1024]{1,0:T(8,128)}, bf16[2048,1024]{1,0:T(8,128)(2,1)}) custom-call(bf16[2048,256]{1,0:T(8,128)(2,1)} %get-tuple-element.44.left.mixed_ref, bf16[256,1024]{1,0:T(8,128)(2,1)} %bitcast.59, bf16[512,1024]{1,0:T(8,128)(2,1)} %x_ref.5, f32[1,1024]{1,0:T(1,128)} %bitcast.62, ...), custom_call_target="tpu_custom_call" | custom-call | flops 5368709120 | bytes 23609344 | tf_op jit(solution)/shard_map/pallas_call | solution.py:885
  145.6 13.6 %convert_reduce_fusion = (f32[1024]{0:T(1024)S(1)}, bf16[2048,1024]{1,0:T(8,128)(2,1)S(1)}) fusion(f32[2048,1024]{1,0:T(8,128)} %get-tuple-element.45, bf16[2048,1024]{1,0:T(8,128)(2,1)} %all-gather.2.cloned.1.call-done, bf16[1024,1024]{1,0:T(8,128)(2,1)S(1)} %copy-done.5), kind=kOutput, calls=%fused_computation.10 | convolution fusion | flops 4349492224 | bytes 18878464 | tf_op jit(solution)/shard_map/dot_general | solution.py:32
  159.2 5.8 %convolution_convert_fusion.1 = bf16[1024,1024]{1,0:T(8,128)(2,1)} fusion(bf16[2048,1024]{1,0:T(8,128)(2,1)S(1)} %bitcast.71, bf16[2048,1024]{1,0:T(8,128)(2,1)S(1)} %get-tuple-element.50.left), kind=kOutput, calls=%fused_computation.13 | convolution fusion | flops 4296015872 | bytes 10485760 | tf_op jit(solution)/shard_map/dot_general | solution.py:28
  165.0 6.0 %convolution_convert_fusion = bf16[1024,1024]{1,0:T(8,128)(2,1)} fusion(bf16[2048,1024]{1,0:T(8,128)(2,1)S(1)} %copy-done.8, bf16[2048,1024]{1,0:T(8,128)(2,1)S(1)} %copy-done.4), kind=kOutput, calls=%fused_computation.12 | convolution fusion | flops 4296015872 | bytes 10485760 | tf_op jit(solution)/shard_map/dot_general | solution.py:28
  171.1 60.8 %shard_map.282 = (f32[512,1024]{1,0:T(8,128)}, f32[8,1024]{1,0:T(8,128)}, bf16[2048,256]{1,0:T(8,128)(2,1)}, bf16[256,1024]{1,0:T(8,128)(2,1)}) custom-call(bf16[2048,1024]{1,0:T(8,128)(2,1)} %copy-done.7, bf16[1024,1024]{1,0:T(8,128)(2,1)} %weight.2, f32[512,1024]{1,0:T(8,128)} %get-tuple-element.51.residual_ref, bf16[512,1024]{1,0:T(8,128)(2,1)} %dy_ref.1, ...), custom_call_target="tpu_custom_call" | custom-call | flops 4294967296 | bytes 14716928 | tf_op jit(solution)/shard_map/pallas_call | solution.py:885
  231.9 47.3 %shard_map.283 = (bf16[2048,768]{1,0:T(8,128)(2,1)}, bf16[2048,128]{1,0:T(8,128)(2,1)}, f32[8,768]{1,0:T(8,128)}, bf16[512,1024]{1,0:T(8,128)(2,1)}) custom-call(s32[4]{0:T(128)} %lengths.3, s32[8]{0:T(128)} %owner.5, bf16[2048,768]{1,0:T(8,128)(2,1)} %get-tuple-element.42.qkv_ref, bf16[4,2048,128]{2,1,0:T(8,128)(2,1)} %get-tuple-element.43.first_ref, ...), custom_call_target="tpu_custom_call" | custom-call | flops 10737418240 | bytes 21524528 | tf_op jit(solution)/shard_map/pallas_call | solution.py:885
  279.2 0.8 slice_reduce_fusion
  280.0 6.9 %convolution_convert_fusion.2 = bf16[768,1024]{1,0:T(8,128)(2,1)S(1)} fusion(bf16[2048,768]{1,0:T(8,128)(2,1)} %get-tuple-element.55.left, bf16[2048,1024]{1,0:T(8,128)(2,1)} %bitcast.70), kind=kOutput, calls=%fused_computation.14 | convolution fusion | flops 3222011904 | bytes 8912896 | tf_op jit(solution)/shard_map/dot_general | solution.py:28
  286.9 1.2 slice.62
  288.2 0.7 pad_maximum_fusion.small_ref
  288.9 93.0 %shard_map.284 = (bf16[512,1024]{1,0:T(8,128)(2,1)}, f32[8,1024]{1,0:T(8,128)}, bf16[2048,128]{1,0:T(8,128)(2,1)}, bf16[4,2,80,1024]{3,2,1,0:T(8,128)(2,1)}, bf16[4,2,32,1024]{3,2,1,0:T(8,128)(2,1)}) custom-call(s32[8]{0:T(128)} %owner.5, bf16[2048,768]{1,0:T(8,128)(2,1)} %get-tuple-element.55.left, bf16[768,1024]{1,0:T(8,128)(2,1)} %get-tuple-element.56.weight, ...), custom_call_target="tpu_custom_call" | custom-call | flops 3221225472 | bytes 13701152 | tf_op jit(solution)/shard_map/pallas_call | solution.py:885
  381.9 0.7 slice_reduce_fusion.1
  383.3 2.0 copy.38
  385.3 2.1 convert.4
  387.5 1.6 fusion.7
  389.1 3.1 convert_bitcast_fusion
  392.2 4.2 %convert_element_type.41 = f32[1024,1024]{1,0:T(8,128)} convert(bf16[1024,1024]{1,0:T(8,128)(2,1)} %get-tuple-element.99) | non-fusion elementwise | flops 1048576 | bytes 6291456 | tf_op jit(solution)/shard_map/convert_element_type | solution.py:1021
  396.5 2.5 convert_element_type.42
  398.9 1.0 copy.44
  399.9 1.0 copy.45
  (41 shorter events, 2.7 us)
Async XLA Ops:
  7.2 138.4 %all-gather.2.cloned.1.call-start = ((), (), s32[]{:S(2)}) async-start(), calls=%async_computation | async-start | bytes 5242880 | tf_op jit(solution)/shard_map/all_gather | solution.py:954
  57.3 335.0 %all-reduce.4.cloned.1.call-start = ((), (), s32[]{:S(2)}) async-start(), calls=%async_computation.1 | async-start | bytes 8388608 | tf_op jit(solution)/shard_map/psum | solution.py:977
  74.5 71.0 %copy-start.5 = (bf16[1024,1024]{1,0:T(8,128)(2,1)S(1)}, bf16[1024,1024]{1,0:T(8,128)(2,1)}, u32[]{:S(2)}) copy-start(bf16[1024,1024]{1,0:T(8,128)(2,1)} %weight.3) | copy-start | bytes 6291460
  145.6 13.6 %copy-start.6 = (bf16[4,512,1024]{2,1,0:T(8,128)(2,1)S(1)}, bf16[4,512,1024]{2,1,0:T(8,128)(2,1)}, u32[]{:S(2)}) copy-start(bf16[4,512,1024]{2,1,0:T(8,128)(2,1)} %get-tuple-element.48) | copy-start | bytes 12582916
  159.2 5.8 %copy-start.7 = (bf16[2048,1024]{1,0:T(8,128)(2,1)}, bf16[2048,1024]{1,0:T(8,128)(2,1)S(1)}, u32[]{:S(2)}) copy-start(bf16[2048,1024]{1,0:T(8,128)(2,1)S(1)} %get-tuple-element.50.left) | copy-start | bytes 12582916
  159.2 5.8 %copy-start.4 = (bf16[2048,1024]{1,0:T(8,128)(2,1)S(1)}, bf16[2048,1024]{1,0:T(8,128)(2,1)}, u32[]{:S(2)}) copy-start(bf16[2048,1024]{1,0:T(8,128)(2,1)} %all-gather.2.cloned.1.call-done) | copy-start | bytes 12582916
  159.2 5.8 %copy-start.8 = (bf16[2048,1024]{1,0:T(8,128)(2,1)S(1)}, bf16[2048,1024]{1,0:T(8,128)(2,1)}, u32[]{:S(2)}) copy-start(bf16[2048,1024]{1,0:T(8,128)(2,1)} %get-tuple-element.49.left) | copy-start | bytes 12582916
  280.0 8.2 %copy-start.3 = (f32[8,1024]{1,0:T(8,128)S(1)}, f32[8,1024]{1,0:T(8,128)}, u32[]{:S(2)}) copy-start(f32[8,1024]{1,0:T(8,128)} %get-tuple-element.58) | copy-start | bytes 98308
  392.2 4.2 %copy-start = (bf16[1024,1024]{1,0:T(8,128)(2,1)S(1)}, bf16[1024,1024]{1,0:T(8,128)(2,1)}, u32[]{:S(2)}) copy-start(bf16[1024,1024]{1,0:T(8,128)(2,1)} %get-tuple-element.100) | copy-start | bytes 6291460
  396.5 2.5 copy-start.1
  396.5 3.5 copy-start.2
Sparse Core Ops, SparseCore 0:
  57.4 44.6 all-gather.1
  171.1 176.0 all-reduce.3
